TPU v7x, 128 devices: a whole 4x4x4 slice. The times are simulated.
128 devices in a mesh: section: 4 (over z), rows: 32 (over y, x, core).
Axes of the slice: x: 4, y: 4, z: 4, core: 2. Of those that a mesh axis runs over, the one named last changes fastest.
Arguments:
- rows_data: float32 [16, 32768, 128], P('section', 'rows'), may hold values from -6 to 6
- row_keys: int32 [16, 32768], P('section', 'rows'), may hold values from 0 to 8191
- valid_counts: int32 [16, 32], P('section', 'rows'), may hold values from 256 to 1024
- predicates: int32 [4, 16, 1024], P('section', None, 'rows'), may hold values from -2147483648 to 2147483647, as said below
- section_weight: float32 [4, 128, 128], P('section'), may hold values from -0.5 to 0.5
- section_bias: float32 [4, 128], P('section'), may hold values from -3 to 3
Outputs:
- key_means: float32 [8192, 128], P(('section', 'rows'))
- key_counts: float32 [8192], P(('section', 'rows'))
Inputs may be any that keep to these rules, and one draw needn't show every extreme that they name: Bit j of predicates[s, m, w] is the flag of row 32 w + j of micro-batch m for section s; about three flags in four are 1. `row_keys`: keys are drawn from a skewed distribution: a few keys are very frequent and most are rare.
All inputs are finite; a program needn't handle non-finite values.
Results may differ from a plain program's by a relative error of at most 0.0001.
Values sent between devices are 32-bit elements; how exact they have to be, the bound alone decides.
A program may use at most 64 MiB of HBM per device.

v0:
```python
import math

import jax
import jax.numpy as jnp
from jax import lax
from jax.sharding import Mesh
from jax.sharding import PartitionSpec as P

KEYS = 8192
SECTIONS = 4
SECTION_ROWS = ("section", "rows_0", "rows_1", "rows_2")
ROWS = ("rows_0", "rows_1", "rows_2")


def in_order(pieces, dim):
    lengths = list(pieces.shape[1:])
    lengths[dim] *= pieces.shape[0]
    return jnp.moveaxis(pieces, 0, dim).reshape(lengths)


def from_everyone(x, axis):
    count = lax.axis_size(axis)
    return lax.all_to_all(jnp.broadcast_to(x[None], (count, *x.shape)), axis, 0, 0, tiled=True)


def gathered_copies(x, axis, dim):
    return in_order(from_everyone(x, axis), dim)


def side_by_side(arrays, axis, dim, along):
    widths = [math.prod(a.shape[along:]) for a in arrays]
    both = jnp.concatenate(
        [a.reshape(*a.shape[:along], w) for a, w in zip(arrays, widths)], axis=along
    )
    result = lax.all_gather(both, axis, axis=dim, tiled=True)
    pieces = jnp.split(result, [sum(widths[:k]) for k in range(1, len(widths))], axis=along)
    return tuple(
        (b.reshape(*result.shape[:along], *a.shape[along:]) for a, b in zip(arrays, pieces))
    )


def in_blocks(x, dim, count):
    before, after = (x.shape[:dim], x.shape[dim + 1 :])
    return jnp.moveaxis(x.reshape(*before, count, -1, *after), dim, 0)


def sum_at_owner(x, axis, dim):
    count = lax.axis_size(axis)
    pieces = lax.all_to_all(in_blocks(x, dim, count), axis, 0, 0, tiled=True)
    return jnp.sum(pieces, axis=0)


def sum_in_two_steps(x, axes, dim):
    far, near = axes
    pieces = in_blocks(x, dim, lax.axis_size(far))
    nearer = sum_at_owner(pieces, near, dim + 1)
    arrived = lax.all_to_all(nearer, far, split_axis=0, concat_axis=0, tiled=True)
    return arrived.sum(axis=0)


def sent_together(arrays, axis, dim, along):
    columns = [a.reshape(*a.shape[:along], -1) for a in arrays]
    both = jnp.concatenate(columns, axis=along)
    result, at, outs = (sum_in_two_steps(both, axis, dim), 0, [])
    for a, column in zip(arrays, columns):
        piece = result[..., at : at + column.shape[along]]
        outs.append(piece.reshape(*piece.shape[:along], *a.shape[along:]))
        at += column.shape[along]
    return tuple(outs)


def advance(hidden, weight, bias):
    return hidden + jnp.tanh(
        jnp.dot(hidden, weight, precision=lax.Precision.HIGHEST, preferred_element_type=jnp.float32)
        + bias
    )


def unpack_flags(words):
    shifts = lax.broadcasted_iota(jnp.int32, (32,), 0)
    flags = jnp.right_shift(words[..., None], shifts) & 1
    return flags.reshape(words.shape[:-1] + (words.shape[-1] * 32,))


def tally_rows(row_sums, row_counts, keys):
    sums = jax.ops.segment_sum(row_sums, keys, num_segments=KEYS)
    counts = jax.ops.segment_sum(row_counts, keys, num_segments=KEYS)
    return (sums, counts)


def shards(rows_data, row_keys, valid_counts, predicates, section_weight, section_bias):
    held_batches = rows_data.shape[0]
    block = rows_data.shape[1]
    width = rows_data.shape[2]
    section = lax.axis_index("section")
    position = lax.broadcasted_iota(jnp.int32, (block,), 0)
    every_words = gathered_copies(predicates, "section", 0)
    weights, biases = side_by_side((section_weight, section_bias), "section", 0, 2)
    first = section * held_batches
    hidden = rows_data.reshape(held_batches * block, width)
    alive = (position[None, :] < valid_counts).reshape(-1)
    held_words = lax.dynamic_slice_in_dim(every_words, first, held_batches, 1)
    marks = unpack_flags(held_words)
    row_sums = jnp.zeros((held_batches * block, width), jnp.float32)
    row_counts = jnp.zeros((held_batches * block,), jnp.float32)
    for level in range(SECTIONS):
        alive = alive & (marks[level].reshape(-1) == 1)
        hidden = advance(hidden, weights[level], biases[level])
        row_sums = row_sums + jnp.where(alive[:, None], hidden, 0.0)
        row_counts = row_counts + alive.astype(jnp.float32)
    sums, counts = tally_rows(row_sums, row_counts, row_keys.reshape(-1))
    owned_sums, owned_counts = sent_together(
        (sums, counts), (("section", "rows_0", "rows_1"), "rows_2"), 0, 1
    )
    key_means = owned_sums / jnp.maximum(owned_counts, 1.0)[:, None]
    return (key_means, owned_counts)


def solution(mesh):
    finer = Mesh(
        mesh.devices.reshape(mesh.shape["section"], 4, 4, 2),
        ("section", "rows_0", "rows_1", "rows_2"),
    )
    placed = (
        P("section", ROWS, None),
        P("section", ROWS),
        P("section", ROWS),
        P("section", None, ROWS),
        P("section", None, None),
        P("section", None),
    )
    return jax.shard_map(
        shards,
        mesh=finer,
        in_specs=placed,
        out_specs=(P(SECTION_ROWS, None), P(SECTION_ROWS)),
        check_vma=False,
    )
```

profile of v0, /device:TPU:0, one launch (start us, length us, event | category | flops | bytes accessed | tf_op | source)
XLA Modules:
  0.0 184.9 jit_solution(7599997873755483914)
XLA Ops:
  0.6 0.7 broadcast_in_dim.54
  1.3 0.7 reshape.150
  2.0 5.4 %all-to-all-start = ((s32[4,1,512]{2,1,0:T(1,128)}), s32[4,1,512]{2,1,0:T(1,128)S(1)}, u32[]{:S(2)}, u32[]{:S(2)}) async-start(s32[4,1,512]{2,1,0:T(1,128)} %reshape.150), calls=%async_computation | async-start | bytes 16384 | tf_op jit(solution)/shard_map/all_to_all | solution.py:23
  7.4 0.9 copy.29
  8.4 0.7 pad_maximum_fusion
  9.0 13.1 %all_gather.3 = f32[4,128,129]{1,2,0:T(8,128)S(1)} all-gather(f32[1,128,129]{1,2,0:T(8,128)S(1)} %pad_maximum_fusion), channel_id=1, replica_groups=mesh['section'=4,'rows_0'=4,'rows_1'=4,'rows_2'=2] {'section'}, dimensions={0}, use_global_device_ids=true | all-gather | bytes 330240 | tf_op jit(solution)/shard_map/all_gather | solution.py:35
  22.2 2.9 %copy.39 = f32[4096,128]{0,1:T(8,128)} copy(f32[4096,128]{1,0:T(8,128)} %bitcast.55) | data formatting | bytes 4194304 | tf_op jit(solution)/shard_map/reshape | solution.py:100
  25.1 4.2 %fusion.10 = f32[4096,128]{0,1:T(8,128)S(1)} fusion(f32[4096,128]{0,1:T(8,128)} %copy.39, f32[4096,128]{1,0:T(8,128)} %bitcast.56, f32[128]{0:T(128)S(1)} %get-tuple-element.12, f32[4,128,129]{1,2,0:T(8,128)S(1)} %all_gather.3), kind=kOutput, calls=%fused_computation.17 | convolution fusion | flops 806354944 | bytes 6357504 | tf_op jit(solution)/shard_map/dot_general | solution.py:74
  29.3 2.1 %fusion.7 = f32[4096,128]{0,1:T(8,128)S(1)} fusion(f32[4096,128]{0,1:T(8,128)S(1)} %fusion.10, f32[128]{0:T(128)S(1)} %get-tuple-element.11, f32[4,128,129]{1,2,0:T(8,128)S(1)} %all_gather.3), kind=kOutput, calls=%fused_computation.13 | convolution fusion | flops 806354944 | bytes 6357504 | tf_op jit(solution)/shard_map/dot_general | solution.py:74
  31.4 0.0 copy-start
  31.4 0.0 copy-start.2
  31.5 0.0 copy-start.1
  31.5 3.5 %fusion.5 = f32[4096,128]{0,1:T(8,128)} fusion(f32[4096,128]{0,1:T(8,128)S(1)} %fusion.7, f32[128]{0:T(128)S(1)} %get-tuple-element.10, f32[4,128,129]{1,2,0:T(8,128)S(1)} %all_gather.3), kind=kOutput, calls=%fused_computation.10 | convolution fusion | flops 806354944 | bytes 6357504 | tf_op jit(solution)/shard_map/dot_general | solution.py:74
  35.0 0.0 copy-done
  35.0 0.0 copy-done.2
  35.0 0.1 fusion.15
  35.1 0.0 copy-done.1
  35.1 0.0 all-to-all-done
  35.1 0.5 broadcast.54
  35.6 0.7 reduce.4
  36.3 0.1 reshape.151
  36.4 0.1 shift-right-arithmetic_and_fusion
  36.6 0.1 eq.59
  36.7 0.1 eq.65
  36.7 0.1 eq.63
  36.8 0.1 eq.61
  37.0 22.1 %scatter_custom_fusion.1 = f32[8192]{0:T(1024)S(1)} fusion(s32[4096]{0:T(1024)S(1)} %bitcast.58, f32[4096]{0:T(1024)S(1)} %get-tuple-element.4, f32[]{:T(128)} %constant.8.clone.1), kind=kCustom, calls=%fused_computation.35 | custom fusion | flops 4096 | bytes 32772 | tf_op jit(solution)/shard_map/scatter-add | solution.py:87
  59.1 0.1 concatenate.13
  59.2 6.8 %fusion.3 = f32[4096,128]{0,1:T(8,128)} fusion(f32[4096,128]{0,1:T(8,128)} %fusion.5, f32[4096,128]{0,1:T(8,128)} %copy-done, f32[4096,128]{0,1:T(8,128)S(1)} %fusion.10, f32[128]{0:T(128)S(1)} %get-tuple-element.9, pred[4096]{0:T(1024)(128)(4,1)S(1)} %get-tuple-element.5, pred[4096]{0:T(1024)(128)(4,1)S(1)} %get-tuple-element.6, ...), kind=kOutput, calls=%fused_computation.7 | convolution fusion | flops 810024960 | bytes 10568192 | tf_op jit(solution)/shard_map/dot_general | solution.py:74
  66.0 1.9 %copy.33 = f32[4096,128]{1,0:T(8,128)S(1)} copy(f32[4096,128]{0,1:T(8,128)} %fusion.3) | data formatting | bytes 4194304 | tf_op jit(solution)/shard_map/add | solution.py:109
  67.9 24.5 %scatter_custom_fusion = f32[8192,128]{1,0:T(8,128)} fusion(s32[4096]{0:T(1024)S(1)} %bitcast.59, f32[4096,128]{1,0:T(8,128)S(1)} %copy.33, f32[]{:T(128)} %constant.8.clone.1), kind=kCustom, calls=%fused_computation.18 | custom fusion | flops 524288 | bytes 4194308 | tf_op jit(solution)/shard_map/scatter-add | solution.py:86
  92.4 2.7 %copy.35 = f32[64,2,64,1]{3,2,0,1:T(8,128)} copy(f32[64,2,64,1]{2,1,0,3:T(2,128)S(1)} %concatenate.13) | data formatting | bytes 65536 | tf_op jit(solution)/shard_map/concatenate | solution.py:63
  95.1 4.4 %maximum_bitcast_fusion = f32[2,64,64,129]{3,2,1,0:T(8,128)S(1)} fusion(f32[64,2,64,1]{3,2,0,1:T(8,128)} %copy.35, f32[64,2,64,128]{3,2,1,0:T(8,128)} %bitcast.54), kind=kLoop, calls=%fused_computation.2 | loop fusion | flops 1056768 | bytes 8454144 | tf_op jit(solution)/shard_map/transpose | solution.py:44
  99.5 11.7 %all_to_all.15 = f32[2,64,64,129]{3,2,1,0:T(8,128)} all-to-all(f32[2,64,64,129]{3,2,1,0:T(8,128)S(1)} %maximum_bitcast_fusion), channel_id=1, replica_groups=mesh['section'=4,'rows_0'=4,'rows_1'=4,'rows_2'=2] {'rows_2'}, dimensions={0} | all-to-all | bytes 8454144 | tf_op jit(solution)/shard_map/all_to_all | solution.py:49
  111.3 6.8 %reduce_sum.18 = f32[64,64,129]{2,1,0:T(8,128)} reduce(f32[2,64,64,129]{3,2,1,0:T(8,128)} %all_to_all.15, f32[]{:T(128)} %constant.8.clone.1), dimensions={0}, to_apply=%region_2.3 | reduce | flops 528384 | bytes 6340612 | tf_op jit(solution)/shard_map/reduce_sum | solution.py:50
  118.0 63.0 %all_to_all.16 = f32[64,64,129]{2,1,0:T(8,128)} all-to-all(f32[64,64,129]{2,1,0:T(8,128)} %reduce_sum.18), channel_id=1, replica_groups=mesh['section'=4,'rows_0'=4,'rows_1'=4,'rows_2'=2] {'section','rows_0','..., dimensions={0} | all-to-all | bytes 4227072 | tf_op jit(solution)/shard_map/all_to_all | solution.py:57
  181.1 2.5 %reduce_sum.19 = f32[64,129]{1,0:T(8,128)S(1)} reduce(f32[64,64,129]{2,1,0:T(8,128)} %all_to_all.16, f32[]{:T(128)} %constant.8.clone.1), dimensions={0}, to_apply=%region_3.4 | reduce | flops 520128 | bytes 2146564 | tf_op jit(solution)/shard_map/reduce_sum | solution.py:58
  183.6 0.6 slice_reduce_fusion
  184.2 0.7 slice_divide_fusion
  (5 shorter events, 0.1 us)
Async XLA Ops:
  2.0 33.1 %all-to-all-start = ((s32[4,1,512]{2,1,0:T(1,128)}), s32[4,1,512]{2,1,0:T(1,128)S(1)}, u32[]{:S(2)}, u32[]{:S(2)}) async-start(s32[4,1,512]{2,1,0:T(1,128)} %reshape.150), calls=%async_computation | async-start | bytes 16384 | tf_op jit(solution)/shard_map/all_to_all | solution.py:23
  31.4 3.6 %copy-start = (f32[4096,128]{0,1:T(8,128)}, f32[4096,128]{0,1:T(8,128)S(1)}, u32[]{:S(2)}) copy-start(f32[4096,128]{0,1:T(8,128)S(1)} %fusion.7) | copy-start | bytes 6291460
  31.4 3.5 %copy-start.2 = (s32[4,1]{0,1:T(1,128)S(1)}, s32[4,1]{0,1:T(1,128)}, u32[]{:S(2)}) copy-start(s32[4,1]{0,1:T(1,128)} %param.8) | copy-start | bytes 52
  31.5 3.6 %copy-start.1 = (s32[4,1024]{1,0:T(4,128)S(1)}, s32[4,1024]{1,0:T(4,128)}, u32[]{:S(2)}) copy-start(s32[4,1024]{1,0:T(4,128)} %param.7) | copy-start | bytes 49156
where the time goes:
time: 185 us
  blocking collectives  87.9 us (48%)
  other arithmetic  63.2 us (34%)
  matrix products  16.6 us (9%)
  local copies, waits for them, and re-layouts  10.9 us (6%)
  starting transfers between devices  5.42 us (3%)
    all_to_all x1, blocking collectives, sum_in_two_steps(): lax.all_to_all(nearer, far, split_axis=0, concat_axis=0, tiled=True)  63 us
    scatter-add x1, other arithmetic, tally_rows(): sums = jax.ops.segment_sum(row_sums, keys, num_segments=KEYS)  24.5 us
    scatter-add x1, other arithmetic, tally_rows(): counts = jax.ops.segment_sum(row_counts, keys, num_segments=KEYS)  22.1 us
    dot_general x4, matrix products, advance(): jnp.dot(hidden, weight, precision=lax.Precision.HIGHEST, preferred_elemen...  16.6 us
    all_gather x1, blocking collectives, side_by_side(): result = lax.all_gather(both, axis, axis=dim, tiled=True)  13.1 us
    all_to_all x1, blocking collectives, sum_at_owner(): pieces = lax.all_to_all(in_blocks(x, dim, count), axis, 0, 0, tiled=True)  11.7 us
    reduce_sum x1, other arithmetic, sum_at_owner(): return jnp.sum(pieces, axis=0)  6.8 us
    all_to_all x1, starting transfers between devices, from_everyone(): lax.all_to_all(jnp.broadcast_to(x[None], (count, *x.shape)), axis, 0, 0,...  5.42 us
  transfers between devices with their start and end apart: 1, of which 0 were waited for; matrix products, arithmetic and copies ran while one was open for 8% of the time, Pallas kernels for 0%

commit v1 on v0

v1 whole, which is shorter than its diff:
```python
import functools

import jax
import jax.numpy as jnp
from jax import lax
from jax.experimental import pallas as pl
from jax.experimental.pallas import tpu as pltpu
from jax.sharding import PartitionSpec as P

KEYS = 8192
SECTIONS = 4
D = 128
MICRO = 4
BLOCK = 1024
ROWS = MICRO * BLOCK
GROUP = 16
STEP = 256
f32, bf16, i32 = jnp.float32, jnp.bfloat16, jnp.int32
MESH = pl.DeviceIdType.MESH
VM, SM, HB = pltpu.VMEM, pltpu.SMEM, pltpu.HBM


def spec(space):
    return pl.BlockSpec(memory_space=space)


def high_low(x):
    high = x.astype(bf16)
    return high, (x - high.astype(f32)).astype(bf16)


def exchange_kernel(w_in, b_in, p_in, keys, valid, w_all, b_all, same, level, counts, words_v, words, send, recv, local):
    me = lax.axis_index("section")
    row = lax.axis_index("rows")
    barrier = pltpu.get_barrier_semaphore()
    for k in range(1, 4):
        pl.semaphore_signal(barrier, inc=1, device_id=(lax.rem(me + k, 4), row), device_id_type=MESH)
    pl.semaphore_wait(barrier, 3)
    copies = []
    for n, k in enumerate((2, 1, 3)):
        to = lax.rem(me + k, 4)
        for a, (src, dst) in enumerate(
            ((p_in.at[to], words_v.at[me]), (b_in.at[0], b_all.at[me]), (w_in.at[0], w_all.at[me]))
        ):
            copies.append((a, pltpu.make_async_remote_copy(
                src_ref=src, dst_ref=dst, send_sem=send.at[n, a], recv_sem=recv.at[n, a],
                device_id=(to, row), device_id_type=MESH)))
    for a in range(3):
        for which, copy in copies:
            if which == a:
                copy.start()
    own = [
        pltpu.make_async_copy(p_in.at[me], words_v.at[me], local.at[0]),
        pltpu.make_async_copy(b_in.at[0], b_all.at[me], local.at[1]),
        pltpu.make_async_copy(w_in.at[0], w_all.at[me], local.at[2]),
    ]
    for copy in own:
        copy.start()
    group_i = (lax.broadcasted_iota(i32, (1, 128), 1) // GROUP) * KEYS

    def sameness(j, carry):
        key_row = keys[pl.ds(j, 1), :] + group_i
        key_col = jnp.transpose(jnp.broadcast_to(key_row, (128, 128)))
        same[j] = jnp.where(key_col == key_row, 1.0, 0.0).astype(bf16)
        return carry

    lax.fori_loop(0, 32, sameness, 0)
    own[0].wait()
    for which, copy in copies:
        if which == 0:
            copy.wait()
    to_scalar = pltpu.make_async_copy(words_v, words, local.at[3])
    to_scalar.start()
    to_scalar.wait()
    counts[...] = jnp.zeros_like(counts)
    lane = lax.broadcasted_iota(i32, (64, 128), 1)
    sub64 = lax.broadcasted_iota(i32, (64, 128), 0)
    sub128 = lax.broadcasted_iota(i32, (128, 128), 0)

    def tally(j, carry):
        m = j // 8
        first = (j % 8) * 4
        nv = valid[m, 0]
        total = jnp.zeros((64, 128), i32)
        alive = []
        for w in range(4):
            n = nv - (first + w) * 32
            alive.append(jnp.where(n >= 32, jnp.int32(-1), (jnp.int32(1) << jnp.clip(n, 0, 31)) - 1))
        for s in range(SECTIONS):
            alive = [a & words[s, m, first + w] for w, a in enumerate(alive)]
            v = jnp.where(lane < 64, jnp.where(lane < 32, alive[0], alive[1]), jnp.where(lane < 96, alive[2], alive[3]))
            total = total + ((v >> (lane & 31)) & 1)
        key_row = keys[pl.ds(j, 1), :]
        high = jnp.where((key_row >> 7) == sub64, total.astype(f32), 0.0).astype(bf16)
        low = jnp.where((key_row & 127) == sub128, 1.0, 0.0).astype(bf16)
        counts[...] += lax.dot_general(high, low, (((1,), (1,)), ((), ())), preferred_element_type=f32)
        level[j] = jnp.transpose(jnp.concatenate([total, total], axis=0))
        return carry

    lax.fori_loop(0, 32, tally, 0)
    own[1].wait()
    own[2].wait()
    for which, copy in copies:
        if which != 0:
            copy.wait()


def exchange(weight, bias, predicates, keys, valid):
    return pl.pallas_call(
        exchange_kernel,
        out_shape=(
            jax.ShapeDtypeStruct((4, D, D), f32),
            jax.ShapeDtypeStruct((4, 1, D), f32),
            jax.ShapeDtypeStruct((32, 128, 128), bf16),
            jax.ShapeDtypeStruct((32, 128, 128), i32),
            jax.ShapeDtypeStruct((64, 128), f32),
        ),
        in_specs=[spec(HB), spec(HB), spec(HB), spec(VM), spec(SM)],
        out_specs=(spec(VM),) * 5,
        scratch_shapes=[
            pltpu.VMEM((4, 4, 32), i32),
            pltpu.SMEM((4, 4, 32), i32),
            pltpu.SemaphoreType.DMA((3, 3)),
            pltpu.SemaphoreType.DMA((3, 3)),
            pltpu.SemaphoreType.DMA((4,)),
        ],
        compiler_params=pltpu.CompilerParams(collective_id=0, has_side_effects=True, vmem_limit_bytes=8 << 20),
    )(weight, bias, predicates, keys, valid)


def sections_kernel(rows_in, keys, w, b, same, level, table, rows, w2, ready, sem):
    fetch = pltpu.make_async_copy(rows_in, rows, sem)
    fetch.start()
    for s in range(SECTIONS):
        top = jnp.concatenate(high_low(w[s]), axis=1)
        w2[s] = jnp.concatenate([top, top], axis=0)

    def clear(i, carry):
        table[pl.ds(pl.multiple_of(i * 256, 256), 256), :] = jnp.zeros((256, D), f32)
        return carry

    lax.fori_loop(0, KEYS // 256, clear, 0)
    fetch.wait()

    def compute(t, slot):
        h = rows[pl.ds(pl.multiple_of(t * STEP, STEP), STEP), :]
        lev = level[pl.ds(t * (STEP // 128), STEP // 128)].reshape(STEP, 128)
        acc = jnp.zeros((STEP, D), f32)
        for s in range(SECTIONS):
            p = jnp.dot(jnp.concatenate(high_low(h), axis=1), w2[s], preferred_element_type=f32)
            h = h + jnp.tanh(p[:, :D] + (p[:, D:] + b[s]))
            acc = acc + jnp.where(lev > s, h, 0.0)
        both = jnp.concatenate(high_low(acc), axis=1)
        for j in range(STEP // 128):
            p = jnp.dot(same[t * (STEP // 128) + j], both[j * 128 : (j + 1) * 128], preferred_element_type=f32)
            ready[slot, j * 128 : (j + 1) * 128, :] = p[:, :D] + p[:, D:]

    def scatter(t, slot):
        for g in range(STEP // GROUP):
            at = [keys[t * (STEP // 128) + (g * GROUP + i) // 128, (g * GROUP + i) % 128] for i in range(GROUP)]
            held = [table[pl.ds(k, 1), :] for k in at]
            new = [held[i] + ready[slot, g * GROUP + i : g * GROUP + i + 1, :] for i in range(GROUP)]
            for i in range(GROUP):
                table[pl.ds(at[i], 1), :] = new[i]

    compute(0, 0)

    def body(t, carry):
        compute(t, t % 2)
        scatter(t - 1, (t - 1) % 2)
        return carry

    lax.fori_loop(1, ROWS // STEP, body, 0)
    scatter(ROWS // STEP - 1, (ROWS // STEP - 1) % 2)


def sections(rows, keys, w, b, same, level):
    return pl.pallas_call(
        sections_kernel,
        out_shape=jax.ShapeDtypeStruct((KEYS, D), f32),
        in_specs=[spec(HB), spec(SM)] + [spec(VM)] * 4,
        out_specs=spec(VM),
        scratch_shapes=[
            pltpu.VMEM((ROWS, D), f32),
            pltpu.VMEM((SECTIONS, 256, 256), bf16),
            pltpu.VMEM((2, STEP, D), f32),
            pltpu.SemaphoreType.DMA,
        ],
        compiler_params=pltpu.CompilerParams(vmem_limit_bytes=16 << 20),
    )(rows, keys, w, b, same, level)


PARTS = ((0, 24), (24, 24), (48, 16))
ORDER = ((0, 1, 2), (1, 2, 0), (2, 0, 1), (2, 0, 1))


def reduce_kernel(table, counts, means, count_out, *scratch):
    held = scratch[0:4]
    first = scratch[4:8]
    middle = scratch[8:12]
    second = scratch[12:16]
    last = scratch[16:20]
    third = scratch[20:24]
    core_sems, send, recv = scratch[24:27]
    z = lax.axis_index("section")
    row = lax.axis_index("rows")
    y, x, c = row // 8, (row // 2) % 4, row % 2
    place = (z, y, x)

    def peer(axis, k):
        at = list(place)
        at[axis] = lax.rem(at[axis] + k, 4)
        return at[axis], (at[0], at[1] * 8 + at[2] * 2 + c)

    other = (z, y * 8 + x * 2 + (1 - c))
    barrier = pltpu.get_barrier_semaphore()
    pl.semaphore_signal(barrier, inc=1, device_id=other, device_id_type=MESH)
    for axis in range(3):
        for k in range(1, 4):
            pl.semaphore_signal(barrier, inc=1, device_id=peer(axis, k)[1], device_id_type=MESH)
    pl.semaphore_wait(barrier, 10)

    core = []
    for n in (3, 0, 1, 2):
        if n < 3:
            src = table.at[:, :, :, 1 - c, pl.ds(PARTS[n][0], PARTS[n][1]), :]
        else:
            src = counts
        copy = pltpu.make_async_remote_copy(
            src_ref=src, dst_ref=held[n], send_sem=core_sems.at[0, n], recv_sem=core_sems.at[1, n],
            device_id=other, device_id_type=MESH)
        copy.start()
        core.append((n, copy))

    def piece(ref, axes, axis, index):
        where = [slice(None)] * len(axes)
        where[axes.index(axis)] = index
        return ref.at[tuple(where)]

    def send_stage(n, stage, source, axes, target):
        axis = ORDER[n][stage]
        copies = []
        for k in (2, 1, 3):
            index, device = peer(axis, k)
            copy = pltpu.make_async_remote_copy(
                src_ref=piece(source, axes, axis, index), dst_ref=target.at[k - 1],
                send_sem=send.at[n, stage, k - 1], recv_sem=recv.at[n, stage, k - 1],
                device_id=device, device_id_type=MESH)
            copy.start()
            copies.append(copy)
        return copies

    def summed(n, stage, source, axes, target):
        mine = piece(source, axes, ORDER[n][stage], place[ORDER[n][stage]])[...]
        return (mine + target[0]) + (target[1] + target[2])

    axes = [[0, 1, 2] for _ in range(4)]
    flying = {}
    for n, copy in core:
        copy.wait()
        if n < 3:
            for a in range(4):
                held[n][a] += table[a, :, :, c, PARTS[n][0] : PARTS[n][0] + PARTS[n][1], :]
        else:
            held[n][...] += counts[...]
        flying[n] = send_stage(n, 0, held[n], axes[n], first[n])
    for stage, (source, target, result) in enumerate(((held, first, middle), (middle, second, last))):
        for n in (3, 0, 1, 2) if stage else (3, 2, 0, 1):
            for copy in flying[n]:
                copy.wait()
            result[n][...] = summed(n, stage, source[n], axes[n], target[n])
            axes[n] = [a for a in axes[n] if a != ORDER[n][stage]]
            flying[n] = send_stage(n, stage + 1, result[n], axes[n], (second, third)[stage][n])
    total = None
    for n in (3, 0, 1, 2):
        for copy in flying[n]:
            copy.wait()
        value = summed(n, 2, last[n], axes[n], third[n])
        if n == 3:
            wide = jnp.transpose(jnp.broadcast_to(value, (128, 128)))
            total = jnp.where(c == 0, wide[:64], wide[64:])
            count_out[...] = jnp.broadcast_to(jnp.where(c == 0, value, pltpu.roll(value, 64, 1)), (8, 128))
            total = jnp.maximum(total, 1.0)
        else:
            lo, size = PARTS[n]
            means[lo : lo + size, :] = value / total[lo : lo + size]


def reduce_to_owner(table, counts):
    sizes = [24, 24, 16, 1]
    buffers = []
    for lead in ((4, 4, 4), (3, 4, 4), (4, 4), (3, 4), (4,), (3,)):
        buffers += [pltpu.VMEM((*lead, n, D), f32) for n in sizes]
    return pl.pallas_call(
        reduce_kernel,
        out_shape=(jax.ShapeDtypeStruct((64, D), f32), jax.ShapeDtypeStruct((8, D), f32)),
        in_specs=[spec(VM), spec(VM)],
        out_specs=(spec(VM), spec(VM)),
        scratch_shapes=buffers + [
            pltpu.SemaphoreType.DMA((2, 4)),
            pltpu.SemaphoreType.DMA((4, 3, 3)),
            pltpu.SemaphoreType.DMA((4, 3, 3)),
        ],
        compiler_params=pltpu.CompilerParams(collective_id=1, has_side_effects=True, vmem_limit_bytes=16 << 20),
    )(table.reshape(4, 4, 4, 2, 64, D), counts.reshape(4, 4, 4, 1, D))


def shards(rows_data, row_keys, valid_counts, predicates, section_weight, section_bias):
    keys = row_keys.reshape(32, 128)
    w, b, same, level, counts = exchange(
        section_weight, section_bias.reshape(1, 1, D), predicates.reshape(4, MICRO, 32), keys, valid_counts)
    table = sections(rows_data.reshape(ROWS, D), keys, w, b, same, level)
    means, total = reduce_to_owner(table, counts)
    return means, total[0, :64]


def solution(mesh):
    placed = (
        P("section", "rows", None),
        P("section", "rows"),
        P("section", "rows"),
        P("section", None, "rows"),
        P("section", None, None),
        P("section", None),
    )
    return jax.shard_map(
        shards,
        mesh=mesh,
        in_specs=placed,
        out_specs=(P(("section", "rows"), None), P(("section", "rows"))),
        check_vma=False,
    )
```

time: 185 us -> 66.9 us (0.36)
  blocking collectives: 87.9 us -> 0 us
  other arithmetic: 63.2 us -> 0 us
  Pallas kernels: 0 us -> 59.6 us
  matrix products: 16.6 us -> 0 us
  starting transfers between devices: 5.42 us -> 0 us
  local copies, waits for them, and re-layouts: 10.9 us -> 6.37 us
    all_to_all x2 -> x0, blocking collectives: 74.8 us -> none  [the longest x1 63 us: sum_in_two_steps(): lax.all_to_all(nearer, far, split_axis=0, concat_axis=0, tiled=True)]
    pallas_call x0 -> x3, Pallas kernels: none -> 59.6 us  [the longest x1 27.6 us: reduce_to_owner(): pl.pallas_call(reduce_kernel, out_shape=(jax.ShapeDtypeStruct((64, D), f3...]
    scatter-add x2 -> x0, other arithmetic: 46.6 us -> none  [the longest x1 24.5 us: tally_rows(): sums = jax.ops.segment_sum(row_sums, keys, num_segments=KEYS)]
    dot_general x4 -> x0, matrix products: 16.6 us -> none  [advance(): jnp.dot(hidden, weight, precision=lax.Precision.HIGHEST, preferred_elemen...]
    all_gather x1 -> x0, blocking collectives: 13.1 us -> none  [side_by_side(): result = lax.all_gather(both, axis, axis=dim, tiled=True)]
    reduce_sum x2 -> x0, other arithmetic: 9.28 us -> none  [the longest x1 6.8 us: sum_at_owner(): return jnp.sum(pieces, axis=0)]
    all_to_all x1 -> x0, starting transfers between devices: 5.42 us -> none  [from_everyone(): lax.all_to_all(jnp.broadcast_to(x[None], (count, *x.shape)), axis, 0, 0,...]
    transpose x1 -> x0, other arithmetic: 4.37 us -> none  [in_blocks(): return jnp.moveaxis(x.reshape(*before, count, -1, *after), dim, 0)]
  transfers between devices with their start and end apart: 1 -> 0, of which waited for: 0 -> 0; matrix products, arithmetic and copies ran while one was open for 8% -> 0% of each run, Pallas kernels for 0% -> 0%
where the time goes in v1:
time: 66.9 us; the launch traced here: 66.7 us
  Pallas kernels  59.6 us (89%)
  local copies, waits for them, and re-layouts  6.37 us (10%)
  between operations  0.67 us (1%)
    pallas_call x1, Pallas kernels, reduce_to_owner(): pl.pallas_call(reduce_kernel, out_shape=(jax.ShapeDtypeStruct((64, D), f3...  27.6 us
    pallas_call x1, Pallas kernels, sections(): pl.pallas_call(sections_kernel, out_shape=jax.ShapeDtypeStruct((KEYS, D),...  17.9 us
    pallas_call x1, Pallas kernels, exchange(): pl.pallas_call(exchange_kernel, out_shape=(jax.ShapeDtypeStruct((4, D, D)...  14.2 us
    unnamed x10, local copies, waits for them, and re-layouts  5.13 us

profile of v1, /device:TPU:0, one launch (start us, length us, event | category | flops | bytes accessed | tf_op | source)
XLA Modules:
  0.0 66.7 jit_solution(17512915202187269342)
XLA Ops:
  0.6 0.7 %copy.8.valid = s32[4,1]{1,0:T(4,128)S(1)} copy(s32[4,1]{0,1:T(1,128)} %param.8) | data formatting | bytes 32 | tf_op args[2]
  1.4 0.7 %reshape.23.keys = s32[32,128]{1,0:T(8,128)S(1)} reshape(s32[4,1024]{1,0:T(4,128)} %param.7) | data formatting | bytes 32768 | tf_op jit(solution)/shard_map/reshape | solution.py:309
  2.1 0.0 copy-start.1
  2.1 0.8 %copy-done.1 = f32[1,128,128]{2,1,0:T(8,128)S(1)} copy-done((f32[1,128,128]{2,1,0:T(8,128)S(1)}, f32[1,128,128]{2,1,0:T(8,128)}, u32[]{:S(2)}) %copy-start.1) | copy-done | bytes 65560
  2.9 0.0 copy-start.2
  2.9 0.7 %copy-done.2 = s32[1,16,32]{2,1,0:T(8,128)S(1)} copy-done((s32[1,16,32]{2,1,0:T(8,128)S(1)}, s32[1,16,32]{2,1,0:T(8,128)}, u32[]{:S(2)}) %copy-start.2) | copy-done | bytes 2072
  3.6 0.0 copy-start.3
  3.6 0.7 copy-done.3
  4.3 14.2 %shard_map.77 = (f32[4,128,128]{2,1,0:T(8,128)S(1)}, f32[4,1,128]{2,1,0:T(1,128)S(1)}, bf16[32,128,128]{2,1,0:T(8,128)(2,1)S(1)}, s32[32,128,128]{2,1,0:T(8,128)S(1)}, f32[64,128]{1,0:T(8,128)S(1)}) custom-call(f32[1,128,128]{2,1,0:T(8,128)S(1)} %copy-done.1, f32[1,1,128]{2,1,0:T(1,128)S(1)} %bitcast.11, s32[4,4,32]{2,1,0:T(4,128)S(1)} %bitcast.10, ...), custom_call_target="tpu_custom_call" | custom-call | tf_op jit(solution)/shard_map/pallas_call | solution.py:109
  18.5 0.0 copy-start
  18.5 1.6 %copy-done = f32[4,1024,128]{2,1,0:T(8,128)S(1)} copy-done((f32[4,1024,128]{2,1,0:T(8,128)S(1)}, f32[4,1024,128]{2,1,0:T(8,128)}, u32[]{:S(2)}) %copy-start) | copy-done | bytes 2097176
  20.1 17.9 %shard_map.78 = f32[8192,128]{1,0:T(8,128)S(1)} custom-call(f32[4096,128]{1,0:T(8,128)S(1)} %bitcast.8, s32[32,128]{1,0:T(8,128)S(1)} %reshape.23.keys, f32[4,128,128]{2,1,0:T(8,128)S(1)} %get-tuple-element.9.w, f32[4,1,128]{2,1,0:T(1,128)S(1)} %get-tuple-element.10.b, bf16[32,128,128]{2,1,0:T(8,128)(2,1)S(1)} %get-tuple-element.11.same, ...), custom_call_target="tpu_custom_call" | custom-call | tf_op jit(solution)/shard_map/pallas_call | solution.py:178
  37.9 27.6 %shard_map.79 = (f32[64,128]{1,0:T(8,128)S(1)}, f32[8,128]{1,0:T(8,128)S(1)}) custom-call(f32[4,4,4,2,64,128]{5,4,3,2,1,0:T(8,128)S(1)} %bitcast.7, f32[4,4,4,1,128]{4,3,2,1,0:T(1,128)S(1)} %bitcast.9), custom_call_target="tpu_custom_call" | custom-call | tf_op jit(solution)/shard_map/pallas_call | solution.py:294
  65.5 0.5 slice_bitcast_fusion
  66.0 0.6 copy.10
Async XLA Ops:
  2.1 0.8 %copy-start.1 = (f32[1,128,128]{2,1,0:T(8,128)S(1)}, f32[1,128,128]{2,1,0:T(8,128)}, u32[]{:S(2)}) copy-start(f32[1,128,128]{2,1,0:T(8,128)} %w_in.1) | copy-start | bytes 196612
  2.9 0.7 %copy-start.2 = (s32[1,16,32]{2,1,0:T(8,128)S(1)}, s32[1,16,32]{2,1,0:T(8,128)}, u32[]{:S(2)}) copy-start(s32[1,16,32]{2,1,0:T(8,128)} %param.9) | copy-start | bytes 6148
  3.6 0.7 copy-start.3
  18.5 1.6 %copy-start = (f32[4,1024,128]{2,1,0:T(8,128)S(1)}, f32[4,1024,128]{2,1,0:T(8,128)}, u32[]{:S(2)}) copy-start(f32[4,1024,128]{2,1,0:T(8,128)} %param.6) | copy-start | bytes 6291460

commit v2 on v1

--- a/solution.py
+++ b/solution.py
@@ -13,8 +13,8 @@
 MICRO = 4
 BLOCK = 1024
 ROWS = MICRO * BLOCK
-GROUP = 16
-STEP = 256
+GROUP = 8
+CHUNK = 256
 f32, bf16, i32 = jnp.float32, jnp.bfloat16, jnp.int32
 MESH = pl.DeviceIdType.MESH
 VM, SM, HB = pltpu.VMEM, pltpu.SMEM, pltpu.HBM
@@ -24,17 +24,41 @@
     return pl.BlockSpec(memory_space=space)
 
 
+def pinned(x):
+    return pltpu.with_memory_space_constraint(x, HB)
+
+
 def high_low(x):
     high = x.astype(bf16)
     return high, (x - high.astype(f32)).astype(bf16)
 
 
-def exchange_kernel(w_in, b_in, p_in, keys, valid, w_all, b_all, same, level, counts, words_v, words, send, recv, local):
+def exchange_kernel(
+    w_in, b_in, p_in, k_in, v_in,
+    w_all, b_all, same, level, counts, table_a, table_b,
+    keys, key_rows, valid, words_v, words, send, recv, local,
+):
     me = lax.axis_index("section")
     row = lax.axis_index("rows")
+    own = [
+        pltpu.make_async_copy(src, dst, local.at[n])
+        for n, (src, dst) in enumerate((
+            (k_in, keys), (v_in, valid), (p_in.at[me], words_v.at[me]),
+            (b_in.at[0], b_all.at[me]), (w_in.at[0], w_all.at[me])))
+    ]
+    for copy in own:
+        copy.start()
     barrier = pltpu.get_barrier_semaphore()
     for k in range(1, 4):
         pl.semaphore_signal(barrier, inc=1, device_id=(lax.rem(me + k, 4), row), device_id_type=MESH)
+
+    def clear(i, carry):
+        at = pl.ds(pl.multiple_of(i * 512, 512), 512)
+        table_a[at, :] = jnp.zeros((512, D), f32)
+        table_b[at, :] = jnp.zeros((512, D), f32)
+        return carry
+
+    lax.fori_loop(0, KEYS // 512, clear, 0)
     pl.semaphore_wait(barrier, 3)
     copies = []
     for n, k in enumerate((2, 1, 3)):
@@ -49,27 +73,30 @@
         for which, copy in copies:
             if which == a:
                 copy.start()
-    own = [
-        pltpu.make_async_copy(p_in.at[me], words_v.at[me], local.at[0]),
-        pltpu.make_async_copy(b_in.at[0], b_all.at[me], local.at[1]),
-        pltpu.make_async_copy(w_in.at[0], w_all.at[me], local.at[2]),
-    ]
-    for copy in own:
-        copy.start()
+    own[0].wait()
+    own[1].wait()
     group_i = (lax.broadcasted_iota(i32, (1, 128), 1) // GROUP) * KEYS
 
-    def sameness(j, carry):
-        key_row = keys[pl.ds(j, 1), :] + group_i
-        key_col = jnp.transpose(jnp.broadcast_to(key_row, (128, 128)))
-        same[j] = jnp.where(key_col == key_row, 1.0, 0.0).astype(bf16)
-        return carry
-
-    lax.fori_loop(0, 32, sameness, 0)
-    own[0].wait()
+    for m in range(MICRO):
+        for j in range(8):
+            key_rows[m * 8 + j : m * 8 + j + 1, :] = keys[m : m + 1, j * 128 : (j + 1) * 128]
+
+    def key_row_at(m, j):
+        return key_rows[pl.ds(m * 8 + j, 1), :]
+
+    def sameness(i, carry):
+        for u in range(4):
+            key_row = key_row_at(i // 2, (i % 2) * 4 + u) + group_i
+            key_col = jnp.transpose(jnp.broadcast_to(key_row, (128, 128)))
+            same[i * 4 + u] = jnp.where(key_col == key_row, 1.0, 0.0).astype(bf16)
+        return carry
+
+    lax.fori_loop(0, 8, sameness, 0)
+    own[2].wait()
     for which, copy in copies:
         if which == 0:
             copy.wait()
-    to_scalar = pltpu.make_async_copy(words_v, words, local.at[3])
+    to_scalar = pltpu.make_async_copy(words_v, words, local.at[5])
     to_scalar.start()
     to_scalar.wait()
     counts[...] = jnp.zeros_like(counts)
@@ -77,29 +104,36 @@
     sub64 = lax.broadcasted_iota(i32, (64, 128), 0)
     sub128 = lax.broadcasted_iota(i32, (128, 128), 0)
 
-    def tally(j, carry):
-        m = j // 8
-        first = (j % 8) * 4
-        nv = valid[m, 0]
-        total = jnp.zeros((64, 128), i32)
-        alive = []
-        for w in range(4):
-            n = nv - (first + w) * 32
-            alive.append(jnp.where(n >= 32, jnp.int32(-1), (jnp.int32(1) << jnp.clip(n, 0, 31)) - 1))
-        for s in range(SECTIONS):
-            alive = [a & words[s, m, first + w] for w, a in enumerate(alive)]
-            v = jnp.where(lane < 64, jnp.where(lane < 32, alive[0], alive[1]), jnp.where(lane < 96, alive[2], alive[3]))
-            total = total + ((v >> (lane & 31)) & 1)
-        key_row = keys[pl.ds(j, 1), :]
-        high = jnp.where((key_row >> 7) == sub64, total.astype(f32), 0.0).astype(bf16)
-        low = jnp.where((key_row & 127) == sub128, 1.0, 0.0).astype(bf16)
-        counts[...] += lax.dot_general(high, low, (((1,), (1,)), ((), ())), preferred_element_type=f32)
-        level[j] = jnp.transpose(jnp.concatenate([total, total], axis=0))
-        return carry
-
-    lax.fori_loop(0, 32, tally, 0)
-    own[1].wait()
-    own[2].wait()
+    def tally(i, carry):
+        m = i // 2
+        nv = valid[0, m]
+        found = jnp.zeros((64, 128), f32)
+        for u in range(4):
+            j = (i % 2) * 4 + u
+            total = jnp.zeros((8, 128), i32)
+            alive = []
+            for w in range(4):
+                n = nv - (j * 4 + w) * 32
+                alive.append(jnp.where(n >= 32, jnp.int32(-1), (jnp.int32(1) << jnp.clip(n, 0, 31)) - 1))
+            for s in range(SECTIONS):
+                alive = [a & words[s, m, j * 4 + w] for w, a in enumerate(alive)]
+                v = jnp.where(
+                    lane[:8] < 64,
+                    jnp.where(lane[:8] < 32, alive[0], alive[1]),
+                    jnp.where(lane[:8] < 96, alive[2], alive[3]))
+                total = total + ((v >> (lane[:8] & 31)) & 1)
+            key_row = key_row_at(m, j)
+            lives = jnp.concatenate([total] * 8, axis=0).astype(f32)
+            high = jnp.where((key_row >> 7) == sub64, lives, 0.0).astype(bf16)
+            low = jnp.where((key_row & 127) == sub128, 1.0, 0.0).astype(bf16)
+            found = found + lax.dot_general(high, low, (((1,), (1,)), ((), ())), preferred_element_type=f32)
+            level[i * 4 + u] = jnp.transpose(jnp.concatenate([total] * 16, axis=0))
+        counts[...] += found
+        return carry
+
+    lax.fori_loop(0, 8, tally, 0)
+    own[3].wait()
+    own[4].wait()
     for which, copy in copies:
         if which != 0:
             copy.wait()
@@ -114,80 +148,95 @@
             jax.ShapeDtypeStruct((32, 128, 128), bf16),
             jax.ShapeDtypeStruct((32, 128, 128), i32),
             jax.ShapeDtypeStruct((64, 128), f32),
+            jax.ShapeDtypeStruct((KEYS, D), f32),
+            jax.ShapeDtypeStruct((KEYS, D), f32),
         ),
-        in_specs=[spec(HB), spec(HB), spec(HB), spec(VM), spec(SM)],
-        out_specs=(spec(VM),) * 5,
+        in_specs=[spec(HB)] * 5,
+        out_specs=(spec(VM),) * 7,
         scratch_shapes=[
+            pltpu.VMEM((MICRO, BLOCK), i32),
+            pltpu.VMEM((32, 128), i32),
+            pltpu.SMEM((1, MICRO), i32),
             pltpu.VMEM((4, 4, 32), i32),
             pltpu.SMEM((4, 4, 32), i32),
             pltpu.SemaphoreType.DMA((3, 3)),
             pltpu.SemaphoreType.DMA((3, 3)),
-            pltpu.SemaphoreType.DMA((4,)),
+            pltpu.SemaphoreType.DMA((6,)),
         ],
         compiler_params=pltpu.CompilerParams(collective_id=0, has_side_effects=True, vmem_limit_bytes=8 << 20),
-    )(weight, bias, predicates, keys, valid)
-
-
-def sections_kernel(rows_in, keys, w, b, same, level, table, rows, w2, ready, sem):
-    fetch = pltpu.make_async_copy(rows_in, rows, sem)
+        cost_estimate=pl.CostEstimate(flops=40_000_000_000, bytes_accessed=1 << 20, transcendentals=0),
+    )(pinned(weight), pinned(bias), pinned(predicates), pinned(keys), pinned(valid))
+
+
+def sections_kernel(rows, keys_in, w, b, same, level, clear_a, clear_b, table_a, table_b, w2, ready, keys, sem):
+    fetch = pltpu.make_async_copy(keys_in, keys, sem)
     fetch.start()
     for s in range(SECTIONS):
         top = jnp.concatenate(high_low(w[s]), axis=1)
         w2[s] = jnp.concatenate([top, top], axis=0)
 
-    def clear(i, carry):
-        table[pl.ds(pl.multiple_of(i * 256, 256), 256), :] = jnp.zeros((256, D), f32)
-        return carry
-
-    lax.fori_loop(0, KEYS // 256, clear, 0)
-    fetch.wait()
-
-    def compute(t, slot):
-        h = rows[pl.ds(pl.multiple_of(t * STEP, STEP), STEP), :]
-        lev = level[pl.ds(t * (STEP // 128), STEP // 128)].reshape(STEP, 128)
-        acc = jnp.zeros((STEP, D), f32)
+    def batch(m, carry):
+        h = rows[m]
+        alive = level[pl.ds(m * 8, 8)].reshape(BLOCK, 128)
+        total = jnp.zeros((BLOCK, D), f32)
         for s in range(SECTIONS):
             p = jnp.dot(jnp.concatenate(high_low(h), axis=1), w2[s], preferred_element_type=f32)
             h = h + jnp.tanh(p[:, :D] + (p[:, D:] + b[s]))
-            acc = acc + jnp.where(lev > s, h, 0.0)
-        both = jnp.concatenate(high_low(acc), axis=1)
-        for j in range(STEP // 128):
-            p = jnp.dot(same[t * (STEP // 128) + j], both[j * 128 : (j + 1) * 128], preferred_element_type=f32)
-            ready[slot, j * 128 : (j + 1) * 128, :] = p[:, :D] + p[:, D:]
-
-    def scatter(t, slot):
-        for g in range(STEP // GROUP):
-            at = [keys[t * (STEP // 128) + (g * GROUP + i) // 128, (g * GROUP + i) % 128] for i in range(GROUP)]
-            held = [table[pl.ds(k, 1), :] for k in at]
-            new = [held[i] + ready[slot, g * GROUP + i : g * GROUP + i + 1, :] for i in range(GROUP)]
-            for i in range(GROUP):
-                table[pl.ds(at[i], 1), :] = new[i]
-
-    compute(0, 0)
-
-    def body(t, carry):
-        compute(t, t % 2)
-        scatter(t - 1, (t - 1) % 2)
-        return carry
-
-    lax.fori_loop(1, ROWS // STEP, body, 0)
-    scatter(ROWS // STEP - 1, (ROWS // STEP - 1) % 2)
-
-
-def sections(rows, keys, w, b, same, level):
+            total = total + jnp.where(alive > s, h, 0.0)
+        both = jnp.concatenate(high_low(total), axis=1)
+        for j in range(8):
+            p = jnp.dot(same[m * 8 + j], both[j * 128 : (j + 1) * 128], preferred_element_type=f32)
+            ready[m, j * 128 : (j + 1) * 128, :] = p[:, :D] + p[:, D:]
+        return carry
+
+    lax.fori_loop(0, MICRO, batch, 0)
+    fetch.wait()
+    tables = (table_a, table_b)
+    groups = CHUNK // GROUP
+
+    def scatter(u, carry):
+        m, base = u // (BLOCK // CHUNK), (u % (BLOCK // CHUNK)) * CHUNK
+
+        def load(g):
+            at = [keys[m, base + g * GROUP + i] for i in range(GROUP)]
+            return at, [tables[g % 2][pl.ds(k, 1), :] for k in at]
+
+        def store(g, at, held):
+            for i, k in enumerate(at):
+                tables[g % 2][pl.ds(k, 1), :] = held[i] + ready[m, pl.ds(base + g * GROUP + i, 1), :]
+
+        flying = {g: load(g) for g in range(2)}
+        for g in range(groups):
+            store(g, *flying.pop(g))
+            if g + 2 < groups:
+                flying[g + 2] = load(g + 2)
+        return carry
+
+    lax.fori_loop(0, ROWS // CHUNK, scatter, 0)
+
+    def join(i, carry):
+        at = pl.ds(pl.multiple_of(i * 512, 512), 512)
+        table_a[at, :] += table_b[at, :]
+        return carry
+
+    lax.fori_loop(0, KEYS // 512, join, 0)
+
+
+def sections(rows, keys, w, b, same, level, clear_a, clear_b):
     return pl.pallas_call(
         sections_kernel,
-        out_shape=jax.ShapeDtypeStruct((KEYS, D), f32),
-        in_specs=[spec(HB), spec(SM)] + [spec(VM)] * 4,
-        out_specs=spec(VM),
+        out_shape=(jax.ShapeDtypeStruct((KEYS, D), f32),) * 2,
+        in_specs=[spec(VM), spec(HB)] + [spec(VM)] * 6,
+        out_specs=(spec(VM),) * 2,
         scratch_shapes=[
-            pltpu.VMEM((ROWS, D), f32),
             pltpu.VMEM((SECTIONS, 256, 256), bf16),
-            pltpu.VMEM((2, STEP, D), f32),
+            pltpu.VMEM((MICRO, BLOCK, D), f32),
+            pltpu.SMEM((MICRO, BLOCK), i32),
             pltpu.SemaphoreType.DMA,
         ],
-        compiler_params=pltpu.CompilerParams(vmem_limit_bytes=16 << 20),
-    )(rows, keys, w, b, same, level)
+        input_output_aliases={6: 0, 7: 1},
+        compiler_params=pltpu.CompilerParams(vmem_limit_bytes=12 << 20),
+    )(rows, pinned(keys), w, b, same, level, clear_a, clear_b)[0]
 
 
 PARTS = ((0, 24), (24, 24), (48, 16))
@@ -306,10 +355,9 @@
 
 
 def shards(rows_data, row_keys, valid_counts, predicates, section_weight, section_bias):
-    keys = row_keys.reshape(32, 128)
-    w, b, same, level, counts = exchange(
-        section_weight, section_bias.reshape(1, 1, D), predicates.reshape(4, MICRO, 32), keys, valid_counts)
-    table = sections(rows_data.reshape(ROWS, D), keys, w, b, same, level)
+    w, b, same, level, counts, clear_a, clear_b = exchange(
+        section_weight, section_bias.reshape(1, 1, D), predicates.reshape(4, MICRO, 32), row_keys, valid_counts.T)
+    table = sections(rows_data, row_keys, w, b, same, level, clear_a, clear_b)
     means, total = reduce_to_owner(table, counts)
     return means, total[0, :64]
 

time: 66.9 us -> 55.1 us (0.82)
  Pallas kernels: 59.6 us -> 53.2 us
  local copies, waits for them, and re-layouts: 6.37 us -> 1.13 us
    unnamed x10 -> x3, local copies, waits for them, and re-layouts: 5.13 us -> 0.62 us
    pallas_call x1, Pallas kernels: 14.2 us -> 10.7 us  [exchange(): pl.pallas_call(exchange_kernel, out_shape=(jax.ShapeDtypeStruct((4, D, D)...]
    pallas_call x1, Pallas kernels: 17.9 us -> 15 us  [sections(): pl.pallas_call(sections_kernel, out_shape=(jax.ShapeDtypeStruct((KEYS, D)...]
    reshape x1 -> x0, local copies, waits for them, and re-layouts: 0.73 us -> none  [shards(): keys = row_keys.reshape(32, 128)]
where the time goes in v2:
time: 55.1 us; the launch traced here: 55 us
  Pallas kernels  53.2 us (97%)
  local copies, waits for them, and re-layouts  1.13 us (2%)
  between operations  0.67 us (1%)
    pallas_call x1, Pallas kernels, reduce_to_owner(): pl.pallas_call(reduce_kernel, out_shape=(jax.ShapeDtypeStruct((64, D), f3...  27.6 us
    pallas_call x1, Pallas kernels, sections(): pl.pallas_call(sections_kernel, out_shape=(jax.ShapeDtypeStruct((KEYS, D)...  15 us
    pallas_call x1, Pallas kernels, exchange(): pl.pallas_call(exchange_kernel, out_shape=(jax.ShapeDtypeStruct((4, D, D)...  10.7 us

profile of v2, /device:TPU:0, one launch (start us, length us, event | category | flops | bytes accessed | tf_op | source)
XLA Modules:
  0.0 55.0 jit_solution(4424526995877584658)
XLA Ops:
  0.6 0.0 copy-start
  0.6 10.7 %shard_map.77 = (f32[4,128,128]{2,1,0:T(8,128)S(1)}, f32[4,1,128]{2,1,0:T(1,128)S(1)}, bf16[32,128,128]{2,1,0:T(8,128)(2,1)S(1)}, s32[32,128,128]{2,1,0:T(8,128)...) custom-call(f32[1,128,128]{2,1,0:T(8,128)} %w_in.1, f32[1,1,128]{2,1,0:T(1,128)} %bitcast.10, ...), custom_call_target="tpu_custom_call" | custom-call | flops 40000000000 | bytes 1048576 | tf_op jit(solution)/shard_map/pallas_call | solution.py:143
  11.3 0.0 copy-done
  11.3 15.0 %shard_map.78 = (f32[8192,128]{1,0:T(8,128)S(1)}, f32[8192,128]{1,0:T(8,128)S(1)}) custom-call(f32[4,1024,128]{2,1,0:T(8,128)S(1)} %copy-done, s32[4,1024]{1,0:T(4,128)} %keys_in.1, f32[4,128,128]{2,1,0:T(8,128)S(1)} %get-tuple-element.12.w, f32[4,1,128]{2,1,0:T(1,128)S(1)} %get-tuple-element.13.b, ...), custom_call_target="tpu_custom_call", output_to_operand_aliasing={{0}: (6, {}), {1}: (7, {})} | custom-call | tf_op jit(solution)/shard_map/pallas_call | solution.py:226
  26.3 27.6 %shard_map.79 = (f32[64,128]{1,0:T(8,128)S(1)}, f32[8,128]{1,0:T(8,128)S(1)}) custom-call(f32[4,4,4,2,64,128]{5,4,3,2,1,0:T(8,128)S(1)} %bitcast.7, f32[4,4,4,1,128]{4,3,2,1,0:T(1,128)S(1)} %bitcast.8), custom_call_target="tpu_custom_call" | custom-call | tf_op jit(solution)/shard_map/pallas_call | solution.py:343
  53.9 0.5 slice_bitcast_fusion
  54.4 0.6 %copy.13 = f32[64,128]{1,0:T(8,128)} copy(f32[64,128]{1,0:T(8,128)S(1)} %get-tuple-element.24) | data formatting | bytes 65536
Async XLA Ops:
  0.6 10.7 %copy-start = (f32[4,1024,128]{2,1,0:T(8,128)S(1)}, f32[4,1024,128]{2,1,0:T(8,128)}, u32[]{:S(2)}) copy-start(f32[4,1024,128]{2,1,0:T(8,128)} %rows.1) | copy-start | bytes 6291460

commit v3 on v2

--- a/solution.py
+++ b/solution.py
@@ -35,8 +35,8 @@
 
 def exchange_kernel(
     w_in, b_in, p_in, k_in, v_in,
-    w_all, b_all, same, level, counts, table_a, table_b,
-    keys, key_rows, valid, words_v, words, send, recv, local,
+    w_all, b_all, same, level, counts, table_a, table_b, key_rows,
+    keys, valid, words_v, words, send, recv, local,
 ):
     me = lax.axis_index("section")
     row = lax.axis_index("rows")
@@ -150,12 +150,12 @@
             jax.ShapeDtypeStruct((64, 128), f32),
             jax.ShapeDtypeStruct((KEYS, D), f32),
             jax.ShapeDtypeStruct((KEYS, D), f32),
+            jax.ShapeDtypeStruct((32, 128), i32),
         ),
         in_specs=[spec(HB)] * 5,
-        out_specs=(spec(VM),) * 7,
+        out_specs=(spec(VM),) * 8,
         scratch_shapes=[
             pltpu.VMEM((MICRO, BLOCK), i32),
-            pltpu.VMEM((32, 128), i32),
             pltpu.SMEM((1, MICRO), i32),
             pltpu.VMEM((4, 4, 32), i32),
             pltpu.SMEM((4, 4, 32), i32),
@@ -186,7 +186,7 @@
         both = jnp.concatenate(high_low(total), axis=1)
         for j in range(8):
             p = jnp.dot(same[m * 8 + j], both[j * 128 : (j + 1) * 128], preferred_element_type=f32)
-            ready[m, j * 128 : (j + 1) * 128, :] = p[:, :D] + p[:, D:]
+            ready[pl.ds(pl.multiple_of(m * BLOCK + j * 128, 128), 128), :] = p[:, :D] + p[:, D:]
         return carry
 
     lax.fori_loop(0, MICRO, batch, 0)
@@ -195,15 +195,13 @@
     groups = CHUNK // GROUP
 
     def scatter(u, carry):
-        m, base = u // (BLOCK // CHUNK), (u % (BLOCK // CHUNK)) * CHUNK
-
         def load(g):
-            at = [keys[m, base + g * GROUP + i] for i in range(GROUP)]
+            at = [keys[u * (CHUNK // 128) + (g * GROUP + i) // 128, (g * GROUP + i) % 128] for i in range(GROUP)]
             return at, [tables[g % 2][pl.ds(k, 1), :] for k in at]
 
         def store(g, at, held):
             for i, k in enumerate(at):
-                tables[g % 2][pl.ds(k, 1), :] = held[i] + ready[m, pl.ds(base + g * GROUP + i, 1), :]
+                tables[g % 2][pl.ds(k, 1), :] = held[i] + ready[pl.ds(u * CHUNK + g * GROUP + i, 1), :]
 
         flying = {g: load(g) for g in range(2)}
         for g in range(groups):
@@ -226,138 +224,155 @@
     return pl.pallas_call(
         sections_kernel,
         out_shape=(jax.ShapeDtypeStruct((KEYS, D), f32),) * 2,
-        in_specs=[spec(VM), spec(HB)] + [spec(VM)] * 6,
+        in_specs=[spec(VM)] * 8,
         out_specs=(spec(VM),) * 2,
         scratch_shapes=[
             pltpu.VMEM((SECTIONS, 256, 256), bf16),
-            pltpu.VMEM((MICRO, BLOCK, D), f32),
-            pltpu.SMEM((MICRO, BLOCK), i32),
+            pltpu.VMEM((ROWS, D), f32),
+            pltpu.SMEM((32, 128), i32),
             pltpu.SemaphoreType.DMA,
         ],
         input_output_aliases={6: 0, 7: 1},
         compiler_params=pltpu.CompilerParams(vmem_limit_bytes=12 << 20),
-    )(rows, pinned(keys), w, b, same, level, clear_a, clear_b)[0]
-
-
-PARTS = ((0, 24), (24, 24), (48, 16))
-ORDER = ((0, 1, 2), (1, 2, 0), (2, 0, 1), (2, 0, 1))
+    )(rows, keys, w, b, same, level, clear_a, clear_b)[0]
+
+
+PARTS = ((0, 1, (2, 0, 1)), (0, 24, (0, 1, 2)), (24, 24, (1, 2, 0)), (48, 16, (2, 0, 1)))
+N = len(PARTS)
 
 
 def reduce_kernel(table, counts, means, count_out, *scratch):
-    held = scratch[0:4]
-    first = scratch[4:8]
-    middle = scratch[8:12]
-    second = scratch[12:16]
-    last = scratch[16:20]
-    third = scratch[20:24]
-    core_sems, send, recv = scratch[24:27]
+    held, near, middle, second, last, third = (scratch[i * N : (i + 1) * N] for i in range(6))
+    core_sems, near_send, near_recv, send, recv = scratch[6 * N :]
     z = lax.axis_index("section")
     row = lax.axis_index("rows")
     y, x, c = row // 8, (row // 2) % 4, row % 2
     place = (z, y, x)
 
-    def peer(axis, k):
+    def position(axis, k):
+        return lax.rem(place[axis] + k, 4)
+
+    def device(axis, k):
         at = list(place)
-        at[axis] = lax.rem(at[axis] + k, 4)
-        return at[axis], (at[0], at[1] * 8 + at[2] * 2 + c)
+        at[axis] = position(axis, k)
+        return (at[0], at[1] * 8 + at[2] * 2 + c)
 
     other = (z, y * 8 + x * 2 + (1 - c))
     barrier = pltpu.get_barrier_semaphore()
     pl.semaphore_signal(barrier, inc=1, device_id=other, device_id_type=MESH)
     for axis in range(3):
         for k in range(1, 4):
-            pl.semaphore_signal(barrier, inc=1, device_id=peer(axis, k)[1], device_id_type=MESH)
+            pl.semaphore_signal(barrier, inc=1, device_id=device(axis, k), device_id_type=MESH)
     pl.semaphore_wait(barrier, 10)
 
-    core = []
-    for n in (3, 0, 1, 2):
-        if n < 3:
-            src = table.at[:, :, :, 1 - c, pl.ds(PARTS[n][0], PARTS[n][1]), :]
-        else:
-            src = counts
+    def remote(src, dst, send_sem, recv_sem, to):
         copy = pltpu.make_async_remote_copy(
-            src_ref=src, dst_ref=held[n], send_sem=core_sems.at[0, n], recv_sem=core_sems.at[1, n],
-            device_id=other, device_id_type=MESH)
+            src_ref=src, dst_ref=dst, send_sem=send_sem, recv_sem=recv_sem, device_id=to, device_id_type=MESH)
         copy.start()
-        core.append((n, copy))
-
-    def piece(ref, axes, axis, index):
+        return copy
+
+    def piece(ref, axes, axis, index, half=None):
         where = [slice(None)] * len(axes)
         where[axes.index(axis)] = index
+        if half is not None:
+            where[1 if axes[0] == axis else 0] = pl.ds(2 * half, 2)
         return ref.at[tuple(where)]
 
-    def send_stage(n, stage, source, axes, target):
-        axis = ORDER[n][stage]
-        copies = []
-        for k in (2, 1, 3):
-            index, device = peer(axis, k)
-            copy = pltpu.make_async_remote_copy(
-                src_ref=piece(source, axes, axis, index), dst_ref=target.at[k - 1],
-                send_sem=send.at[n, stage, k - 1], recv_sem=recv.at[n, stage, k - 1],
-                device_id=device, device_id_type=MESH)
-            copy.start()
-            copies.append(copy)
-        return copies
+    every = [0, 1, 2]
+    core = []
+    for n, (start, size, order) in enumerate(PARTS):
+        src = counts if n == 0 else table.at[:, :, :, 1 - c, pl.ds(start, size), :]
+        core.append(remote(src, held[n], core_sems.at[0, n], core_sems.at[1, n], other))
+
+    sent = [[] for _ in PARTS]
+    relay = [None] * N
+    for n, (start, size, order) in enumerate(PARTS):
+        core[n].wait()
+        if n == 0:
+            held[n][...] += counts[...]
+        else:
+            for a in range(4):
+                held[n][a] += table[a, :, :, c, start : start + size, :]
+        axis = order[0]
+
+        def hop(slot, index, half, k):
+            return remote(
+                piece(held[n], every, axis, index, half), near[n].at[slot],
+                near_send.at[n, slot], near_recv.at[n, slot], device(axis, k))
+
+        relay[n] = [hop(0, position(axis, 2), 0, 1), hop(1, position(axis, 2), 1, 3)]
+        sent[n] = [hop(2, position(axis, 1), 1, 1), hop(3, position(axis, 3), 0, 3)]
+    for n, (start, size, order) in enumerate(PARTS):
+        axis = order[0]
+        for half, k in ((0, 1), (1, 3)):
+            relay[n][half].wait()
+            block = piece(held[n], every, axis, position(axis, k), half)
+            block[...] += near[n][half]
+            sent[n].append(remote(
+                block, near[n].at[4 + half], near_send.at[n, 4 + half], near_recv.at[n, 4 + half], device(axis, k)))
+
+    def spread(n, stage, source, axes, target):
+        axis = PARTS[n][2][stage]
+        return [
+            remote(
+                piece(source, axes, axis, position(axis, k)), target.at[k - 1],
+                send.at[n, stage - 1, k - 1], recv.at[n, stage - 1, k - 1], device(axis, k))
+            for k in (2, 1, 3)
+        ]
 
     def summed(n, stage, source, axes, target):
-        mine = piece(source, axes, ORDER[n][stage], place[ORDER[n][stage]])[...]
-        return (mine + target[0]) + (target[1] + target[2])
-
-    axes = [[0, 1, 2] for _ in range(4)]
-    flying = {}
-    for n, copy in core:
-        copy.wait()
-        if n < 3:
-            for a in range(4):
-                held[n][a] += table[a, :, :, c, PARTS[n][0] : PARTS[n][0] + PARTS[n][1], :]
+        axis = PARTS[n][2][stage]
+        return (piece(source, axes, axis, place[axis])[...] + target[0]) + (target[1] + target[2])
+
+    for n, (start, size, order) in enumerate(PARTS):
+        for copy in sent[n]:
+            copy.wait()
+        axis = order[0]
+        middle[n][0:2] = (piece(held[n], every, axis, place[axis], 0)[...] + near[n][3]) + near[n][4]
+        middle[n][2:4] = (piece(held[n], every, axis, place[axis], 1)[...] + near[n][2]) + near[n][5]
+        sent[n] = spread(n, 1, middle[n], [a for a in every if a != axis], second[n])
+    for n, (start, size, order) in enumerate(PARTS):
+        for copy in sent[n]:
+            copy.wait()
+        axes = [a for a in every if a != order[0]]
+        last[n][...] = summed(n, 1, middle[n], axes, second[n])
+        sent[n] = spread(n, 2, last[n], [order[2]], third[n])
+    for n, (start, size, order) in enumerate(PARTS):
+        for copy in sent[n]:
+            copy.wait()
+        value = summed(n, 2, last[n], [order[2]], third[n])
+        if n == 0:
+            wide = jnp.transpose(jnp.broadcast_to(value, (128, 128)))
+            total = jnp.maximum(jnp.where(c == 0, wide[:64], wide[64:]), 1.0)
+            count_out[...] = jnp.broadcast_to(jnp.where(c == 0, value, pltpu.roll(value, 64, 1)), (8, 128))
         else:
-            held[n][...] += counts[...]
-        flying[n] = send_stage(n, 0, held[n], axes[n], first[n])
-    for stage, (source, target, result) in enumerate(((held, first, middle), (middle, second, last))):
-        for n in (3, 0, 1, 2) if stage else (3, 2, 0, 1):
-            for copy in flying[n]:
-                copy.wait()
-            result[n][...] = summed(n, stage, source[n], axes[n], target[n])
-            axes[n] = [a for a in axes[n] if a != ORDER[n][stage]]
-            flying[n] = send_stage(n, stage + 1, result[n], axes[n], (second, third)[stage][n])
-    total = None
-    for n in (3, 0, 1, 2):
-        for copy in flying[n]:
-            copy.wait()
-        value = summed(n, 2, last[n], axes[n], third[n])
-        if n == 3:
-            wide = jnp.transpose(jnp.broadcast_to(value, (128, 128)))
-            total = jnp.where(c == 0, wide[:64], wide[64:])
-            count_out[...] = jnp.broadcast_to(jnp.where(c == 0, value, pltpu.roll(value, 64, 1)), (8, 128))
-            total = jnp.maximum(total, 1.0)
-        else:
-            lo, size = PARTS[n]
-            means[lo : lo + size, :] = value / total[lo : lo + size]
+            means[start : start + size, :] = value / total[start : start + size]
 
 
 def reduce_to_owner(table, counts):
-    sizes = [24, 24, 16, 1]
     buffers = []
-    for lead in ((4, 4, 4), (3, 4, 4), (4, 4), (3, 4), (4,), (3,)):
-        buffers += [pltpu.VMEM((*lead, n, D), f32) for n in sizes]
+    for lead in ((4, 4, 4), (6, 2, 4), (4, 4), (3, 4), (4,), (3,)):
+        buffers += [pltpu.VMEM((*lead, size, D), f32) for _, size, _ in PARTS]
     return pl.pallas_call(
         reduce_kernel,
         out_shape=(jax.ShapeDtypeStruct((64, D), f32), jax.ShapeDtypeStruct((8, D), f32)),
         in_specs=[spec(VM), spec(VM)],
         out_specs=(spec(VM), spec(VM)),
         scratch_shapes=buffers + [
-            pltpu.SemaphoreType.DMA((2, 4)),
-            pltpu.SemaphoreType.DMA((4, 3, 3)),
-            pltpu.SemaphoreType.DMA((4, 3, 3)),
+            pltpu.SemaphoreType.DMA((2, N)),
+            pltpu.SemaphoreType.DMA((N, 6)),
+            pltpu.SemaphoreType.DMA((N, 6)),
+            pltpu.SemaphoreType.DMA((N, 2, 3)),
+            pltpu.SemaphoreType.DMA((N, 2, 3)),
         ],
         compiler_params=pltpu.CompilerParams(collective_id=1, has_side_effects=True, vmem_limit_bytes=16 << 20),
     )(table.reshape(4, 4, 4, 2, 64, D), counts.reshape(4, 4, 4, 1, D))
 
 
 def shards(rows_data, row_keys, valid_counts, predicates, section_weight, section_bias):
-    w, b, same, level, counts, clear_a, clear_b = exchange(
+    w, b, same, level, counts, clear_a, clear_b, key_rows = exchange(
         section_weight, section_bias.reshape(1, 1, D), predicates.reshape(4, MICRO, 32), row_keys, valid_counts.T)
-    table = sections(rows_data, row_keys, w, b, same, level, clear_a, clear_b)
+    table = sections(rows_data, key_rows, w, b, same, level, clear_a, clear_b)
     means, total = reduce_to_owner(table, counts)
     return means, total[0, :64]
 

time: 55.1 us -> 47.9 us (0.87)
  Pallas kernels: 53.2 us -> 46 us
    pallas_call x1, Pallas kernels: 15 us -> 8.28 us  [sections(): pl.pallas_call(sections_kernel, out_shape=(jax.ShapeDtypeStruct((KEYS, D)...]
where the time goes in v3:
time: 47.9 us; the launch traced here: 47.8 us
  Pallas kernels  46 us (96%)
  local copies, waits for them, and re-layouts  1.13 us (2%)
  between operations  0.67 us (1%)
    pallas_call x1, Pallas kernels, reduce_to_owner(): pl.pallas_call(reduce_kernel, out_shape=(jax.ShapeDtypeStruct((64, D), f3...  27.1 us
    pallas_call x1, Pallas kernels, exchange(): pl.pallas_call(exchange_kernel, out_shape=(jax.ShapeDtypeStruct((4, D, D)...  10.7 us
    pallas_call x1, Pallas kernels, sections(): pl.pallas_call(sections_kernel, out_shape=(jax.ShapeDtypeStruct((KEYS, D)...  8.28 us

profile of v3, /device:TPU:0, one launch (start us, length us, event | category | flops | bytes accessed | tf_op | source)
XLA Modules:
  0.0 47.8 jit_solution(537980877422918117)
XLA Ops:
  0.6 0.0 copy-start
  0.6 10.7 %shard_map.77 = (f32[4,128,128]{2,1,0:T(8,128)S(1)}, f32[4,1,128]{2,1,0:T(1,128)S(1)}, bf16[32,128,128]{2,1,0:T(8,128)(2,1)S(1)}, s32[32,128,128]{2,1,0:T(8,128)...) custom-call(f32[1,128,128]{2,1,0:T(8,128)} %w_in.1, ...), custom_call_target="tpu_custom_call" | custom-call | flops 40000000000 | bytes 1048576 | tf_op jit(solution)/shard_map/pallas_call | solution.py:143
  11.3 0.0 copy-done
  11.3 8.3 %shard_map.78 = (f32[8192,128]{1,0:T(8,128)S(1)}, f32[8192,128]{1,0:T(8,128)S(1)}) custom-call(f32[4,1024,128]{2,1,0:T(8,128)S(1)} %copy-done, s32[32,128]{1,0:T(8,128)S(1)} %get-tuple-element.13.keys_in, f32[4,128,128]{2,1,0:T(8,128)S(1)} %get-tuple-element.14.w, ...), custom_call_target="tpu_custom_call", output_to_operand_aliasing={{0}: (6, {}), {1}: (7, {})} | custom-call | tf_op jit(solution)/shard_map/pallas_call | solution.py:224
  19.6 27.1 %shard_map.79 = (f32[64,128]{1,0:T(8,128)S(1)}, f32[8,128]{1,0:T(8,128)S(1)}) custom-call(f32[4,4,4,2,64,128]{5,4,3,2,1,0:T(8,128)S(1)} %bitcast.7, f32[4,4,4,1,128]{4,3,2,1,0:T(1,128)S(1)} %bitcast.8), custom_call_target="tpu_custom_call" | custom-call | tf_op jit(solution)/shard_map/pallas_call | solution.py:356
  46.7 0.5 %slice_bitcast_fusion = f32[64]{0:T(128)} fusion(f32[8,128]{1,0:T(8,128)S(1)} %get-tuple-element.23), kind=kLoop, calls=%fused_computation | loop fusion | bytes 512 | tf_op jit(solution)/shard_map/squeeze | solution.py:377
  47.2 0.6 %copy.13 = f32[64,128]{1,0:T(8,128)} copy(f32[64,128]{1,0:T(8,128)S(1)} %get-tuple-element.26) | data formatting | bytes 65536
Async XLA Ops:
  0.6 10.7 %copy-start = (f32[4,1024,128]{2,1,0:T(8,128)S(1)}, f32[4,1024,128]{2,1,0:T(8,128)}, u32[]{:S(2)}) copy-start(f32[4,1024,128]{2,1,0:T(8,128)} %rows.1) | copy-start | bytes 6291460

commit v4 on v3

--- a/solution.py
+++ b/solution.py
@@ -237,7 +237,11 @@
     )(rows, keys, w, b, same, level, clear_a, clear_b)[0]
 
 
-PARTS = ((0, 1, (2, 0, 1)), (0, 24, (0, 1, 2)), (24, 24, (1, 2, 0)), (48, 16, (2, 0, 1)))
+PARTS = (
+    (0, 1, (2, 0, 1)),
+    (0, 8, (0, 1, 2)), (8, 8, (1, 2, 0)), (16, 8, (2, 0, 1)),
+    (24, 16, (0, 1, 2)), (40, 16, (1, 2, 0)), (56, 8, (2, 0, 1)),
+)
 N = len(PARTS)
 
 

time: 47.9 us -> 46.6 us (0.973)
  Pallas kernels: 46 us -> 44.7 us
    pallas_call x1, Pallas kernels: 27.1 us -> 25.8 us  [reduce_to_owner(): pl.pallas_call(reduce_kernel, out_shape=(jax.ShapeDtypeStruct((64, D), f3...]
where the time goes in v4:
time: 46.6 us; the launch traced here: 46.5 us
  Pallas kernels  44.7 us (96%)
  local copies, waits for them, and re-layouts  1.13 us (2%)
  between operations  0.67 us (1%)
    pallas_call x1, Pallas kernels, reduce_to_owner(): pl.pallas_call(reduce_kernel, out_shape=(jax.ShapeDtypeStruct((64, D), f3...  25.8 us
    pallas_call x1, Pallas kernels, exchange(): pl.pallas_call(exchange_kernel, out_shape=(jax.ShapeDtypeStruct((4, D, D)...  10.7 us
    pallas_call x1, Pallas kernels, sections(): pl.pallas_call(sections_kernel, out_shape=(jax.ShapeDtypeStruct((KEYS, D)...  8.28 us

profile of v4, /device:TPU:0, one launch (start us, length us, event | category | flops | bytes accessed | tf_op | source)
XLA Modules:
  0.0 46.5 jit_solution(6389448078030700894)
XLA Ops:
  0.6 0.0 copy-start
  0.6 10.7 %shard_map.77 = (f32[4,128,128]{2,1,0:T(8,128)S(1)}, f32[4,1,128]{2,1,0:T(1,128)S(1)}, bf16[32,128,128]{2,1,0:T(8,128)(2,1)S(1)}, s32[32,128,128]{2,1,0:T(8,128)...) custom-call(f32[1,128,128]{2,1,0:T(8,128)} %w_in.1, ...), custom_call_target="tpu_custom_call" | custom-call | flops 40000000000 | bytes 1048576 | tf_op jit(solution)/shard_map/pallas_call | solution.py:143
  11.3 0.0 copy-done
  11.3 8.3 %shard_map.78 = (f32[8192,128]{1,0:T(8,128)S(1)}, f32[8192,128]{1,0:T(8,128)S(1)}) custom-call(f32[4,1024,128]{2,1,0:T(8,128)S(1)} %copy-done, s32[32,128]{1,0:T(8,128)S(1)} %get-tuple-element.13.keys_in, f32[4,128,128]{2,1,0:T(8,128)S(1)} %get-tuple-element.14.w, ...), custom_call_target="tpu_custom_call", output_to_operand_aliasing={{0}: (6, {}), {1}: (7, {})} | custom-call | tf_op jit(solution)/shard_map/pallas_call | solution.py:224
  19.6 25.8 %shard_map.79 = (f32[64,128]{1,0:T(8,128)S(1)}, f32[8,128]{1,0:T(8,128)S(1)}) custom-call(f32[4,4,4,2,64,128]{5,4,3,2,1,0:T(8,128)S(1)} %bitcast.7, f32[4,4,4,1,128]{4,3,2,1,0:T(1,128)S(1)} %bitcast.8), custom_call_target="tpu_custom_call" | custom-call | tf_op jit(solution)/shard_map/pallas_call | solution.py:360
  45.4 0.5 %slice_bitcast_fusion = f32[64]{0:T(128)} fusion(f32[8,128]{1,0:T(8,128)S(1)} %get-tuple-element.23), kind=kLoop, calls=%fused_computation | loop fusion | bytes 512 | tf_op jit(solution)/shard_map/squeeze | solution.py:381
  45.9 0.6 %copy.13 = f32[64,128]{1,0:T(8,128)} copy(f32[64,128]{1,0:T(8,128)S(1)} %get-tuple-element.26) | data formatting | bytes 65536
Async XLA Ops:
  0.6 10.7 %copy-start = (f32[4,1024,128]{2,1,0:T(8,128)S(1)}, f32[4,1024,128]{2,1,0:T(8,128)}, u32[]{:S(2)}) copy-start(f32[4,1024,128]{2,1,0:T(8,128)} %rows.1) | copy-start | bytes 6291460

commit v5 on v4

--- a/solution.py
+++ b/solution.py
@@ -35,7 +35,7 @@
 
 def exchange_kernel(
     w_in, b_in, p_in, k_in, v_in,
-    w_all, b_all, same, level, counts, table_a, table_b, key_rows,
+    w_all, b_all, same, level, lives, table_a, table_b, key_rows,
     keys, valid, words_v, words, send, recv, local,
 ):
     me = lax.axis_index("section")
@@ -99,15 +99,11 @@
     to_scalar = pltpu.make_async_copy(words_v, words, local.at[5])
     to_scalar.start()
     to_scalar.wait()
-    counts[...] = jnp.zeros_like(counts)
-    lane = lax.broadcasted_iota(i32, (64, 128), 1)
-    sub64 = lax.broadcasted_iota(i32, (64, 128), 0)
-    sub128 = lax.broadcasted_iota(i32, (128, 128), 0)
+    lane = lax.broadcasted_iota(i32, (8, 128), 1)
 
     def tally(i, carry):
         m = i // 2
         nv = valid[0, m]
-        found = jnp.zeros((64, 128), f32)
         for u in range(4):
             j = (i % 2) * 4 + u
             total = jnp.zeros((8, 128), i32)
@@ -118,17 +114,12 @@
             for s in range(SECTIONS):
                 alive = [a & words[s, m, j * 4 + w] for w, a in enumerate(alive)]
                 v = jnp.where(
-                    lane[:8] < 64,
-                    jnp.where(lane[:8] < 32, alive[0], alive[1]),
-                    jnp.where(lane[:8] < 96, alive[2], alive[3]))
-                total = total + ((v >> (lane[:8] & 31)) & 1)
-            key_row = key_row_at(m, j)
-            lives = jnp.concatenate([total] * 8, axis=0).astype(f32)
-            high = jnp.where((key_row >> 7) == sub64, lives, 0.0).astype(bf16)
-            low = jnp.where((key_row & 127) == sub128, 1.0, 0.0).astype(bf16)
-            found = found + lax.dot_general(high, low, (((1,), (1,)), ((), ())), preferred_element_type=f32)
+                    lane < 64,
+                    jnp.where(lane < 32, alive[0], alive[1]),
+                    jnp.where(lane < 96, alive[2], alive[3]))
+                total = total + ((v >> (lane & 31)) & 1)
+            lives[pl.ds(i * 4 + u, 1), :] = total[:1]
             level[i * 4 + u] = jnp.transpose(jnp.concatenate([total] * 16, axis=0))
-        counts[...] += found
         return carry
 
     lax.fori_loop(0, 8, tally, 0)
@@ -147,7 +138,7 @@
             jax.ShapeDtypeStruct((4, 1, D), f32),
             jax.ShapeDtypeStruct((32, 128, 128), bf16),
             jax.ShapeDtypeStruct((32, 128, 128), i32),
-            jax.ShapeDtypeStruct((64, 128), f32),
+            jax.ShapeDtypeStruct((32, 128), i32),
             jax.ShapeDtypeStruct((KEYS, D), f32),
             jax.ShapeDtypeStruct((KEYS, D), f32),
             jax.ShapeDtypeStruct((32, 128), i32),
@@ -212,13 +203,6 @@
 
     lax.fori_loop(0, ROWS // CHUNK, scatter, 0)
 
-    def join(i, carry):
-        at = pl.ds(pl.multiple_of(i * 512, 512), 512)
-        table_a[at, :] += table_b[at, :]
-        return carry
-
-    lax.fori_loop(0, KEYS // 512, join, 0)
-
 
 def sections(rows, keys, w, b, same, level, clear_a, clear_b):
     return pl.pallas_call(
@@ -234,18 +218,25 @@
         ],
         input_output_aliases={6: 0, 7: 1},
         compiler_params=pltpu.CompilerParams(vmem_limit_bytes=12 << 20),
-    )(rows, keys, w, b, same, level, clear_a, clear_b)[0]
+    )(rows, keys, w, b, same, level, clear_a, clear_b)
 
 
 PARTS = (
     (0, 1, (2, 0, 1)),
     (0, 8, (0, 1, 2)), (8, 8, (1, 2, 0)), (16, 8, (2, 0, 1)),
-    (24, 16, (0, 1, 2)), (40, 16, (1, 2, 0)), (56, 8, (2, 0, 1)),
+    (24, 8, (0, 1, 2)), (32, 8, (1, 2, 0)), (40, 8, (2, 0, 1)),
+    (48, 8, (0, 1, 2)), (56, 8, (1, 2, 0)),
+)
+TURNS = (
+    (0, 0), (0, 1), (0, 2), (0, 3), (0, 4), (0, 5), (0, 6), (0, 7), (0, 8), (1, 0), (1, 1), (1, 2),
+    (1, 3), (1, 4), (1, 5), (1, 6), (1, 7), (1, 8), (2, 0), (2, 1), (2, 2), (2, 3), (2, 4), (2, 5),
+    (2, 6), (2, 7), (2, 8), (3, 0), (3, 1), (3, 2), (3, 3), (3, 4), (3, 5), (3, 6), (3, 7), (3, 8),
+    (4, 0), (4, 1), (4, 2), (4, 3), (4, 4), (4, 5), (4, 6), (4, 7), (4, 8),
 )
 N = len(PARTS)
 
 
-def reduce_kernel(table, counts, means, count_out, *scratch):
+def reduce_kernel(table_a, table_b, keys, lives, means, count_out, table, counts, *scratch):
     held, near, middle, second, last, third = (scratch[i * N : (i + 1) * N] for i in range(6))
     core_sems, near_send, near_recv, send, recv = scratch[6 * N :]
     z = lax.axis_index("section")
@@ -262,12 +253,33 @@
         return (at[0], at[1] * 8 + at[2] * 2 + c)
 
     other = (z, y * 8 + x * 2 + (1 - c))
+    peers = [device(axis, k) for axis in range(3) for k in (1, 3)] + [other]
     barrier = pltpu.get_barrier_semaphore()
-    pl.semaphore_signal(barrier, inc=1, device_id=other, device_id_type=MESH)
-    for axis in range(3):
-        for k in range(1, 4):
-            pl.semaphore_signal(barrier, inc=1, device_id=device(axis, k), device_id_type=MESH)
-    pl.semaphore_wait(barrier, 10)
+    for peer in peers:
+        pl.semaphore_signal(barrier, inc=1, device_id=peer, device_id_type=MESH)
+
+    def join(i, carry):
+        at = (i // 16, (i // 4) % 4, i % 4)
+        table[at] = table_a[at] + table_b[at]
+        return carry
+
+    lax.fori_loop(0, 64, join, 0)
+    sub64 = lax.broadcasted_iota(i32, (64, 128), 0)
+    sub128 = lax.broadcasted_iota(i32, (128, 128), 0)
+
+    def tally(i, found):
+        for u in range(4):
+            key_row = keys[pl.ds(i * 4 + u, 1), :]
+            alive = lives[pl.ds(i * 4 + u, 1), :].astype(f32)
+            high = jnp.where((key_row >> 7) == sub64, alive, 0.0).astype(bf16)
+            low = jnp.where((key_row & 127) == sub128, 1.0, 0.0).astype(bf16)
+            found = found + lax.dot_general(high, low, (((1,), (1,)), ((), ())), preferred_element_type=f32)
+        return found
+
+    found = lax.fori_loop(0, 8, tally, jnp.zeros((64, 128), f32))
+    for i in range(64):
+        counts[i // 16, (i // 4) % 4, i % 4] = found[i : i + 1]
+    pl.semaphore_wait(barrier, len(peers))
 
     def remote(src, dst, send_sem, recv_sem, to):
         copy = pltpu.make_async_remote_copy(
@@ -281,39 +293,6 @@
         if half is not None:
             where[1 if axes[0] == axis else 0] = pl.ds(2 * half, 2)
         return ref.at[tuple(where)]
-
-    every = [0, 1, 2]
-    core = []
-    for n, (start, size, order) in enumerate(PARTS):
-        src = counts if n == 0 else table.at[:, :, :, 1 - c, pl.ds(start, size), :]
-        core.append(remote(src, held[n], core_sems.at[0, n], core_sems.at[1, n], other))
-
-    sent = [[] for _ in PARTS]
-    relay = [None] * N
-    for n, (start, size, order) in enumerate(PARTS):
-        core[n].wait()
-        if n == 0:
-            held[n][...] += counts[...]
-        else:
-            for a in range(4):
-                held[n][a] += table[a, :, :, c, start : start + size, :]
-        axis = order[0]
-
-        def hop(slot, index, half, k):
-            return remote(
-                piece(held[n], every, axis, index, half), near[n].at[slot],
-                near_send.at[n, slot], near_recv.at[n, slot], device(axis, k))
-
-        relay[n] = [hop(0, position(axis, 2), 0, 1), hop(1, position(axis, 2), 1, 3)]
-        sent[n] = [hop(2, position(axis, 1), 1, 1), hop(3, position(axis, 3), 0, 3)]
-    for n, (start, size, order) in enumerate(PARTS):
-        axis = order[0]
-        for half, k in ((0, 1), (1, 3)):
-            relay[n][half].wait()
-            block = piece(held[n], every, axis, position(axis, k), half)
-            block[...] += near[n][half]
-            sent[n].append(remote(
-                block, near[n].at[4 + half], near_send.at[n, 4 + half], near_recv.at[n, 4 + half], device(axis, k)))
 
     def spread(n, stage, source, axes, target):
         axis = PARTS[n][2][stage]
@@ -328,39 +307,67 @@
         axis = PARTS[n][2][stage]
         return (piece(source, axes, axis, place[axis])[...] + target[0]) + (target[1] + target[2])
 
+    every = [0, 1, 2]
+    core = []
     for n, (start, size, order) in enumerate(PARTS):
-        for copy in sent[n]:
-            copy.wait()
+        src = counts if n == 0 else table.at[:, :, :, 1 - c, pl.ds(start, size), :]
+        core.append(remote(src, held[n], core_sems.at[0, n], core_sems.at[1, n], other))
+    sent = [[] for _ in PARTS]
+    relay = [None] * N
+    total = None
+    for turn, n in TURNS:
+        start, size, order = PARTS[n]
         axis = order[0]
-        middle[n][0:2] = (piece(held[n], every, axis, place[axis], 0)[...] + near[n][3]) + near[n][4]
-        middle[n][2:4] = (piece(held[n], every, axis, place[axis], 1)[...] + near[n][2]) + near[n][5]
-        sent[n] = spread(n, 1, middle[n], [a for a in every if a != axis], second[n])
-    for n, (start, size, order) in enumerate(PARTS):
-        for copy in sent[n]:
-            copy.wait()
-        axes = [a for a in every if a != order[0]]
-        last[n][...] = summed(n, 1, middle[n], axes, second[n])
-        sent[n] = spread(n, 2, last[n], [order[2]], third[n])
-    for n, (start, size, order) in enumerate(PARTS):
-        for copy in sent[n]:
-            copy.wait()
-        value = summed(n, 2, last[n], [order[2]], third[n])
-        if n == 0:
-            wide = jnp.transpose(jnp.broadcast_to(value, (128, 128)))
-            total = jnp.maximum(jnp.where(c == 0, wide[:64], wide[64:]), 1.0)
-            count_out[...] = jnp.broadcast_to(jnp.where(c == 0, value, pltpu.roll(value, 64, 1)), (8, 128))
+
+        def hop(slot, index, half, k):
+            return remote(
+                piece(held[n], every, axis, index, half), near[n].at[slot],
+                near_send.at[n, slot], near_recv.at[n, slot], device(axis, k))
+
+        if turn == 0:
+            core[n].wait()
+            if n == 0:
+                held[n][...] += counts[...]
+            else:
+                for i in range(4):
+                    held[n][i] += table[i, :, :, c, start : start + size, :]
+            relay[n] = [hop(0, position(axis, 2), 0, 1), hop(1, position(axis, 2), 1, 3)]
+            sent[n] = [hop(2, position(axis, 1), 1, 1), hop(3, position(axis, 3), 0, 3)]
+        elif turn == 1:
+            for half, k in ((0, 1), (1, 3)):
+                relay[n][half].wait()
+                block = piece(held[n], every, axis, position(axis, k), half)
+                block[...] += near[n][half]
+                sent[n].append(hop(4 + half, position(axis, k), half, k))
         else:
-            means[start : start + size, :] = value / total[start : start + size]
-
-
-def reduce_to_owner(table, counts):
-    buffers = []
+            for copy in sent[n]:
+                copy.wait()
+            axes = [i for i in every if i != axis]
+            if turn == 2:
+                middle[n][0:2] = (piece(held[n], every, axis, place[axis], 0)[...] + near[n][3]) + near[n][4]
+                middle[n][2:4] = (piece(held[n], every, axis, place[axis], 1)[...] + near[n][2]) + near[n][5]
+                sent[n] = spread(n, 1, middle[n], axes, second[n])
+            elif turn == 3:
+                last[n][...] = summed(n, 1, middle[n], axes, second[n])
+                sent[n] = spread(n, 2, last[n], [order[2]], third[n])
+            else:
+                value = summed(n, 2, last[n], [order[2]], third[n])
+                if n == 0:
+                    wide = jnp.transpose(jnp.broadcast_to(value, (128, 128)))
+                    total = jnp.maximum(jnp.where(c == 0, wide[:64], wide[64:]), 1.0)
+                    count_out[...] = jnp.broadcast_to(jnp.where(c == 0, value, pltpu.roll(value, 64, 1)), (8, 128))
+                else:
+                    means[start : start + size, :] = value / total[start : start + size]
+
+
+def reduce_to_owner(table_a, table_b, keys, lives):
+    buffers = [pltpu.VMEM((4, 4, 4, 2, 64, D), f32), pltpu.VMEM((4, 4, 4, 1, D), f32)]
     for lead in ((4, 4, 4), (6, 2, 4), (4, 4), (3, 4), (4,), (3,)):
         buffers += [pltpu.VMEM((*lead, size, D), f32) for _, size, _ in PARTS]
     return pl.pallas_call(
         reduce_kernel,
         out_shape=(jax.ShapeDtypeStruct((64, D), f32), jax.ShapeDtypeStruct((8, D), f32)),
-        in_specs=[spec(VM), spec(VM)],
+        in_specs=[spec(VM)] * 4,
         out_specs=(spec(VM), spec(VM)),
         scratch_shapes=buffers + [
             pltpu.SemaphoreType.DMA((2, N)),
@@ -369,15 +376,15 @@
             pltpu.SemaphoreType.DMA((N, 2, 3)),
             pltpu.SemaphoreType.DMA((N, 2, 3)),
         ],
-        compiler_params=pltpu.CompilerParams(collective_id=1, has_side_effects=True, vmem_limit_bytes=16 << 20),
-    )(table.reshape(4, 4, 4, 2, 64, D), counts.reshape(4, 4, 4, 1, D))
+        compiler_params=pltpu.CompilerParams(collective_id=1, has_side_effects=True, vmem_limit_bytes=20 << 20),
+    )(table_a.reshape(4, 4, 4, 2, 64, D), table_b.reshape(4, 4, 4, 2, 64, D), keys, lives)
 
 
 def shards(rows_data, row_keys, valid_counts, predicates, section_weight, section_bias):
-    w, b, same, level, counts, clear_a, clear_b, key_rows = exchange(
+    w, b, same, level, lives, clear_a, clear_b, key_rows = exchange(
         section_weight, section_bias.reshape(1, 1, D), predicates.reshape(4, MICRO, 32), row_keys, valid_counts.T)
-    table = sections(rows_data, key_rows, w, b, same, level, clear_a, clear_b)
-    means, total = reduce_to_owner(table, counts)
+    tables = sections(rows_data, key_rows, w, b, same, level, clear_a, clear_b)
+    means, total = reduce_to_owner(*tables, key_rows, lives)
     return means, total[0, :64]
 
 

time: 46.6 us -> 46.4 us (level)
    pallas_call x1, Pallas kernels: 25.8 us -> 26.5 us  [reduce_to_owner(): pl.pallas_call(reduce_kernel, out_shape=(jax.ShapeDtypeStruct((64, D), f3...]
    pallas_call x1, Pallas kernels: 8.28 us -> 7.8 us  [sections(): pl.pallas_call(sections_kernel, out_shape=(jax.ShapeDtypeStruct((KEYS, D)...]
where the time goes in v5:
time: 46.4 us; the launch traced here: 46.3 us
  Pallas kernels  44.5 us (96%)
  local copies, waits for them, and re-layouts  1.13 us (2%)
  between operations  0.67 us (1%)
    pallas_call x1, Pallas kernels, reduce_to_owner(): pl.pallas_call(reduce_kernel, out_shape=(jax.ShapeDtypeStruct((64, D), f3...  26.5 us
    pallas_call x1, Pallas kernels, exchange(): pl.pallas_call(exchange_kernel, out_shape=(jax.ShapeDtypeStruct((4, D, D)...  10.2 us
    pallas_call x1, Pallas kernels, sections(): pl.pallas_call(sections_kernel, out_shape=(jax.ShapeDtypeStruct((KEYS, D)...  7.8 us

profile of v5, /device:TPU:0, one launch (start us, length us, event | category | flops | bytes accessed | tf_op | source)
XLA Modules:
  0.0 46.3 jit_solution(4132873942769065563)
XLA Ops:
  0.6 0.0 copy-start
  0.6 10.2 %shard_map.77 = (f32[4,128,128]{2,1,0:T(8,128)S(1)}, f32[4,1,128]{2,1,0:T(1,128)S(1)}, bf16[32,128,128]{2,1,0:T(8,128)(2,1)S(1)}, s32[32,128,128]{2,1,0:T(8,128)...) custom-call(f32[1,128,128]{2,1,0:T(8,128)} %w_in.1, ...), custom_call_target="tpu_custom_call" | custom-call | flops 40000000000 | bytes 1048576 | tf_op jit(solution)/shard_map/pallas_call | solution.py:134
  10.9 0.0 copy-done
  10.9 7.8 %shard_map.78 = (f32[8192,128]{1,0:T(8,128)S(1)}, f32[8192,128]{1,0:T(8,128)S(1)}) custom-call(f32[4,1024,128]{2,1,0:T(8,128)S(1)} %copy-done, s32[32,128]{1,0:T(8,128)S(1)} %get-tuple-element.14.keys_in.keys, f32[4,128,128]{2,1,0:T(8,128)S(1)} %get-tuple-element.15.w, ...), custom_call_target="tpu_custom_call", output_to_operand_aliasing={{0}: (6, {}), {1}: (7, {})} | custom-call | tf_op jit(solution)/shard_map/pallas_call | solution.py:208
  18.7 26.5 %shard_map.79 = (f32[64,128]{1,0:T(8,128)S(1)}, f32[8,128]{1,0:T(8,128)S(1)}) custom-call(f32[4,4,4,2,64,128]{5,4,3,2,1,0:T(8,128)S(1)} %bitcast.7, f32[4,4,4,2,64,128]{5,4,3,2,1,0:T(8,128)S(1)} %bitcast.8, s32[32,128]{1,0:T(8,128)S(1)} %get-tuple-element.14.keys_in.keys, s32[32,128]{1,0:T(8,128)S(1)} %get-tuple-element.23.lives), custom_call_target="tpu_custom_call" | custom-call | tf_op jit(solution)/shard_map/pallas_call | solution.py:367
  45.2 0.5 %slice_bitcast_fusion = f32[64]{0:T(128)} fusion(f32[8,128]{1,0:T(8,128)S(1)} %get-tuple-element.25), kind=kLoop, calls=%fused_computation | loop fusion | bytes 512 | tf_op jit(solution)/shard_map/squeeze | solution.py:388
  45.7 0.6 %copy.13 = f32[64,128]{1,0:T(8,128)} copy(f32[64,128]{1,0:T(8,128)S(1)} %get-tuple-element.28) | data formatting | bytes 65536
Async XLA Ops:
  0.6 10.3 %copy-start = (f32[4,1024,128]{2,1,0:T(8,128)S(1)}, f32[4,1024,128]{2,1,0:T(8,128)}, u32[]{:S(2)}) copy-start(f32[4,1024,128]{2,1,0:T(8,128)} %rows.1) | copy-start | bytes 6291460

commit v6 on v5

--- a/solution.py
+++ b/solution.py
@@ -36,21 +36,24 @@
 def exchange_kernel(
     w_in, b_in, p_in, k_in, v_in,
     w_all, b_all, same, level, lives, table_a, table_b, key_rows,
-    keys, valid, words_v, words, send, recv, local,
+    keys, valid, flags, words_v, words, send, recv, pair_send, pair_recv, local,
 ):
     me = lax.axis_index("section")
     row = lax.axis_index("rows")
+    c = row % 2
+    other = (me, row + 1 - 2 * c)
     own = [
         pltpu.make_async_copy(src, dst, local.at[n])
         for n, (src, dst) in enumerate((
-            (k_in, keys), (v_in, valid), (p_in.at[me], words_v.at[me]),
-            (b_in.at[0], b_all.at[me]), (w_in.at[0], w_all.at[me])))
+            (p_in, flags), (p_in.at[me], words_v.at[me]), (b_in.at[0], b_all.at[me]), (w_in.at[0], w_all.at[me]),
+            (k_in, keys), (v_in, valid)))
     ]
     for copy in own:
         copy.start()
     barrier = pltpu.get_barrier_semaphore()
     for k in range(1, 4):
         pl.semaphore_signal(barrier, inc=1, device_id=(lax.rem(me + k, 4), row), device_id_type=MESH)
+    pl.semaphore_signal(barrier, inc=1, device_id=other, device_id_type=MESH)
 
     def clear(i, carry):
         at = pl.ds(pl.multiple_of(i * 512, 512), 512)
@@ -59,13 +62,16 @@
         return carry
 
     lax.fori_loop(0, KEYS // 512, clear, 0)
-    pl.semaphore_wait(barrier, 3)
+    for copy in own[:4]:
+        copy.wait()
+    pl.semaphore_wait(barrier, 4)
+    half = pl.ds(pl.multiple_of(c * 64, 64), 64)
     copies = []
     for n, k in enumerate((2, 1, 3)):
         to = lax.rem(me + k, 4)
-        for a, (src, dst) in enumerate(
-            ((p_in.at[to], words_v.at[me]), (b_in.at[0], b_all.at[me]), (w_in.at[0], w_all.at[me]))
-        ):
+        for a, (src, dst) in enumerate((
+            (flags.at[to], words_v.at[me]), (w_all.at[me, half], w_all.at[me, half]), (b_all.at[me], b_all.at[me]),
+        )):
             copies.append((a, pltpu.make_async_remote_copy(
                 src_ref=src, dst_ref=dst, send_sem=send.at[n, a], recv_sem=recv.at[n, a],
                 device_id=(to, row), device_id_type=MESH)))
@@ -73,8 +79,8 @@
         for which, copy in copies:
             if which == a:
                 copy.start()
-    own[0].wait()
-    own[1].wait()
+    own[4].wait()
+    own[5].wait()
     group_i = (lax.broadcasted_iota(i32, (1, 128), 1) // GROUP) * KEYS
 
     for m in range(MICRO):
@@ -92,12 +98,21 @@
         return carry
 
     lax.fori_loop(0, 8, sameness, 0)
-    own[2].wait()
     for which, copy in copies:
         if which == 0:
             copy.wait()
-    to_scalar = pltpu.make_async_copy(words_v, words, local.at[5])
+    to_scalar = pltpu.make_async_copy(words_v, words, local.at[6])
     to_scalar.start()
+    passed = []
+    for n, k in enumerate((2, 1, 3)):
+        origin = lax.rem(me + 4 - k, 4)
+        copies[3 * n + 1][1].wait()
+        block = w_all.at[origin, half]
+        copy = pltpu.make_async_remote_copy(
+            src_ref=block, dst_ref=block, send_sem=pair_send.at[n], recv_sem=pair_recv.at[n],
+            device_id=other, device_id_type=MESH)
+        copy.start()
+        passed.append(copy)
     to_scalar.wait()
     lane = lax.broadcasted_iota(i32, (8, 128), 1)
 
@@ -123,11 +138,11 @@
         return carry
 
     lax.fori_loop(0, 8, tally, 0)
-    own[3].wait()
-    own[4].wait()
     for which, copy in copies:
-        if which != 0:
+        if which == 2:
             copy.wait()
+    for copy in passed:
+        copy.wait()
 
 
 def exchange(weight, bias, predicates, keys, valid):
@@ -149,19 +164,25 @@
             pltpu.VMEM((MICRO, BLOCK), i32),
             pltpu.SMEM((1, MICRO), i32),
             pltpu.VMEM((4, 4, 32), i32),
+            pltpu.VMEM((4, 4, 32), i32),
             pltpu.SMEM((4, 4, 32), i32),
             pltpu.SemaphoreType.DMA((3, 3)),
             pltpu.SemaphoreType.DMA((3, 3)),
-            pltpu.SemaphoreType.DMA((6,)),
+            pltpu.SemaphoreType.DMA((3,)),
+            pltpu.SemaphoreType.DMA((3,)),
+            pltpu.SemaphoreType.DMA((7,)),
         ],
         compiler_params=pltpu.CompilerParams(collective_id=0, has_side_effects=True, vmem_limit_bytes=8 << 20),
         cost_estimate=pl.CostEstimate(flops=40_000_000_000, bytes_accessed=1 << 20, transcendentals=0),
     )(pinned(weight), pinned(bias), pinned(predicates), pinned(keys), pinned(valid))
 
 
-def sections_kernel(rows, keys_in, w, b, same, level, clear_a, clear_b, table_a, table_b, w2, ready, keys, sem):
-    fetch = pltpu.make_async_copy(keys_in, keys, sem)
-    fetch.start()
+def sections_kernel(
+    rows, keys_in, w, b, same, level, clear_a, clear_b, v_in, table_a, table_b, w2, ready, keys, valid, sems
+):
+    fetch = [pltpu.make_async_copy(keys_in, keys, sems.at[0]), pltpu.make_async_copy(v_in, valid, sems.at[1])]
+    for copy in fetch:
+        copy.start()
     for s in range(SECTIONS):
         top = jnp.concatenate(high_low(w[s]), axis=1)
         w2[s] = jnp.concatenate([top, top], axis=0)
@@ -181,11 +202,13 @@
         return carry
 
     lax.fori_loop(0, MICRO, batch, 0)
-    fetch.wait()
+    for copy in fetch:
+        copy.wait()
     tables = (table_a, table_b)
     groups = CHUNK // GROUP
 
-    def scatter(u, carry):
+    def scatter(first, i, carry):
+        u = first + i
         def load(g):
             at = [keys[u * (CHUNK // 128) + (g * GROUP + i) // 128, (g * GROUP + i) % 128] for i in range(GROUP)]
             return at, [tables[g % 2][pl.ds(k, 1), :] for k in at]
@@ -201,24 +224,27 @@
                 flying[g + 2] = load(g + 2)
         return carry
 
-    lax.fori_loop(0, ROWS // CHUNK, scatter, 0)
-
-
-def sections(rows, keys, w, b, same, level, clear_a, clear_b):
+    for m in range(MICRO):
+        chunks = (valid[0, m] + CHUNK - 1) // CHUNK
+        lax.fori_loop(0, chunks, functools.partial(scatter, m * (BLOCK // CHUNK)), 0)
+
+
+def sections(rows, keys, w, b, same, level, clear_a, clear_b, valid):
     return pl.pallas_call(
         sections_kernel,
         out_shape=(jax.ShapeDtypeStruct((KEYS, D), f32),) * 2,
-        in_specs=[spec(VM)] * 8,
+        in_specs=[spec(VM)] * 8 + [spec(HB)],
         out_specs=(spec(VM),) * 2,
         scratch_shapes=[
             pltpu.VMEM((SECTIONS, 256, 256), bf16),
             pltpu.VMEM((ROWS, D), f32),
             pltpu.SMEM((32, 128), i32),
-            pltpu.SemaphoreType.DMA,
+            pltpu.SMEM((1, MICRO), i32),
+            pltpu.SemaphoreType.DMA((2,)),
         ],
         input_output_aliases={6: 0, 7: 1},
         compiler_params=pltpu.CompilerParams(vmem_limit_bytes=12 << 20),
-    )(rows, keys, w, b, same, level, clear_a, clear_b)
+    )(rows, keys, w, b, same, level, clear_a, clear_b, pinned(valid))
 
 
 PARTS = (
@@ -383,7 +409,7 @@
 def shards(rows_data, row_keys, valid_counts, predicates, section_weight, section_bias):
     w, b, same, level, lives, clear_a, clear_b, key_rows = exchange(
         section_weight, section_bias.reshape(1, 1, D), predicates.reshape(4, MICRO, 32), row_keys, valid_counts.T)
-    tables = sections(rows_data, key_rows, w, b, same, level, clear_a, clear_b)
+    tables = sections(rows_data, key_rows, w, b, same, level, clear_a, clear_b, valid_counts.T)
     means, total = reduce_to_owner(*tables, key_rows, lives)
     return means, total[0, :64]
 

time: 46.4 us -> 45.7 us (0.985)
  Pallas kernels: 44.5 us -> 44 us
    pallas_call x1, Pallas kernels: 7.8 us -> 6.81 us  [sections(): pl.pallas_call(sections_kernel, out_shape=(jax.ShapeDtypeStruct((KEYS, D)...]
    pallas_call x1, Pallas kernels: 26.5 us -> 27.1 us  [reduce_to_owner(): pl.pallas_call(reduce_kernel, out_shape=(jax.ShapeDtypeStruct((64, D), f3...]
where the time goes in v6:
time: 45.7 us; the launch traced here: 45.8 us
  Pallas kernels  44 us (96%)
  local copies, waits for them, and re-layouts  1.13 us (2%)
  between operations  0.67 us (1%)
    pallas_call x1, Pallas kernels, reduce_to_owner(): pl.pallas_call(reduce_kernel, out_shape=(jax.ShapeDtypeStruct((64, D), f3...  27.1 us
    pallas_call x1, Pallas kernels, exchange(): pl.pallas_call(exchange_kernel, out_shape=(jax.ShapeDtypeStruct((4, D, D)...  10.1 us
    pallas_call x1, Pallas kernels, sections(): pl.pallas_call(sections_kernel, out_shape=(jax.ShapeDtypeStruct((KEYS, D)...  6.81 us

profile of v6, /device:TPU:0, one launch (start us, length us, event | category | flops | bytes accessed | tf_op | source)
XLA Modules:
  0.0 45.8 jit_solution(5542220552447026642)
XLA Ops:
  0.6 0.0 copy-start
  0.6 10.1 %shard_map.77 = (f32[4,128,128]{2,1,0:T(8,128)S(1)}, f32[4,1,128]{2,1,0:T(1,128)S(1)}, bf16[32,128,128]{2,1,0:T(8,128)(2,1)S(1)}, s32[32,128,128]{2,1,0:T(8,128)...) custom-call(f32[1,128,128]{2,1,0:T(8,128)} %w_in.1, ...), custom_call_target="tpu_custom_call" | custom-call | flops 40000000000 | bytes 1048576 | tf_op jit(solution)/shard_map/pallas_call | solution.py:149
  10.7 0.0 copy-done
  10.7 6.8 %shard_map.78 = (f32[8192,128]{1,0:T(8,128)S(1)}, f32[8192,128]{1,0:T(8,128)S(1)}) custom-call(f32[4,1024,128]{2,1,0:T(8,128)S(1)} %copy-done, s32[32,128]{1,0:T(8,128)S(1)} %get-tuple-element.14.keys_in.keys, f32[4,128,128]{2,1,0:T(8,128)S(1)} %get-tuple-element.15.w, ...), custom_call_target="tpu_custom_call", output_to_operand_aliasing={{0}: (6, {}), {1}: (7, {})} | custom-call | tf_op jit(solution)/shard_map/pallas_call | solution.py:233
  17.5 27.1 %shard_map.79 = (f32[64,128]{1,0:T(8,128)S(1)}, f32[8,128]{1,0:T(8,128)S(1)}) custom-call(f32[4,4,4,2,64,128]{5,4,3,2,1,0:T(8,128)S(1)} %bitcast.7, f32[4,4,4,2,64,128]{5,4,3,2,1,0:T(8,128)S(1)} %bitcast.8, s32[32,128]{1,0:T(8,128)S(1)} %get-tuple-element.14.keys_in.keys, s32[32,128]{1,0:T(8,128)S(1)} %get-tuple-element.23.lives), custom_call_target="tpu_custom_call" | custom-call | tf_op jit(solution)/shard_map/pallas_call | solution.py:393
  44.7 0.5 %slice_bitcast_fusion = f32[64]{0:T(128)} fusion(f32[8,128]{1,0:T(8,128)S(1)} %get-tuple-element.25), kind=kLoop, calls=%fused_computation | loop fusion | bytes 512 | tf_op jit(solution)/shard_map/squeeze | solution.py:414
  45.2 0.6 %copy.13 = f32[64,128]{1,0:T(8,128)} copy(f32[64,128]{1,0:T(8,128)S(1)} %get-tuple-element.28) | data formatting | bytes 65536
Async XLA Ops:
  0.6 10.1 %copy-start = (f32[4,1024,128]{2,1,0:T(8,128)S(1)}, f32[4,1024,128]{2,1,0:T(8,128)}, u32[]{:S(2)}) copy-start(f32[4,1024,128]{2,1,0:T(8,128)} %rows.1) | copy-start | bytes 6291460

commit v7 on v6

--- a/solution.py
+++ b/solution.py
@@ -248,23 +248,30 @@
 
 
 PARTS = (
-    (0, 1, (2, 0, 1)),
-    (0, 8, (0, 1, 2)), (8, 8, (1, 2, 0)), (16, 8, (2, 0, 1)),
-    (24, 8, (0, 1, 2)), (32, 8, (1, 2, 0)), (40, 8, (2, 0, 1)),
-    (48, 8, (0, 1, 2)), (56, 8, (1, 2, 0)),
+    (0, 8, (0, 1, 2)),
+    (24, 8, (1, 2, 0)),
+    (64, 8, (2, 0, 1)),
+    (8, 8, (0, 1, 2)),
+    (32, 8, (1, 2, 0)),
+    (48, 8, (2, 0, 1)),
+    (16, 8, (0, 1, 2)),
+    (40, 8, (1, 2, 0)),
+    (56, 8, (2, 0, 1)),
 )
 TURNS = (
-    (0, 0), (0, 1), (0, 2), (0, 3), (0, 4), (0, 5), (0, 6), (0, 7), (0, 8), (1, 0), (1, 1), (1, 2),
-    (1, 3), (1, 4), (1, 5), (1, 6), (1, 7), (1, 8), (2, 0), (2, 1), (2, 2), (2, 3), (2, 4), (2, 5),
-    (2, 6), (2, 7), (2, 8), (3, 0), (3, 1), (3, 2), (3, 3), (3, 4), (3, 5), (3, 6), (3, 7), (3, 8),
-    (4, 0), (4, 1), (4, 2), (4, 3), (4, 4), (4, 5), (4, 6), (4, 7), (4, 8),
+    (0, 0), (5, 0), (0, 1), (5, 1), (0, 2), (5, 2), (0, 3), (5, 3), (0, 4), (5, 4), (0, 5), (5, 5),
+    (0, 6), (5, 6), (0, 7), (5, 7), (0, 8), (5, 8), (1, 0), (1, 1), (1, 2), (1, 3), (1, 4), (1, 5),
+    (1, 6), (1, 7), (1, 8), (2, 0), (2, 1), (2, 2), (2, 3), (2, 4), (2, 5), (2, 6), (2, 7), (2, 8),
+    (3, 0), (3, 1), (3, 2), (3, 3), (3, 4), (3, 5), (3, 6), (3, 7), (3, 8), (4, 0), (4, 1), (4, 2),
+    (4, 3), (4, 4), (4, 5), (4, 6), (4, 7), (4, 8),
 )
 N = len(PARTS)
-
-
-def reduce_kernel(table_a, table_b, keys, lives, means, count_out, table, counts, *scratch):
+HEIGHT = 72
+
+
+def reduce_kernel(table_a, table_b, keys, lives, means, count_out, table, *scratch):
     held, near, middle, second, last, third = (scratch[i * N : (i + 1) * N] for i in range(6))
-    core_sems, near_send, near_recv, send, recv = scratch[6 * N :]
+    core_sems, near_sems, far_sems = scratch[6 * N :]
     z = lax.axis_index("section")
     row = lax.axis_index("rows")
     y, x, c = row // 8, (row // 2) % 4, row % 2
@@ -286,7 +293,7 @@
 
     def join(i, carry):
         at = (i // 16, (i // 4) % 4, i % 4)
-        table[at] = table_a[at] + table_b[at]
+        table[(*at, slice(None), slice(0, 64))] = table_a[at] + table_b[at]
         return carry
 
     lax.fori_loop(0, 64, join, 0)
@@ -304,14 +311,18 @@
 
     found = lax.fori_loop(0, 8, tally, jnp.zeros((64, 128), f32))
     for i in range(64):
-        counts[i // 16, (i // 4) % 4, i % 4] = found[i : i + 1]
+        line = jnp.broadcast_to(found[i : i + 1], (8, 128))
+        for core in range(2):
+            table[i // 16, (i // 4) % 4, i % 4, core, 64:72, :] = line
     pl.semaphore_wait(barrier, len(peers))
 
-    def remote(src, dst, send_sem, recv_sem, to):
-        copy = pltpu.make_async_remote_copy(
-            src_ref=src, dst_ref=dst, send_sem=send_sem, recv_sem=recv_sem, device_id=to, device_id_type=MESH)
-        copy.start()
-        return copy
+    def send(src, dst, send_sem, recv_sem, to):
+        pltpu.make_async_remote_copy(
+            src_ref=src, dst_ref=dst, send_sem=send_sem, recv_sem=recv_sem, device_id=to, device_id_type=MESH
+        ).start()
+
+    def wait(ref, sem):
+        pltpu.make_async_copy(ref, ref, sem).wait()
 
     def piece(ref, axes, axis, index, half=None):
         where = [slice(None)] * len(axes)
@@ -322,72 +333,74 @@
 
     def spread(n, stage, source, axes, target):
         axis = PARTS[n][2][stage]
-        return [
-            remote(
+        for k in (2, 1, 3):
+            send(
                 piece(source, axes, axis, position(axis, k)), target.at[k - 1],
-                send.at[n, stage - 1, k - 1], recv.at[n, stage - 1, k - 1], device(axis, k))
-            for k in (2, 1, 3)
-        ]
+                far_sems.at[n, stage - 1, 0], far_sems.at[n, stage - 1, 1], device(axis, k))
 
     def summed(n, stage, source, axes, target):
         axis = PARTS[n][2][stage]
+        wait(target, far_sems.at[n, stage - 1, 1])
         return (piece(source, axes, axis, place[axis])[...] + target[0]) + (target[1] + target[2])
 
     every = [0, 1, 2]
-    core = []
     for n, (start, size, order) in enumerate(PARTS):
-        src = counts if n == 0 else table.at[:, :, :, 1 - c, pl.ds(start, size), :]
-        core.append(remote(src, held[n], core_sems.at[0, n], core_sems.at[1, n], other))
-    sent = [[] for _ in PARTS]
-    relay = [None] * N
-    total = None
+        send(table.at[:, :, :, 1 - c, pl.ds(start, size), :], held[n], core_sems.at[0, n], core_sems.at[1, n], other)
+    values = []
     for turn, n in TURNS:
         start, size, order = PARTS[n]
         axis = order[0]
 
-        def hop(slot, index, half, k):
-            return remote(
+        def hop(slot, recv, index, half, k):
+            send(
                 piece(held[n], every, axis, index, half), near[n].at[slot],
-                near_send.at[n, slot], near_recv.at[n, slot], device(axis, k))
-
+                near_sems.at[n, 3], near_sems.at[n, recv], device(axis, k))
+
+        axes = [i for i in every if i != axis]
         if turn == 0:
-            core[n].wait()
-            if n == 0:
-                held[n][...] += counts[...]
-            else:
-                for i in range(4):
-                    held[n][i] += table[i, :, :, c, start : start + size, :]
-            relay[n] = [hop(0, position(axis, 2), 0, 1), hop(1, position(axis, 2), 1, 3)]
-            sent[n] = [hop(2, position(axis, 1), 1, 1), hop(3, position(axis, 3), 0, 3)]
+            wait(held[n], core_sems.at[1, n])
+            for i in range(4):
+                held[n][i] += table[i, :, :, c, start : start + size, :]
+            hop(0, 0, position(axis, 2), 0, 1)
+            hop(1, 1, position(axis, 2), 1, 3)
+        elif turn == 5:
+            hop(2, 2, position(axis, 1), 1, 1)
+            hop(3, 2, position(axis, 3), 0, 3)
         elif turn == 1:
             for half, k in ((0, 1), (1, 3)):
-                relay[n][half].wait()
+                wait(near[n].at[half], near_sems.at[n, half])
                 block = piece(held[n], every, axis, position(axis, k), half)
                 block[...] += near[n][half]
-                sent[n].append(hop(4 + half, position(axis, k), half, k))
+                hop(4 + half, 2, position(axis, k), half, k)
+        elif turn == 2:
+            wait(near[n].at[2:6], near_sems.at[n, 2])
+            middle[n][0:2] = (piece(held[n], every, axis, place[axis], 0)[...] + near[n][3]) + near[n][4]
+            middle[n][2:4] = (piece(held[n], every, axis, place[axis], 1)[...] + near[n][2]) + near[n][5]
+            spread(n, 1, middle[n], axes, second[n])
+        elif turn == 3:
+            last[n][...] = summed(n, 1, middle[n], axes, second[n])
+            spread(n, 2, last[n], [order[2]], third[n])
         else:
-            for copy in sent[n]:
-                copy.wait()
-            axes = [i for i in every if i != axis]
-            if turn == 2:
-                middle[n][0:2] = (piece(held[n], every, axis, place[axis], 0)[...] + near[n][3]) + near[n][4]
-                middle[n][2:4] = (piece(held[n], every, axis, place[axis], 1)[...] + near[n][2]) + near[n][5]
-                sent[n] = spread(n, 1, middle[n], axes, second[n])
-            elif turn == 3:
-                last[n][...] = summed(n, 1, middle[n], axes, second[n])
-                sent[n] = spread(n, 2, last[n], [order[2]], third[n])
-            else:
-                value = summed(n, 2, last[n], [order[2]], third[n])
-                if n == 0:
-                    wide = jnp.transpose(jnp.broadcast_to(value, (128, 128)))
-                    total = jnp.maximum(jnp.where(c == 0, wide[:64], wide[64:]), 1.0)
-                    count_out[...] = jnp.broadcast_to(jnp.where(c == 0, value, pltpu.roll(value, 64, 1)), (8, 128))
-                else:
-                    means[start : start + size, :] = value / total[start : start + size]
+            value = summed(n, 2, last[n], [order[2]], third[n])
+            if start + size == HEIGHT:
+                line = value[size - 8 : size - 7]
+                wide = jnp.transpose(jnp.broadcast_to(line, (128, 128)))
+                total = jnp.maximum(jnp.where(c == 0, wide[:64], wide[64:]), 1.0)
+                count_out[...] = jnp.broadcast_to(jnp.where(c == 0, line, pltpu.roll(line, 64, 1)), (8, 128))
+                size -= 8
+            values.append((start, size, value))
+    for start, size, value in values:
+        if size:
+            means[start : start + size, :] = value[:size] / total[start : start + size]
+    for n in range(N):
+        wait(held[n], core_sems.at[0, n])
+        wait(near[n], near_sems.at[n, 3])
+        wait(second[n], far_sems.at[n, 0, 0])
+        wait(third[n], far_sems.at[n, 1, 0])
 
 
 def reduce_to_owner(table_a, table_b, keys, lives):
-    buffers = [pltpu.VMEM((4, 4, 4, 2, 64, D), f32), pltpu.VMEM((4, 4, 4, 1, D), f32)]
+    buffers = [pltpu.VMEM((4, 4, 4, 2, HEIGHT, D), f32)]
     for lead in ((4, 4, 4), (6, 2, 4), (4, 4), (3, 4), (4,), (3,)):
         buffers += [pltpu.VMEM((*lead, size, D), f32) for _, size, _ in PARTS]
     return pl.pallas_call(
@@ -397,10 +410,8 @@
         out_specs=(spec(VM), spec(VM)),
         scratch_shapes=buffers + [
             pltpu.SemaphoreType.DMA((2, N)),
-            pltpu.SemaphoreType.DMA((N, 6)),
-            pltpu.SemaphoreType.DMA((N, 6)),
-            pltpu.SemaphoreType.DMA((N, 2, 3)),
-            pltpu.SemaphoreType.DMA((N, 2, 3)),
+            pltpu.SemaphoreType.DMA((N, 4)),
+            pltpu.SemaphoreType.DMA((N, 2, 2)),
         ],
         compiler_params=pltpu.CompilerParams(collective_id=1, has_side_effects=True, vmem_limit_bytes=20 << 20),
     )(table_a.reshape(4, 4, 4, 2, 64, D), table_b.reshape(4, 4, 4, 2, 64, D), keys, lives)

time: 45.7 us -> 43.6 us (0.954); the launches traced: 45.8 us -> 43.2 us
  Pallas kernels: 44 us -> 41.4 us
    pallas_call x1, Pallas kernels: 27.1 us -> 23.9 us  [reduce_to_owner(): pl.pallas_call(reduce_kernel, out_shape=(jax.ShapeDtypeStruct((64, D), f3...]
    pallas_call x1, Pallas kernels: 6.81 us -> 7.44 us  [sections(): pl.pallas_call(sections_kernel, out_shape=(jax.ShapeDtypeStruct((KEYS, D)...]
where the time goes in v7:
time: 43.6 us; the launch traced here: 43.2 us
  Pallas kernels  41.4 us (95%)
  local copies, waits for them, and re-layouts  1.13 us (3%)
  between operations  0.67 us (2%)
    pallas_call x1, Pallas kernels, reduce_to_owner(): pl.pallas_call(reduce_kernel, out_shape=(jax.ShapeDtypeStruct((64, D), f3...  23.9 us
    pallas_call x1, Pallas kernels, exchange(): pl.pallas_call(exchange_kernel, out_shape=(jax.ShapeDtypeStruct((4, D, D)...  10.1 us
    pallas_call x1, Pallas kernels, sections(): pl.pallas_call(sections_kernel, out_shape=(jax.ShapeDtypeStruct((KEYS, D)...  7.44 us

profile of v7, /device:TPU:0, one launch (start us, length us, event | category | flops | bytes accessed | tf_op | source)
XLA Modules:
  0.0 43.2 jit_solution(11624695640767778694)
XLA Ops:
  0.6 0.0 copy-start
  0.6 10.1 %shard_map.77 = (f32[4,128,128]{2,1,0:T(8,128)S(1)}, f32[4,1,128]{2,1,0:T(1,128)S(1)}, bf16[32,128,128]{2,1,0:T(8,128)(2,1)S(1)}, s32[32,128,128]{2,1,0:T(8,128)...) custom-call(f32[1,128,128]{2,1,0:T(8,128)} %w_in.1, ...), custom_call_target="tpu_custom_call" | custom-call | flops 40000000000 | bytes 1048576 | tf_op jit(solution)/shard_map/pallas_call | solution.py:149
  10.7 0.0 copy-done
  10.7 7.4 %shard_map.78 = (f32[8192,128]{1,0:T(8,128)S(1)}, f32[8192,128]{1,0:T(8,128)S(1)}) custom-call(f32[4,1024,128]{2,1,0:T(8,128)S(1)} %copy-done, s32[32,128]{1,0:T(8,128)S(1)} %get-tuple-element.14.keys_in.keys, f32[4,128,128]{2,1,0:T(8,128)S(1)} %get-tuple-element.15.w, ...), custom_call_target="tpu_custom_call", output_to_operand_aliasing={{0}: (6, {}), {1}: (7, {})} | custom-call | tf_op jit(solution)/shard_map/pallas_call | solution.py:233
  18.2 23.9 %shard_map.79 = (f32[64,128]{1,0:T(8,128)S(1)}, f32[8,128]{1,0:T(8,128)S(1)}) custom-call(f32[4,4,4,2,64,128]{5,4,3,2,1,0:T(8,128)S(1)} %bitcast.7, f32[4,4,4,2,64,128]{5,4,3,2,1,0:T(8,128)S(1)} %bitcast.8, s32[32,128]{1,0:T(8,128)S(1)} %get-tuple-element.14.keys_in.keys, s32[32,128]{1,0:T(8,128)S(1)} %get-tuple-element.23.lives), custom_call_target="tpu_custom_call" | custom-call | tf_op jit(solution)/shard_map/pallas_call | solution.py:406
  42.1 0.5 %slice_bitcast_fusion = f32[64]{0:T(128)} fusion(f32[8,128]{1,0:T(8,128)S(1)} %get-tuple-element.25), kind=kLoop, calls=%fused_computation | loop fusion | bytes 512 | tf_op jit(solution)/shard_map/squeeze | solution.py:425
  42.6 0.6 %copy.13 = f32[64,128]{1,0:T(8,128)} copy(f32[64,128]{1,0:T(8,128)S(1)} %get-tuple-element.28) | data formatting | bytes 65536
Async XLA Ops:
  0.6 10.1 %copy-start = (f32[4,1024,128]{2,1,0:T(8,128)S(1)}, f32[4,1024,128]{2,1,0:T(8,128)}, u32[]{:S(2)}) copy-start(f32[4,1024,128]{2,1,0:T(8,128)} %rows.1) | copy-start | bytes 6291460

commit v8 on v7

--- a/solution.py
+++ b/solution.py
@@ -35,8 +35,8 @@
 
 def exchange_kernel(
     w_in, b_in, p_in, k_in, v_in,
-    w_all, b_all, same, level, lives, table_a, table_b, key_rows,
-    keys, valid, flags, words_v, words, send, recv, pair_send, pair_recv, local,
+    w_twice, b_all, same, lives, table_a, table_b, key_rows,
+    w_all, keys, valid, flags, words_v, words, send, recv, pair_send, pair_recv, local,
 ):
     me = lax.axis_index("section")
     row = lax.axis_index("rows")
@@ -79,6 +79,12 @@
         for which, copy in copies:
             if which == a:
                 copy.start()
+
+    def prepare(origin):
+        top = jnp.concatenate(high_low(w_all[origin]), axis=1)
+        w_twice[origin] = jnp.concatenate([top, top], axis=0)
+
+    prepare(me)
     own[4].wait()
     own[5].wait()
     group_i = (lax.broadcasted_iota(i32, (1, 128), 1) // GROUP) * KEYS
@@ -134,33 +140,33 @@
                     jnp.where(lane < 96, alive[2], alive[3]))
                 total = total + ((v >> (lane & 31)) & 1)
             lives[pl.ds(i * 4 + u, 1), :] = total[:1]
-            level[i * 4 + u] = jnp.transpose(jnp.concatenate([total] * 16, axis=0))
         return carry
 
     lax.fori_loop(0, 8, tally, 0)
     for which, copy in copies:
         if which == 2:
             copy.wait()
-    for copy in passed:
-        copy.wait()
+    for n, k in enumerate((2, 1, 3)):
+        passed[n].wait()
+        prepare(lax.rem(me + 4 - k, 4))
 
 
 def exchange(weight, bias, predicates, keys, valid):
     return pl.pallas_call(
         exchange_kernel,
         out_shape=(
-            jax.ShapeDtypeStruct((4, D, D), f32),
+            jax.ShapeDtypeStruct((4, 256, 256), bf16),
             jax.ShapeDtypeStruct((4, 1, D), f32),
             jax.ShapeDtypeStruct((32, 128, 128), bf16),
-            jax.ShapeDtypeStruct((32, 128, 128), i32),
             jax.ShapeDtypeStruct((32, 128), i32),
             jax.ShapeDtypeStruct((KEYS, D), f32),
             jax.ShapeDtypeStruct((KEYS, D), f32),
             jax.ShapeDtypeStruct((32, 128), i32),
         ),
         in_specs=[spec(HB)] * 5,
-        out_specs=(spec(VM),) * 8,
+        out_specs=(spec(VM),) * 7,
         scratch_shapes=[
+            pltpu.VMEM((4, D, D), f32),
             pltpu.VMEM((MICRO, BLOCK), i32),
             pltpu.SMEM((1, MICRO), i32),
             pltpu.VMEM((4, 4, 32), i32),
@@ -178,18 +184,16 @@
 
 
 def sections_kernel(
-    rows, keys_in, w, b, same, level, clear_a, clear_b, v_in, table_a, table_b, w2, ready, keys, valid, sems
+    rows, keys_in, w2, b, same, lives, clear_a, clear_b, v_in, table_a, table_b, ready, keys, valid, sems
 ):
     fetch = [pltpu.make_async_copy(keys_in, keys, sems.at[0]), pltpu.make_async_copy(v_in, valid, sems.at[1])]
     for copy in fetch:
         copy.start()
-    for s in range(SECTIONS):
-        top = jnp.concatenate(high_low(w[s]), axis=1)
-        w2[s] = jnp.concatenate([top, top], axis=0)
 
     def batch(m, carry):
         h = rows[m]
-        alive = level[pl.ds(m * 8, 8)].reshape(BLOCK, 128)
+        columns = jnp.transpose(jnp.concatenate([lives[pl.ds(pl.multiple_of(m * 8, 8), 8), :]] * 16, axis=0))
+        alive = jnp.concatenate([jnp.broadcast_to(columns[:, j : j + 1], (128, 128)) for j in range(8)], axis=0)
         total = jnp.zeros((BLOCK, D), f32)
         for s in range(SECTIONS):
             p = jnp.dot(jnp.concatenate(high_low(h), axis=1), w2[s], preferred_element_type=f32)
@@ -229,14 +233,13 @@
         lax.fori_loop(0, chunks, functools.partial(scatter, m * (BLOCK // CHUNK)), 0)
 
 
-def sections(rows, keys, w, b, same, level, clear_a, clear_b, valid):
+def sections(rows, keys, w, b, same, lives, clear_a, clear_b, valid):
     return pl.pallas_call(
         sections_kernel,
         out_shape=(jax.ShapeDtypeStruct((KEYS, D), f32),) * 2,
         in_specs=[spec(VM)] * 8 + [spec(HB)],
         out_specs=(spec(VM),) * 2,
         scratch_shapes=[
-            pltpu.VMEM((SECTIONS, 256, 256), bf16),
             pltpu.VMEM((ROWS, D), f32),
             pltpu.SMEM((32, 128), i32),
             pltpu.SMEM((1, MICRO), i32),
@@ -244,19 +247,19 @@
         ],
         input_output_aliases={6: 0, 7: 1},
         compiler_params=pltpu.CompilerParams(vmem_limit_bytes=12 << 20),
-    )(rows, keys, w, b, same, level, clear_a, clear_b, pinned(valid))
+    )(rows, keys, w, b, same, lives, clear_a, clear_b, pinned(valid))
 
 
 PARTS = (
     (0, 8, (0, 1, 2)),
     (24, 8, (1, 2, 0)),
-    (64, 8, (2, 0, 1)),
+    (48, 8, (2, 0, 1)),
     (8, 8, (0, 1, 2)),
     (32, 8, (1, 2, 0)),
-    (48, 8, (2, 0, 1)),
+    (56, 8, (2, 0, 1)),
     (16, 8, (0, 1, 2)),
     (40, 8, (1, 2, 0)),
-    (56, 8, (2, 0, 1)),
+    (64, 8, (2, 0, 1)),
 )
 TURNS = (
     (0, 0), (5, 0), (0, 1), (5, 1), (0, 2), (5, 2), (0, 3), (5, 3), (0, 4), (5, 4), (0, 5), (5, 5),
@@ -269,7 +272,7 @@
 HEIGHT = 72
 
 
-def reduce_kernel(table_a, table_b, keys, lives, means, count_out, table, *scratch):
+def reduce_kernel(table_a, table_b, keys, lives, sums, pair, *scratch):
     held, near, middle, second, last, third = (scratch[i * N : (i + 1) * N] for i in range(6))
     core_sems, near_sems, far_sems = scratch[6 * N :]
     z = lax.axis_index("section")
@@ -293,10 +296,47 @@
 
     def join(i, carry):
         at = (i // 16, (i // 4) % 4, i % 4)
-        table[(*at, slice(None), slice(0, 64))] = table_a[at] + table_b[at]
+        pair[(*at, slice(0, 64))] = table_a[(*at, 1 - c)] + table_b[(*at, 1 - c)]
         return carry
 
     lax.fori_loop(0, 64, join, 0)
+    pl.semaphore_wait(barrier, len(peers))
+
+    def send(src, dst, send_sem, recv_sem, to):
+        pltpu.make_async_remote_copy(
+            src_ref=src, dst_ref=dst, send_sem=send_sem, recv_sem=recv_sem, device_id=to, device_id_type=MESH
+        ).start()
+
+    def wait(ref, sem):
+        pltpu.make_async_copy(ref, ref, sem).wait()
+
+    def piece(ref, axes, axis, index, half=None):
+        where = [slice(None)] * len(axes)
+        where[axes.index(axis)] = index
+        if half is not None:
+            where[1 if axes[0] == axis else 0] = pl.ds(2 * half, 2)
+        return ref.at[tuple(where)]
+
+    def spread(n, stage, source, axes, target):
+        axis = PARTS[n][2][stage]
+        for k in (2, 1, 3):
+            send(
+                piece(source, axes, axis, position(axis, k)), target.at[k - 1],
+                far_sems.at[n, stage - 1, 0], far_sems.at[n, stage - 1, 1], device(axis, k))
+
+    def summed(n, stage, source, axes, target):
+        axis = PARTS[n][2][stage]
+        wait(target, far_sems.at[n, stage - 1, 1])
+        return (piece(source, axes, axis, place[axis])[...] + target[0]) + (target[1] + target[2])
+
+    every = [0, 1, 2]
+
+    def swap(n):
+        start, size, order = PARTS[n]
+        send(pair.at[:, :, :, pl.ds(start, size), :], held[n], core_sems.at[0, n], core_sems.at[1, n], other)
+
+    for n in range(N - 1):
+        swap(n)
     sub64 = lax.broadcasted_iota(i32, (64, 128), 0)
     sub128 = lax.broadcasted_iota(i32, (128, 128), 0)
 
@@ -311,42 +351,8 @@
 
     found = lax.fori_loop(0, 8, tally, jnp.zeros((64, 128), f32))
     for i in range(64):
-        line = jnp.broadcast_to(found[i : i + 1], (8, 128))
-        for core in range(2):
-            table[i // 16, (i // 4) % 4, i % 4, core, 64:72, :] = line
-    pl.semaphore_wait(barrier, len(peers))
-
-    def send(src, dst, send_sem, recv_sem, to):
-        pltpu.make_async_remote_copy(
-            src_ref=src, dst_ref=dst, send_sem=send_sem, recv_sem=recv_sem, device_id=to, device_id_type=MESH
-        ).start()
-
-    def wait(ref, sem):
-        pltpu.make_async_copy(ref, ref, sem).wait()
-
-    def piece(ref, axes, axis, index, half=None):
-        where = [slice(None)] * len(axes)
-        where[axes.index(axis)] = index
-        if half is not None:
-            where[1 if axes[0] == axis else 0] = pl.ds(2 * half, 2)
-        return ref.at[tuple(where)]
-
-    def spread(n, stage, source, axes, target):
-        axis = PARTS[n][2][stage]
-        for k in (2, 1, 3):
-            send(
-                piece(source, axes, axis, position(axis, k)), target.at[k - 1],
-                far_sems.at[n, stage - 1, 0], far_sems.at[n, stage - 1, 1], device(axis, k))
-
-    def summed(n, stage, source, axes, target):
-        axis = PARTS[n][2][stage]
-        wait(target, far_sems.at[n, stage - 1, 1])
-        return (piece(source, axes, axis, place[axis])[...] + target[0]) + (target[1] + target[2])
-
-    every = [0, 1, 2]
-    for n, (start, size, order) in enumerate(PARTS):
-        send(table.at[:, :, :, 1 - c, pl.ds(start, size), :], held[n], core_sems.at[0, n], core_sems.at[1, n], other)
-    values = []
+        pair[i // 16, (i // 4) % 4, i % 4, 64:72, :] = jnp.broadcast_to(found[i : i + 1], (8, 128))
+    swap(N - 1)
     for turn, n in TURNS:
         start, size, order = PARTS[n]
         axis = order[0]
@@ -360,7 +366,12 @@
         if turn == 0:
             wait(held[n], core_sems.at[1, n])
             for i in range(4):
-                held[n][i] += table[i, :, :, c, start : start + size, :]
+                if n == N - 1:
+                    mine = pair[i, :, :, 64:72, :]
+                else:
+                    at = (i, slice(None), slice(None), c, slice(start, start + size))
+                    mine = table_a[at] + table_b[at]
+                held[n][i] += mine
             hop(0, 0, position(axis, 2), 0, 1)
             hop(1, 1, position(axis, 2), 1, 3)
         elif turn == 5:
@@ -381,17 +392,7 @@
             last[n][...] = summed(n, 1, middle[n], axes, second[n])
             spread(n, 2, last[n], [order[2]], third[n])
         else:
-            value = summed(n, 2, last[n], [order[2]], third[n])
-            if start + size == HEIGHT:
-                line = value[size - 8 : size - 7]
-                wide = jnp.transpose(jnp.broadcast_to(line, (128, 128)))
-                total = jnp.maximum(jnp.where(c == 0, wide[:64], wide[64:]), 1.0)
-                count_out[...] = jnp.broadcast_to(jnp.where(c == 0, line, pltpu.roll(line, 64, 1)), (8, 128))
-                size -= 8
-            values.append((start, size, value))
-    for start, size, value in values:
-        if size:
-            means[start : start + size, :] = value[:size] / total[start : start + size]
+            sums[start : start + size, :] = summed(n, 2, last[n], [order[2]], third[n])
     for n in range(N):
         wait(held[n], core_sems.at[0, n])
         wait(near[n], near_sems.at[n, 3])
@@ -400,14 +401,14 @@
 
 
 def reduce_to_owner(table_a, table_b, keys, lives):
-    buffers = [pltpu.VMEM((4, 4, 4, 2, HEIGHT, D), f32)]
+    buffers = [pltpu.VMEM((4, 4, 4, HEIGHT, D), f32)]
     for lead in ((4, 4, 4), (6, 2, 4), (4, 4), (3, 4), (4,), (3,)):
         buffers += [pltpu.VMEM((*lead, size, D), f32) for _, size, _ in PARTS]
     return pl.pallas_call(
         reduce_kernel,
-        out_shape=(jax.ShapeDtypeStruct((64, D), f32), jax.ShapeDtypeStruct((8, D), f32)),
+        out_shape=jax.ShapeDtypeStruct((HEIGHT, D), f32),
         in_specs=[spec(VM)] * 4,
-        out_specs=(spec(VM), spec(VM)),
+        out_specs=spec(VM),
         scratch_shapes=buffers + [
             pltpu.SemaphoreType.DMA((2, N)),
             pltpu.SemaphoreType.DMA((N, 4)),
@@ -417,12 +418,30 @@
     )(table_a.reshape(4, 4, 4, 2, 64, D), table_b.reshape(4, 4, 4, 2, 64, D), keys, lives)
 
 
+def means_kernel(sums, means, counts):
+    c = lax.axis_index("rows") % 2
+    line = sums[64:65, :]
+    wide = jnp.transpose(jnp.broadcast_to(line, (128, 128)))
+    means[...] = sums[:64] / jnp.maximum(jnp.where(c == 0, wide[:64], wide[64:]), 1.0)
+    counts[...] = jnp.where(c == 0, line, pltpu.roll(line, 64, 1))[:, :64]
+
+
+def means_of(sums):
+    return pl.pallas_call(
+        means_kernel,
+        out_shape=(jax.ShapeDtypeStruct((64, D), f32), jax.ShapeDtypeStruct((1, 64), f32)),
+        in_specs=[spec(VM)],
+        out_specs=(spec(VM), spec(VM)),
+        compiler_params=pltpu.CompilerParams(vmem_limit_bytes=1 << 20),
+    )(sums)
+
+
 def shards(rows_data, row_keys, valid_counts, predicates, section_weight, section_bias):
-    w, b, same, level, lives, clear_a, clear_b, key_rows = exchange(
+    w, b, same, lives, clear_a, clear_b, key_rows = exchange(
         section_weight, section_bias.reshape(1, 1, D), predicates.reshape(4, MICRO, 32), row_keys, valid_counts.T)
-    tables = sections(rows_data, key_rows, w, b, same, level, clear_a, clear_b, valid_counts.T)
-    means, total = reduce_to_owner(*tables, key_rows, lives)
-    return means, total[0, :64]
+    tables = sections(rows_data, key_rows, w, b, same, lives, clear_a, clear_b, valid_counts.T)
+    means, counts = means_of(reduce_to_owner(*tables, key_rows, lives))
+    return means, counts.reshape(64)
 
 
 def solution(mesh):

time: 43.6 us -> 42.5 us (0.975)
  local copies, waits for them, and re-layouts: 1.13 us -> 0.01 us
    pallas_call x2 -> x3, Pallas kernels: 34 us -> 34.7 us  [the longest x1 24.6 us: reduce_to_owner(): pl.pallas_call(reduce_kernel, out_shape=jax.ShapeDtypeStruct((HEIGHT, D),...]
    unnamed x3 -> x2, local copies, waits for them, and re-layouts: 0.62 us -> 0.01 us
    squeeze x1 -> x0, local copies, waits for them, and re-layouts: 0.51 us -> none  [shards(): return (means, total[0, :64])]
    pallas_call x1, Pallas kernels: 7.44 us -> 6.96 us  [sections(): pl.pallas_call(sections_kernel, out_shape=(jax.ShapeDtypeStruct((KEYS, D)...]
where the time goes in v8:
time: 42.5 us; the launch traced here: 42.3 us
  Pallas kernels  41.7 us (98%)
  between operations  0.67 us (2%)
    pallas_call x1, Pallas kernels, reduce_to_owner(): pl.pallas_call(reduce_kernel, out_shape=jax.ShapeDtypeStruct((HEIGHT, D),...  24.6 us
    pallas_call x1, Pallas kernels, exchange(): pl.pallas_call(exchange_kernel, out_shape=(jax.ShapeDtypeStruct((4, 256,...  9.42 us
    pallas_call x1, Pallas kernels, sections(): pl.pallas_call(sections_kernel, out_shape=(jax.ShapeDtypeStruct((KEYS, D)...  6.96 us

profile of v8, /device:TPU:0, one launch (start us, length us, event | category | flops | bytes accessed | tf_op | source)
XLA Modules:
  0.0 42.3 jit_solution(8665417000922905886)
XLA Ops:
  0.6 0.0 copy-start
  0.6 9.4 %shard_map.77 = (bf16[4,256,256]{2,1,0:T(8,128)(2,1)S(1)}, f32[4,1,128]{2,1,0:T(1,128)S(1)}, bf16[32,128,128]{2,1,0:T(8,128)(2,1)S(1)}, s32[32,128]{1,0:T(8,128)...) custom-call(f32[1,128,128]{2,1,0:T(8,128)} %w_in.1, f32[1,1,128]{2,1,0:T(1,128)} %bitcast.11, ...), custom_call_target="tpu_custom_call" | custom-call | flops 40000000000 | bytes 1048576 | tf_op jit(solution)/shard_map/pallas_call | solution.py:155
  10.1 0.0 copy-done
  10.1 7.0 %shard_map.78 = (f32[8192,128]{1,0:T(8,128)S(1)}, f32[8192,128]{1,0:T(8,128)S(1)}) custom-call(f32[4,1024,128]{2,1,0:T(8,128)S(1)} %copy-done, s32[32,128]{1,0:T(8,128)S(1)} %get-tuple-element.13.keys_in.keys, bf16[4,256,256]{2,1,0:T(8,128)(2,1)S(1)} %get-tuple-element.14.w2, ...), custom_call_target="tpu_custom_call", output_to_operand_aliasing={{0}: (6, {}), {1}: (7, {})} | custom-call | tf_op jit(solution)/shard_map/pallas_call | solution.py:237
  17.0 24.6 %shard_map.79.sums = f32[72,128]{1,0:T(8,128)S(1)} custom-call(f32[4,4,4,2,64,128]{5,4,3,2,1,0:T(8,128)S(1)} %bitcast.6, f32[4,4,4,2,64,128]{5,4,3,2,1,0:T(8,128)S(1)} %bitcast.7, s32[32,128]{1,0:T(8,128)S(1)} %get-tuple-element.13.keys_in.keys, s32[32,128]{1,0:T(8,128)S(1)} %get-tuple-element.17.lives), custom_call_target="tpu_custom_call" | custom-call | tf_op jit(solution)/shard_map/pallas_call | solution.py:407
  41.6 0.7 %shard_map.80 = (f32[64,128]{1,0:T(8,128)}, f32[1,64]{1,0:T(1,128)}) custom-call(f32[72,128]{1,0:T(8,128)S(1)} %shard_map.79.sums), custom_call_target="tpu_custom_call" | custom-call | tf_op jit(solution)/shard_map/pallas_call | solution.py:430
Async XLA Ops:
  0.6 9.4 %copy-start = (f32[4,1024,128]{2,1,0:T(8,128)S(1)}, f32[4,1024,128]{2,1,0:T(8,128)}, u32[]{:S(2)}) copy-start(f32[4,1024,128]{2,1,0:T(8,128)} %rows.1) | copy-start | bytes 6291460

commit v9 on v8

--- a/solution.py
+++ b/solution.py
@@ -250,31 +250,16 @@
     )(rows, keys, w, b, same, lives, clear_a, clear_b, pinned(valid))
 
 
-PARTS = (
-    (0, 8, (0, 1, 2)),
-    (24, 8, (1, 2, 0)),
-    (48, 8, (2, 0, 1)),
-    (8, 8, (0, 1, 2)),
-    (32, 8, (1, 2, 0)),
-    (56, 8, (2, 0, 1)),
-    (16, 8, (0, 1, 2)),
-    (40, 8, (1, 2, 0)),
-    (64, 8, (2, 0, 1)),
-)
-TURNS = (
-    (0, 0), (5, 0), (0, 1), (5, 1), (0, 2), (5, 2), (0, 3), (5, 3), (0, 4), (5, 4), (0, 5), (5, 5),
-    (0, 6), (5, 6), (0, 7), (5, 7), (0, 8), (5, 8), (1, 0), (1, 1), (1, 2), (1, 3), (1, 4), (1, 5),
-    (1, 6), (1, 7), (1, 8), (2, 0), (2, 1), (2, 2), (2, 3), (2, 4), (2, 5), (2, 6), (2, 7), (2, 8),
-    (3, 0), (3, 1), (3, 2), (3, 3), (3, 4), (3, 5), (3, 6), (3, 7), (3, 8), (4, 0), (4, 1), (4, 2),
-    (4, 3), (4, 4), (4, 5), (4, 6), (4, 7), (4, 8),
-)
-N = len(PARTS)
+ORDERS = ((0, 1, 2), (1, 2, 0), (2, 0, 1))
+BAND, PART, COUNTED = 24, 8, 8
+N = 9
 HEIGHT = 72
 
 
 def reduce_kernel(table_a, table_b, keys, lives, sums, pair, *scratch):
-    held, near, middle, second, last, third = (scratch[i * N : (i + 1) * N] for i in range(6))
-    core_sems, near_sems, far_sems = scratch[6 * N :]
+    held = scratch[0:3]
+    near, middle, second, last, third = (scratch[3 + i * N : 3 + (i + 1) * N] for i in range(5))
+    core_recv, core_send, near_sems, far_sems = scratch[3 + 5 * N :]
     z = lax.axis_index("section")
     row = lax.axis_index("rows")
     y, x, c = row // 8, (row // 2) % 4, row % 2
@@ -310,33 +295,36 @@
     def wait(ref, sem):
         pltpu.make_async_copy(ref, ref, sem).wait()
 
-    def piece(ref, axes, axis, index, half=None):
+    every = [0, 1, 2]
+
+    def where_of(axes, axis, index, half=None):
         where = [slice(None)] * len(axes)
         where[axes.index(axis)] = index
         if half is not None:
             where[1 if axes[0] == axis else 0] = pl.ds(2 * half, 2)
-        return ref.at[tuple(where)]
-
-    def spread(n, stage, source, axes, target):
-        axis = PARTS[n][2][stage]
-        for k in (2, 1, 3):
-            send(
-                piece(source, axes, axis, position(axis, k)), target.at[k - 1],
-                far_sems.at[n, stage - 1, 0], far_sems.at[n, stage - 1, 1], device(axis, k))
-
-    def summed(n, stage, source, axes, target):
-        axis = PARTS[n][2][stage]
-        wait(target, far_sems.at[n, stage - 1, 1])
-        return (piece(source, axes, axis, place[axis])[...] + target[0]) + (target[1] + target[2])
-
-    every = [0, 1, 2]
-
-    def swap(n):
-        start, size, order = PARTS[n]
-        send(pair.at[:, :, :, pl.ds(start, size), :], held[n], core_sems.at[0, n], core_sems.at[1, n], other)
-
-    for n in range(N - 1):
-        swap(n)
+        return tuple(where)
+
+    def keyed(band):
+        return BAND - COUNTED if band == 2 else BAND
+
+    def swap(band, index, kind):
+        at, size = where_of(every, ORDERS[band][0], index), keyed(band)
+        send(
+            pair.at[(*at, pl.ds(band * BAND, size))], held[band].at[(*at, pl.ds(0, size))],
+            core_send.at[band], core_recv.at[band, kind], other)
+
+    def swapped(band, kind, blocks):
+        size = keyed(band)
+        wait(held[band].at[0:blocks, :, :, pl.ds(0, size)], core_recv.at[band, kind])
+        for k in {0: (2,), 1: (1, 3), 2: (0,)}[kind]:
+            at = where_of(every, ORDERS[band][0], position(ORDERS[band][0], k))
+            rows = (c, slice(band * BAND, band * BAND + size))
+            held[band][(*at, slice(0, size))] += table_a[(*at, *rows)] + table_b[(*at, *rows)]
+
+    for kind, steps in enumerate(((2,), (1, 3), (0,))):
+        for band in range(3):
+            for k in steps:
+                swap(band, position(ORDERS[band][0], k), kind)
     sub64 = lax.broadcasted_iota(i32, (64, 128), 0)
     sub128 = lax.broadcasted_iota(i32, (128, 128), 0)
 
@@ -352,65 +340,92 @@
     found = lax.fori_loop(0, 8, tally, jnp.zeros((64, 128), f32))
     for i in range(64):
         pair[i // 16, (i // 4) % 4, i % 4, 64:72, :] = jnp.broadcast_to(found[i : i + 1], (8, 128))
-    swap(N - 1)
-    for turn, n in TURNS:
-        start, size, order = PARTS[n]
-        axis = order[0]
-
-        def hop(slot, recv, index, half, k):
+    counted = held[2].at[:, :, :, pl.ds(BAND - COUNTED, COUNTED)]
+    send(pair.at[:, :, :, pl.ds(64, COUNTED)], counted, core_send.at[2], core_recv.at[3, 0], other)
+
+    def block_of(n, k, half):
+        band, step = n % 3, n // 3
+        axis = ORDERS[band][0]
+        return held[band].at[(*where_of(every, axis, position(axis, k), half), pl.ds(step * PART, PART))]
+
+    def hop(n, slot, recv, block, k):
+        send(block, near[n].at[slot], near_sems.at[n, 3], near_sems.at[n, recv], device(ORDERS[n % 3][0], k))
+
+    def relay(n):
+        hop(n, 0, 0, block_of(n, 2, 0), 1)
+        hop(n, 1, 1, block_of(n, 2, 1), 3)
+
+    def direct(n):
+        hop(n, 2, 2, block_of(n, 1, 1), 1)
+        hop(n, 3, 2, block_of(n, 3, 0), 3)
+
+    for band in range(3):
+        swapped(band, 0, 1)
+        for n in range(band, N - 1 if band == 2 else N, 3):
+            relay(n)
+    for band in range(3):
+        swapped(band, 1, 2)
+        for n in range(band, N - 1 if band == 2 else N, 3):
+            direct(n)
+    wait(counted, core_recv.at[3, 0])
+    for i in range(4):
+        held[2][i, :, :, BAND - COUNTED :] += pair[i, :, :, 64:72]
+    relay(N - 1)
+    direct(N - 1)
+
+    def spread(n, stage, source, axes, target):
+        axis = ORDERS[n % 3][stage]
+        for k in (2, 1, 3):
             send(
-                piece(held[n], every, axis, index, half), near[n].at[slot],
-                near_sems.at[n, 3], near_sems.at[n, recv], device(axis, k))
-
-        axes = [i for i in every if i != axis]
-        if turn == 0:
-            wait(held[n], core_sems.at[1, n])
-            for i in range(4):
-                if n == N - 1:
-                    mine = pair[i, :, :, 64:72, :]
-                else:
-                    at = (i, slice(None), slice(None), c, slice(start, start + size))
-                    mine = table_a[at] + table_b[at]
-                held[n][i] += mine
-            hop(0, 0, position(axis, 2), 0, 1)
-            hop(1, 1, position(axis, 2), 1, 3)
-        elif turn == 5:
-            hop(2, 2, position(axis, 1), 1, 1)
-            hop(3, 2, position(axis, 3), 0, 3)
-        elif turn == 1:
-            for half, k in ((0, 1), (1, 3)):
-                wait(near[n].at[half], near_sems.at[n, half])
-                block = piece(held[n], every, axis, position(axis, k), half)
-                block[...] += near[n][half]
-                hop(4 + half, 2, position(axis, k), half, k)
-        elif turn == 2:
-            wait(near[n].at[2:6], near_sems.at[n, 2])
-            middle[n][0:2] = (piece(held[n], every, axis, place[axis], 0)[...] + near[n][3]) + near[n][4]
-            middle[n][2:4] = (piece(held[n], every, axis, place[axis], 1)[...] + near[n][2]) + near[n][5]
-            spread(n, 1, middle[n], axes, second[n])
-        elif turn == 3:
-            last[n][...] = summed(n, 1, middle[n], axes, second[n])
-            spread(n, 2, last[n], [order[2]], third[n])
-        else:
-            sums[start : start + size, :] = summed(n, 2, last[n], [order[2]], third[n])
+                source.at[where_of(axes, axis, position(axis, k))], target.at[k - 1],
+                far_sems.at[n, stage - 1, 0], far_sems.at[n, stage - 1, 1], device(axis, k))
+
+    def summed(n, stage, source, axes, target):
+        axis = ORDERS[n % 3][stage]
+        wait(target, far_sems.at[n, stage - 1, 1])
+        return (source[where_of(axes, axis, place[axis])] + target[0]) + (target[1] + target[2])
+
     for n in range(N):
-        wait(held[n], core_sems.at[0, n])
+        for half, k in ((0, 1), (1, 3)):
+            wait(near[n].at[half], near_sems.at[n, half])
+            block = block_of(n, k, half)
+            block[...] += near[n][half]
+            hop(n, 4 + half, 2, block, k)
+    for band in range(3):
+        swapped(band, 2, 1)
+    for n in range(N):
+        axis = ORDERS[n % 3][0]
+        wait(near[n].at[2:6], near_sems.at[n, 2])
+        middle[n][0:2] = (block_of(n, 0, 0)[...] + near[n][3]) + near[n][4]
+        middle[n][2:4] = (block_of(n, 0, 1)[...] + near[n][2]) + near[n][5]
+        spread(n, 1, middle[n], [i for i in every if i != axis], second[n])
+    for n in range(N):
+        axis = ORDERS[n % 3][0]
+        last[n][...] = summed(n, 1, middle[n], [i for i in every if i != axis], second[n])
+        spread(n, 2, last[n], [ORDERS[n % 3][2]], third[n])
+    for n in range(N):
+        start = (n % 3) * BAND + (n // 3) * PART
+        sums[start : start + PART, :] = summed(n, 2, last[n], [ORDERS[n % 3][2]], third[n])
+    for band in range(3):
+        wait(held[band], core_send.at[band])
+    for n in range(N):
         wait(near[n], near_sems.at[n, 3])
         wait(second[n], far_sems.at[n, 0, 0])
         wait(third[n], far_sems.at[n, 1, 0])
 
 
 def reduce_to_owner(table_a, table_b, keys, lives):
-    buffers = [pltpu.VMEM((4, 4, 4, HEIGHT, D), f32)]
-    for lead in ((4, 4, 4), (6, 2, 4), (4, 4), (3, 4), (4,), (3,)):
-        buffers += [pltpu.VMEM((*lead, size, D), f32) for _, size, _ in PARTS]
+    buffers = [pltpu.VMEM((4, 4, 4, HEIGHT, D), f32)] + [pltpu.VMEM((4, 4, 4, BAND, D), f32)] * 3
+    for lead in ((6, 2, 4), (4, 4), (3, 4), (4,), (3,)):
+        buffers += [pltpu.VMEM((*lead, PART, D), f32)] * N
     return pl.pallas_call(
         reduce_kernel,
         out_shape=jax.ShapeDtypeStruct((HEIGHT, D), f32),
         in_specs=[spec(VM)] * 4,
         out_specs=spec(VM),
         scratch_shapes=buffers + [
-            pltpu.SemaphoreType.DMA((2, N)),
+            pltpu.SemaphoreType.DMA((4, 3)),
+            pltpu.SemaphoreType.DMA((3,)),
             pltpu.SemaphoreType.DMA((N, 4)),
             pltpu.SemaphoreType.DMA((N, 2, 2)),
         ],

time: 42.5 us -> 41.6 us (0.979)
  Pallas kernels: 41.7 us -> 40.7 us
    pallas_call x1, Pallas kernels: 24.6 us -> 23.6 us  [reduce_to_owner(): pl.pallas_call(reduce_kernel, out_shape=jax.ShapeDtypeStruct((HEIGHT, D),...]
where the time goes in v9:
time: 41.6 us; the launch traced here: 41.4 us
  Pallas kernels  40.7 us (98%)
  between operations  0.67 us (2%)
    pallas_call x1, Pallas kernels, reduce_to_owner(): pl.pallas_call(reduce_kernel, out_shape=jax.ShapeDtypeStruct((HEIGHT, D),...  23.6 us
    pallas_call x1, Pallas kernels, exchange(): pl.pallas_call(exchange_kernel, out_shape=(jax.ShapeDtypeStruct((4, 256,...  9.42 us
    pallas_call x1, Pallas kernels, sections(): pl.pallas_call(sections_kernel, out_shape=(jax.ShapeDtypeStruct((KEYS, D)...  6.96 us

profile of v9, /device:TPU:0, one launch (start us, length us, event | category | flops | bytes accessed | tf_op | source)
XLA Modules:
  0.0 41.4 jit_solution(16433132291951044685)
XLA Ops:
  0.6 0.0 copy-start
  0.6 9.4 %shard_map.77 = (bf16[4,256,256]{2,1,0:T(8,128)(2,1)S(1)}, f32[4,1,128]{2,1,0:T(1,128)S(1)}, bf16[32,128,128]{2,1,0:T(8,128)(2,1)S(1)}, s32[32,128]{1,0:T(8,128)...) custom-call(f32[1,128,128]{2,1,0:T(8,128)} %w_in.1, f32[1,1,128]{2,1,0:T(1,128)} %bitcast.11, ...), custom_call_target="tpu_custom_call" | custom-call | flops 40000000000 | bytes 1048576 | tf_op jit(solution)/shard_map/pallas_call | solution.py:155
  10.1 0.0 copy-done
  10.1 7.0 %shard_map.78 = (f32[8192,128]{1,0:T(8,128)S(1)}, f32[8192,128]{1,0:T(8,128)S(1)}) custom-call(f32[4,1024,128]{2,1,0:T(8,128)S(1)} %copy-done, s32[32,128]{1,0:T(8,128)S(1)} %get-tuple-element.13.keys_in.keys, bf16[4,256,256]{2,1,0:T(8,128)(2,1)S(1)} %get-tuple-element.14.w2, ...), custom_call_target="tpu_custom_call", output_to_operand_aliasing={{0}: (6, {}), {1}: (7, {})} | custom-call | tf_op jit(solution)/shard_map/pallas_call | solution.py:237
  17.0 23.6 %shard_map.79.sums = f32[72,128]{1,0:T(8,128)S(1)} custom-call(f32[4,4,4,2,64,128]{5,4,3,2,1,0:T(8,128)S(1)} %bitcast.6, f32[4,4,4,2,64,128]{5,4,3,2,1,0:T(8,128)S(1)} %bitcast.7, s32[32,128]{1,0:T(8,128)S(1)} %get-tuple-element.13.keys_in.keys, s32[32,128]{1,0:T(8,128)S(1)} %get-tuple-element.17.lives), custom_call_target="tpu_custom_call" | custom-call | tf_op jit(solution)/shard_map/pallas_call | solution.py:421
  40.6 0.7 %shard_map.80 = (f32[64,128]{1,0:T(8,128)}, f32[1,64]{1,0:T(1,128)}) custom-call(f32[72,128]{1,0:T(8,128)S(1)} %shard_map.79.sums), custom_call_target="tpu_custom_call" | custom-call | tf_op jit(solution)/shard_map/pallas_call | solution.py:445
Async XLA Ops:
  0.6 9.4 %copy-start = (f32[4,1024,128]{2,1,0:T(8,128)S(1)}, f32[4,1024,128]{2,1,0:T(8,128)}, u32[]{:S(2)}) copy-start(f32[4,1024,128]{2,1,0:T(8,128)} %rows.1) | copy-start | bytes 6291460

commit v10 on v9

--- a/solution.py
+++ b/solution.py
@@ -35,17 +35,15 @@
 
 def exchange_kernel(
     w_in, b_in, p_in, k_in, v_in,
-    w_twice, b_all, same, lives, table_a, table_b, key_rows,
-    w_all, keys, valid, flags, words_v, words, send, recv, pair_send, pair_recv, local,
+    w_twice, b_all, same, words, valid, table_a, table_b, key_rows,
+    w_all, keys, flags, send, recv, local,
 ):
     me = lax.axis_index("section")
     row = lax.axis_index("rows")
-    c = row % 2
-    other = (me, row + 1 - 2 * c)
     own = [
         pltpu.make_async_copy(src, dst, local.at[n])
         for n, (src, dst) in enumerate((
-            (p_in, flags), (p_in.at[me], words_v.at[me]), (b_in.at[0], b_all.at[me]), (w_in.at[0], w_all.at[me]),
+            (p_in, flags), (p_in.at[me], words.at[me]), (b_in.at[0], b_all.at[me]), (w_in.at[0], w_all.at[me]),
             (k_in, keys), (v_in, valid)))
     ]
     for copy in own:
@@ -53,7 +51,6 @@
     barrier = pltpu.get_barrier_semaphore()
     for k in range(1, 4):
         pl.semaphore_signal(barrier, inc=1, device_id=(lax.rem(me + k, 4), row), device_id_type=MESH)
-    pl.semaphore_signal(barrier, inc=1, device_id=other, device_id_type=MESH)
 
     def clear(i, carry):
         at = pl.ds(pl.multiple_of(i * 512, 512), 512)
@@ -64,13 +61,12 @@
     lax.fori_loop(0, KEYS // 512, clear, 0)
     for copy in own[:4]:
         copy.wait()
-    pl.semaphore_wait(barrier, 4)
-    half = pl.ds(pl.multiple_of(c * 64, 64), 64)
+    pl.semaphore_wait(barrier, 3)
     copies = []
     for n, k in enumerate((2, 1, 3)):
         to = lax.rem(me + k, 4)
         for a, (src, dst) in enumerate((
-            (flags.at[to], words_v.at[me]), (w_all.at[me, half], w_all.at[me, half]), (b_all.at[me], b_all.at[me]),
+            (flags.at[to], words.at[me]), (w_all.at[me], w_all.at[me]), (b_all.at[me], b_all.at[me]),
         )):
             copies.append((a, pltpu.make_async_remote_copy(
                 src_ref=src, dst_ref=dst, send_sem=send.at[n, a], recv_sem=recv.at[n, a],
@@ -107,47 +103,11 @@
     for which, copy in copies:
         if which == 0:
             copy.wait()
-    to_scalar = pltpu.make_async_copy(words_v, words, local.at[6])
-    to_scalar.start()
-    passed = []
-    for n, k in enumerate((2, 1, 3)):
-        origin = lax.rem(me + 4 - k, 4)
-        copies[3 * n + 1][1].wait()
-        block = w_all.at[origin, half]
-        copy = pltpu.make_async_remote_copy(
-            src_ref=block, dst_ref=block, send_sem=pair_send.at[n], recv_sem=pair_recv.at[n],
-            device_id=other, device_id_type=MESH)
-        copy.start()
-        passed.append(copy)
-    to_scalar.wait()
-    lane = lax.broadcasted_iota(i32, (8, 128), 1)
-
-    def tally(i, carry):
-        m = i // 2
-        nv = valid[0, m]
-        for u in range(4):
-            j = (i % 2) * 4 + u
-            total = jnp.zeros((8, 128), i32)
-            alive = []
-            for w in range(4):
-                n = nv - (j * 4 + w) * 32
-                alive.append(jnp.where(n >= 32, jnp.int32(-1), (jnp.int32(1) << jnp.clip(n, 0, 31)) - 1))
-            for s in range(SECTIONS):
-                alive = [a & words[s, m, j * 4 + w] for w, a in enumerate(alive)]
-                v = jnp.where(
-                    lane < 64,
-                    jnp.where(lane < 32, alive[0], alive[1]),
-                    jnp.where(lane < 96, alive[2], alive[3]))
-                total = total + ((v >> (lane & 31)) & 1)
-            lives[pl.ds(i * 4 + u, 1), :] = total[:1]
-        return carry
-
-    lax.fori_loop(0, 8, tally, 0)
     for which, copy in copies:
         if which == 2:
             copy.wait()
     for n, k in enumerate((2, 1, 3)):
-        passed[n].wait()
+        copies[3 * n + 1][1].wait()
         prepare(lax.rem(me + 4 - k, 4))
 
 
@@ -158,25 +118,21 @@
             jax.ShapeDtypeStruct((4, 256, 256), bf16),
             jax.ShapeDtypeStruct((4, 1, D), f32),
             jax.ShapeDtypeStruct((32, 128, 128), bf16),
-            jax.ShapeDtypeStruct((32, 128), i32),
+            jax.ShapeDtypeStruct((SECTIONS, MICRO, 32), i32),
+            jax.ShapeDtypeStruct((1, MICRO), i32),
             jax.ShapeDtypeStruct((KEYS, D), f32),
             jax.ShapeDtypeStruct((KEYS, D), f32),
             jax.ShapeDtypeStruct((32, 128), i32),
         ),
         in_specs=[spec(HB)] * 5,
-        out_specs=(spec(VM),) * 7,
+        out_specs=(spec(VM),) * 8,
         scratch_shapes=[
             pltpu.VMEM((4, D, D), f32),
             pltpu.VMEM((MICRO, BLOCK), i32),
-            pltpu.SMEM((1, MICRO), i32),
             pltpu.VMEM((4, 4, 32), i32),
-            pltpu.VMEM((4, 4, 32), i32),
-            pltpu.SMEM((4, 4, 32), i32),
             pltpu.SemaphoreType.DMA((3, 3)),
             pltpu.SemaphoreType.DMA((3, 3)),
-            pltpu.SemaphoreType.DMA((3,)),
-            pltpu.SemaphoreType.DMA((3,)),
-            pltpu.SemaphoreType.DMA((7,)),
+            pltpu.SemaphoreType.DMA((6,)),
         ],
         compiler_params=pltpu.CompilerParams(collective_id=0, has_side_effects=True, vmem_limit_bytes=8 << 20),
         cost_estimate=pl.CostEstimate(flops=40_000_000_000, bytes_accessed=1 << 20, transcendentals=0),
@@ -184,11 +140,24 @@
 
 
 def sections_kernel(
-    rows, keys_in, w2, b, same, lives, clear_a, clear_b, v_in, table_a, table_b, ready, keys, valid, sems
+    rows, keys_in, w2, b, same, words, limits, clear_a, clear_b, v_in, table_a, table_b, lives, ready, keys, valid, sems
 ):
     fetch = [pltpu.make_async_copy(keys_in, keys, sems.at[0]), pltpu.make_async_copy(v_in, valid, sems.at[1])]
     for copy in fetch:
         copy.start()
+
+    sub = lax.broadcasted_iota(i32, (8, 128), 0)
+    lane = lax.broadcasted_iota(i32, (8, 128), 1)
+    for m in range(MICRO):
+        alive = jnp.where(sub * 128 + lane < limits[0:1, m : m + 1], 1, 0)
+        found = jnp.zeros((8, 128), i32)
+        for s in range(SECTIONS):
+            line = jnp.concatenate([words[s, m : m + 1, :]] * 4, axis=1)
+            word = jnp.take_along_axis(
+                jnp.broadcast_to(line, (8, 128)), sub * 4 + (lane >> 5), axis=1, mode="promise_in_bounds")
+            alive = alive & (word >> (lane & 31))
+            found = found + alive
+        lives[m * 8 : (m + 1) * 8, :] = found
 
     def batch(m, carry):
         h = rows[m]
@@ -233,21 +202,21 @@
         lax.fori_loop(0, chunks, functools.partial(scatter, m * (BLOCK // CHUNK)), 0)
 
 
-def sections(rows, keys, w, b, same, lives, clear_a, clear_b, valid):
+def sections(rows, keys, w, b, same, words, limits, clear_a, clear_b, valid):
     return pl.pallas_call(
         sections_kernel,
-        out_shape=(jax.ShapeDtypeStruct((KEYS, D), f32),) * 2,
-        in_specs=[spec(VM)] * 8 + [spec(HB)],
-        out_specs=(spec(VM),) * 2,
+        out_shape=(jax.ShapeDtypeStruct((KEYS, D), f32),) * 2 + (jax.ShapeDtypeStruct((32, 128), i32),),
+        in_specs=[spec(VM)] * 9 + [spec(HB)],
+        out_specs=(spec(VM),) * 3,
         scratch_shapes=[
             pltpu.VMEM((ROWS, D), f32),
             pltpu.SMEM((32, 128), i32),
             pltpu.SMEM((1, MICRO), i32),
             pltpu.SemaphoreType.DMA((2,)),
         ],
-        input_output_aliases={6: 0, 7: 1},
+        input_output_aliases={7: 0, 8: 1},
         compiler_params=pltpu.CompilerParams(vmem_limit_bytes=12 << 20),
-    )(rows, keys, w, b, same, lives, clear_a, clear_b, pinned(valid))
+    )(rows, keys, w, b, same, words, limits, clear_a, clear_b, pinned(valid))
 
 
 ORDERS = ((0, 1, 2), (1, 2, 0), (2, 0, 1))
@@ -452,10 +421,11 @@
 
 
 def shards(rows_data, row_keys, valid_counts, predicates, section_weight, section_bias):
-    w, b, same, lives, clear_a, clear_b, key_rows = exchange(
+    w, b, same, words, limits, clear_a, clear_b, key_rows = exchange(
         section_weight, section_bias.reshape(1, 1, D), predicates.reshape(4, MICRO, 32), row_keys, valid_counts.T)
-    tables = sections(rows_data, key_rows, w, b, same, lives, clear_a, clear_b, valid_counts.T)
-    means, counts = means_of(reduce_to_owner(*tables, key_rows, lives))
+    table_a, table_b, lives = sections(
+        rows_data, key_rows, w, b, same, words, limits, clear_a, clear_b, valid_counts.T)
+    means, counts = means_of(reduce_to_owner(table_a, table_b, key_rows, lives))
     return means, counts.reshape(64)
 
 

time: 41.6 us -> 41.3 us (level)
  no operation moved by 1% of the time
where the time goes in v10:
time: 41.3 us; the launch traced here: 41.1 us
  Pallas kernels  40.4 us (98%)
  between operations  0.67 us (2%)
    pallas_call x1, Pallas kernels, reduce_to_owner(): pl.pallas_call(reduce_kernel, out_shape=jax.ShapeDtypeStruct((HEIGHT, D),...  23.3 us
    pallas_call x1, Pallas kernels, exchange(): pl.pallas_call(exchange_kernel, out_shape=(jax.ShapeDtypeStruct((4, 256,...  9.23 us
    pallas_call x1, Pallas kernels, sections(): pl.pallas_call(sections_kernel, out_shape=(jax.ShapeDtypeStruct((KEYS, D)...  7.14 us

profile of v10, /device:TPU:0, one launch (start us, length us, event | category | flops | bytes accessed | tf_op | source)
XLA Modules:
  0.0 41.1 jit_solution(17121768782841244456)
XLA Ops:
  0.6 0.0 copy-start
  0.6 9.2 %shard_map.77 = (bf16[4,256,256]{2,1,0:T(8,128)(2,1)S(1)}, f32[4,1,128]{2,1,0:T(1,128)S(1)}, bf16[32,128,128]{2,1,0:T(8,128)(2,1)S(1)}, s32[4,4,32]{2,1,0:T(4,12...) custom-call(f32[1,128,128]{2,1,0:T(8,128)} %w_in.1, ...), custom_call_target="tpu_custom_call" | custom-call | flops 40000000000 | bytes 1048576 | tf_op jit(solution)/shard_map/pallas_call | solution.py:115
  9.9 0.0 copy-done
  9.9 7.1 %shard_map.78 = (f32[8192,128]{1,0:T(8,128)S(1)}, f32[8192,128]{1,0:T(8,128)S(1)}, s32[32,128]{1,0:T(8,128)S(1)}) custom-call(f32[4,1024,128]{2,1,0:T(8,128)S(1)} %copy-done, s32[32,128]{1,0:T(8,128)S(1)} %get-tuple-element.15.keys_in.keys, bf16[4,256,256]{2,1,0:T(8,128)(2,1)S(1)} %get-tuple-element.16.w2, ...), custom_call_target="tpu_custom_call", output_to_operand_aliasing={{0}: (7, {}), {1}: (8, {})} | custom-call | tf_op jit(solution)/shard_map/pallas_call | solution.py:206
  17.0 23.3 %shard_map.79.sums = f32[72,128]{1,0:T(8,128)S(1)} custom-call(f32[4,4,4,2,64,128]{5,4,3,2,1,0:T(8,128)S(1)} %bitcast.6, f32[4,4,4,2,64,128]{5,4,3,2,1,0:T(8,128)S(1)} %bitcast.7, s32[32,128]{1,0:T(8,128)S(1)} %get-tuple-element.15.keys_in.keys, s32[32,128]{1,0:T(8,128)S(1)} %get-tuple-element.25.lives), custom_call_target="tpu_custom_call" | custom-call | tf_op jit(solution)/shard_map/pallas_call | solution.py:390
  40.4 0.7 %shard_map.80 = (f32[64,128]{1,0:T(8,128)}, f32[1,64]{1,0:T(1,128)}) custom-call(f32[72,128]{1,0:T(8,128)S(1)} %shard_map.79.sums), custom_call_target="tpu_custom_call" | custom-call | tf_op jit(solution)/shard_map/pallas_call | solution.py:414
Async XLA Ops:
  0.6 9.3 %copy-start = (f32[4,1024,128]{2,1,0:T(8,128)S(1)}, f32[4,1024,128]{2,1,0:T(8,128)}, u32[]{:S(2)}) copy-start(f32[4,1024,128]{2,1,0:T(8,128)} %rows.1) | copy-start | bytes 6291460

commit v11 on v10

--- a/solution.py
+++ b/solution.py
@@ -14,7 +14,9 @@
 BLOCK = 1024
 ROWS = MICRO * BLOCK
 GROUP = 8
-CHUNK = 256
+TILE = 128
+BATCH = 8
+SURE = 256
 f32, bf16, i32 = jnp.float32, jnp.bfloat16, jnp.int32
 MESH = pl.DeviceIdType.MESH
 VM, SM, HB = pltpu.VMEM, pltpu.SMEM, pltpu.HBM
@@ -159,47 +161,67 @@
             found = found + alive
         lives[m * 8 : (m + 1) * 8, :] = found
 
-    def batch(m, carry):
-        h = rows[m]
-        columns = jnp.transpose(jnp.concatenate([lives[pl.ds(pl.multiple_of(m * 8, 8), 8), :]] * 16, axis=0))
+    def compute(slot, tiles):
+        h = jnp.concatenate([rows[t // 8, pl.ds(pl.multiple_of((t % 8) * TILE, TILE), TILE), :] for t in tiles], axis=0)
+        levels = jnp.concatenate([lives[pl.ds(t, 1), :] for t in tiles], axis=0)
+        columns = jnp.transpose(jnp.concatenate([levels] * 16, axis=0))
         alive = jnp.concatenate([jnp.broadcast_to(columns[:, j : j + 1], (128, 128)) for j in range(8)], axis=0)
-        total = jnp.zeros((BLOCK, D), f32)
+        total = jnp.zeros((BATCH * TILE, D), f32)
         for s in range(SECTIONS):
             p = jnp.dot(jnp.concatenate(high_low(h), axis=1), w2[s], preferred_element_type=f32)
             h = h + jnp.tanh(p[:, :D] + (p[:, D:] + b[s]))
             total = total + jnp.where(alive > s, h, 0.0)
         both = jnp.concatenate(high_low(total), axis=1)
-        for j in range(8):
-            p = jnp.dot(same[m * 8 + j], both[j * 128 : (j + 1) * 128], preferred_element_type=f32)
-            ready[pl.ds(pl.multiple_of(m * BLOCK + j * 128, 128), 128), :] = p[:, :D] + p[:, D:]
-        return carry
-
-    lax.fori_loop(0, MICRO, batch, 0)
+        for j, t in enumerate(tiles):
+            p = jnp.dot(same[t], both[j * TILE : (j + 1) * TILE], preferred_element_type=f32)
+            ready[pl.ds(pl.multiple_of((slot + j) * TILE, TILE), TILE), :] = p[:, :D] + p[:, D:]
+
+    compute(0, [m * 8 + j for m in range(MICRO) for j in range(SURE // TILE)])
     for copy in fetch:
         copy.wait()
+    ends = [0]
+    for m in range(MICRO):
+        ends.append(ends[-1] + (valid[0, m] - SURE + TILE - 1) // TILE)
+
+    def tile_at(i):
+        tile = SURE // TILE + i
+        for m in range(1, MICRO):
+            tile = jnp.where(i >= ends[m], m * 8 + SURE // TILE + i - ends[m], tile)
+        return jnp.minimum(tile, 31)
+
+    def batch(n, carry):
+        compute(BATCH + n * BATCH, [tile_at(n * BATCH + j) for j in range(BATCH)])
+        return carry
+
+    lax.fori_loop(0, (ends[MICRO] + BATCH - 1) // BATCH, batch, 0)
     tables = (table_a, table_b)
-    groups = CHUNK // GROUP
-
-    def scatter(first, i, carry):
-        u = first + i
+    groups = TILE // GROUP
+
+    def scatter(slot, tile):
         def load(g):
-            at = [keys[u * (CHUNK // 128) + (g * GROUP + i) // 128, (g * GROUP + i) % 128] for i in range(GROUP)]
+            at = [keys[tile, g * GROUP + i] for i in range(GROUP)]
             return at, [tables[g % 2][pl.ds(k, 1), :] for k in at]
 
         def store(g, at, held):
             for i, k in enumerate(at):
-                tables[g % 2][pl.ds(k, 1), :] = held[i] + ready[pl.ds(u * CHUNK + g * GROUP + i, 1), :]
+                tables[g % 2][pl.ds(k, 1), :] = held[i] + ready[pl.ds(slot * TILE + g * GROUP + i, 1), :]
 
         flying = {g: load(g) for g in range(2)}
         for g in range(groups):
             store(g, *flying.pop(g))
             if g + 2 < groups:
                 flying[g + 2] = load(g + 2)
-        return carry
-
-    for m in range(MICRO):
-        chunks = (valid[0, m] + CHUNK - 1) // CHUNK
-        lax.fori_loop(0, chunks, functools.partial(scatter, m * (BLOCK // CHUNK)), 0)
+
+    def sure(i, carry):
+        scatter(i, (i // 2) * 8 + i % 2)
+        return carry
+
+    def rest(i, carry):
+        scatter(BATCH + i, tile_at(i))
+        return carry
+
+    lax.fori_loop(0, BATCH, sure, 0)
+    lax.fori_loop(0, ends[MICRO], rest, 0)
 
 
 def sections(rows, keys, w, b, same, words, limits, clear_a, clear_b, valid):

time: 41.3 us -> 41.1 us (level)
    pallas_call x1, Pallas kernels: 23.3 us -> 22.7 us  [reduce_to_owner(): pl.pallas_call(reduce_kernel, out_shape=jax.ShapeDtypeStruct((HEIGHT, D),...]
where the time goes in v11:
time: 41.1 us; the launch traced here: 40.8 us
  Pallas kernels  40.1 us (98%)
  between operations  0.67 us (2%)
    pallas_call x1, Pallas kernels, reduce_to_owner(): pl.pallas_call(reduce_kernel, out_shape=jax.ShapeDtypeStruct((HEIGHT, D),...  22.7 us
    pallas_call x1, Pallas kernels, exchange(): pl.pallas_call(exchange_kernel, out_shape=(jax.ShapeDtypeStruct((4, 256,...  9.23 us
    pallas_call x1, Pallas kernels, sections(): pl.pallas_call(sections_kernel, out_shape=(jax.ShapeDtypeStruct((KEYS, D)...  7.48 us

profile of v11, /device:TPU:0, one launch (start us, length us, event | category | flops | bytes accessed | tf_op | source)
XLA Modules:
  0.0 40.8 jit_solution(17690811366839074664)
XLA Ops:
  0.6 0.0 copy-start
  0.6 9.2 %shard_map.77 = (bf16[4,256,256]{2,1,0:T(8,128)(2,1)S(1)}, f32[4,1,128]{2,1,0:T(1,128)S(1)}, bf16[32,128,128]{2,1,0:T(8,128)(2,1)S(1)}, s32[4,4,32]{2,1,0:T(4,12...) custom-call(f32[1,128,128]{2,1,0:T(8,128)} %w_in.1, ...), custom_call_target="tpu_custom_call" | custom-call | flops 40000000000 | bytes 1048576 | tf_op jit(solution)/shard_map/pallas_call | solution.py:117
  9.9 0.0 copy-done
  9.9 7.5 %shard_map.78 = (f32[8192,128]{1,0:T(8,128)S(1)}, f32[8192,128]{1,0:T(8,128)S(1)}, s32[32,128]{1,0:T(8,128)S(1)}) custom-call(f32[4,1024,128]{2,1,0:T(8,128)S(1)} %copy-done, s32[32,128]{1,0:T(8,128)S(1)} %get-tuple-element.15.keys_in.keys, bf16[4,256,256]{2,1,0:T(8,128)(2,1)S(1)} %get-tuple-element.16.w2, ...), custom_call_target="tpu_custom_call", output_to_operand_aliasing={{0}: (7, {}), {1}: (8, {})} | custom-call | tf_op jit(solution)/shard_map/pallas_call | solution.py:228
  17.4 22.7 %shard_map.79.sums = f32[72,128]{1,0:T(8,128)S(1)} custom-call(f32[4,4,4,2,64,128]{5,4,3,2,1,0:T(8,128)S(1)} %bitcast.6, f32[4,4,4,2,64,128]{5,4,3,2,1,0:T(8,128)S(1)} %bitcast.7, s32[32,128]{1,0:T(8,128)S(1)} %get-tuple-element.15.keys_in.keys, s32[32,128]{1,0:T(8,128)S(1)} %get-tuple-element.25.lives), custom_call_target="tpu_custom_call" | custom-call | tf_op jit(solution)/shard_map/pallas_call | solution.py:412
  40.1 0.7 %shard_map.80 = (f32[64,128]{1,0:T(8,128)}, f32[1,64]{1,0:T(1,128)}) custom-call(f32[72,128]{1,0:T(8,128)S(1)} %shard_map.79.sums), custom_call_target="tpu_custom_call" | custom-call | tf_op jit(solution)/shard_map/pallas_call | solution.py:436
Async XLA Ops:
  0.6 9.3 %copy-start = (f32[4,1024,128]{2,1,0:T(8,128)S(1)}, f32[4,1024,128]{2,1,0:T(8,128)}, u32[]{:S(2)}) copy-start(f32[4,1024,128]{2,1,0:T(8,128)} %rows.1) | copy-start | bytes 6291460

commit v12 on v11

--- a/solution.py
+++ b/solution.py
@@ -108,7 +108,7 @@
     for which, copy in copies:
         if which == 2:
             copy.wait()
-    for n, k in enumerate((2, 1, 3)):
+    for n, k in ((1, 1), (2, 3), (0, 2)):
         copies[3 * n + 1][1].wait()
         prepare(lax.rem(me + 4 - k, 4))
 
@@ -161,18 +161,18 @@
             found = found + alive
         lives[m * 8 : (m + 1) * 8, :] = found
 
-    def compute(slot, tiles):
-        h = jnp.concatenate([rows[t // 8, pl.ds(pl.multiple_of((t % 8) * TILE, TILE), TILE), :] for t in tiles], axis=0)
+    def compute(slot, tiles, used=BATCH):
+        h = jnp.concatenate([rows[t // 8, pl.ds(pl.multiple_of((t % 8) * TILE, TILE), TILE), :] for t in tiles[:used]], axis=0)
         levels = jnp.concatenate([lives[pl.ds(t, 1), :] for t in tiles], axis=0)
         columns = jnp.transpose(jnp.concatenate([levels] * 16, axis=0))
-        alive = jnp.concatenate([jnp.broadcast_to(columns[:, j : j + 1], (128, 128)) for j in range(8)], axis=0)
-        total = jnp.zeros((BATCH * TILE, D), f32)
+        alive = jnp.concatenate([jnp.broadcast_to(columns[:, j : j + 1], (128, 128)) for j in range(used)], axis=0)
+        total = jnp.zeros((used * TILE, D), f32)
         for s in range(SECTIONS):
             p = jnp.dot(jnp.concatenate(high_low(h), axis=1), w2[s], preferred_element_type=f32)
             h = h + jnp.tanh(p[:, :D] + (p[:, D:] + b[s]))
             total = total + jnp.where(alive > s, h, 0.0)
         both = jnp.concatenate(high_low(total), axis=1)
-        for j, t in enumerate(tiles):
+        for j, t in enumerate(tiles[:used]):
             p = jnp.dot(same[t], both[j * TILE : (j + 1) * TILE], preferred_element_type=f32)
             ready[pl.ds(pl.multiple_of((slot + j) * TILE, TILE), TILE), :] = p[:, :D] + p[:, D:]
 
@@ -193,7 +193,13 @@
         compute(BATCH + n * BATCH, [tile_at(n * BATCH + j) for j in range(BATCH)])
         return carry
 
-    lax.fori_loop(0, (ends[MICRO] + BATCH - 1) // BATCH, batch, 0)
+    whole = (ends[MICRO] + BATCH // 2 - 1) // BATCH
+    lax.fori_loop(0, whole, batch, 0)
+
+    @pl.when(ends[MICRO] > whole * BATCH)
+    def _():
+        compute(BATCH + whole * BATCH, [tile_at(whole * BATCH + j) for j in range(BATCH)], BATCH // 2)
+
     tables = (table_a, table_b)
     groups = TILE // GROUP
 
@@ -377,13 +383,14 @@
         return (source[where_of(axes, axis, place[axis])] + target[0]) + (target[1] + target[2])
 
     for n in range(N):
+        if n == 6:
+            for band in range(3):
+                swapped(band, 2, 1)
         for half, k in ((0, 1), (1, 3)):
             wait(near[n].at[half], near_sems.at[n, half])
             block = block_of(n, k, half)
             block[...] += near[n][half]
             hop(n, 4 + half, 2, block, k)
-    for band in range(3):
-        swapped(band, 2, 1)
     for n in range(N):
         axis = ORDERS[n % 3][0]
         wait(near[n].at[2:6], near_sems.at[n, 2])

time: 41.1 us -> 41.3 us (level)
  no operation moved by 1% of the time
where the time goes in v12:
time: 41.3 us; the launch traced here: 40.9 us
  Pallas kernels  40.2 us (97%)
  between operations  0.67 us (2%)
    pallas_call x1, Pallas kernels, reduce_to_owner(): pl.pallas_call(reduce_kernel, out_shape=jax.ShapeDtypeStruct((HEIGHT, D),...  22.8 us
    pallas_call x1, Pallas kernels, exchange(): pl.pallas_call(exchange_kernel, out_shape=(jax.ShapeDtypeStruct((4, 256,...  9.23 us
    pallas_call x1, Pallas kernels, sections(): pl.pallas_call(sections_kernel, out_shape=(jax.ShapeDtypeStruct((KEYS, D)...  7.49 us

profile of v12, /device:TPU:0, one launch (start us, length us, event | category | flops | bytes accessed | tf_op | source)
XLA Modules:
  0.0 40.9 jit_solution(6915920809731328392)
XLA Ops:
  0.6 0.0 copy-start
  0.6 9.2 %shard_map.77 = (bf16[4,256,256]{2,1,0:T(8,128)(2,1)S(1)}, f32[4,1,128]{2,1,0:T(1,128)S(1)}, bf16[32,128,128]{2,1,0:T(8,128)(2,1)S(1)}, s32[4,4,32]{2,1,0:T(4,12...) custom-call(f32[1,128,128]{2,1,0:T(8,128)} %w_in.1, ...), custom_call_target="tpu_custom_call" | custom-call | flops 40000000000 | bytes 1048576 | tf_op jit(solution)/shard_map/pallas_call | solution.py:117
  9.9 0.0 copy-done
  9.9 7.5 %shard_map.78 = (f32[8192,128]{1,0:T(8,128)S(1)}, f32[8192,128]{1,0:T(8,128)S(1)}, s32[32,128]{1,0:T(8,128)S(1)}) custom-call(f32[4,1024,128]{2,1,0:T(8,128)S(1)} %copy-done, s32[32,128]{1,0:T(8,128)S(1)} %get-tuple-element.15.keys_in.keys, bf16[4,256,256]{2,1,0:T(8,128)(2,1)S(1)} %get-tuple-element.16.w2, ...), custom_call_target="tpu_custom_call", output_to_operand_aliasing={{0}: (7, {}), {1}: (8, {})} | custom-call | tf_op jit(solution)/shard_map/pallas_call | solution.py:234
  17.4 22.8 %shard_map.79.sums = f32[72,128]{1,0:T(8,128)S(1)} custom-call(f32[4,4,4,2,64,128]{5,4,3,2,1,0:T(8,128)S(1)} %bitcast.6, f32[4,4,4,2,64,128]{5,4,3,2,1,0:T(8,128)S(1)} %bitcast.7, s32[32,128]{1,0:T(8,128)S(1)} %get-tuple-element.15.keys_in.keys, s32[32,128]{1,0:T(8,128)S(1)} %get-tuple-element.25.lives), custom_call_target="tpu_custom_call" | custom-call | tf_op jit(solution)/shard_map/pallas_call | solution.py:419
  40.2 0.7 %shard_map.80 = (f32[64,128]{1,0:T(8,128)}, f32[1,64]{1,0:T(1,128)}) custom-call(f32[72,128]{1,0:T(8,128)S(1)} %shard_map.79.sums), custom_call_target="tpu_custom_call" | custom-call | tf_op jit(solution)/shard_map/pallas_call | solution.py:443
Async XLA Ops:
  0.6 9.3 %copy-start = (f32[4,1024,128]{2,1,0:T(8,128)S(1)}, f32[4,1024,128]{2,1,0:T(8,128)}, u32[]{:S(2)}) copy-start(f32[4,1024,128]{2,1,0:T(8,128)} %rows.1) | copy-start | bytes 6291460

commit v13 on v12

--- a/solution.py
+++ b/solution.py
@@ -201,11 +201,12 @@
         compute(BATCH + whole * BATCH, [tile_at(whole * BATCH + j) for j in range(BATCH)], BATCH // 2)
 
     tables = (table_a, table_b)
-    groups = TILE // GROUP
-
-    def scatter(slot, tile):
+
+    def scatter(slot, *tiles):
+        groups = len(tiles) * TILE // GROUP
+
         def load(g):
-            at = [keys[tile, g * GROUP + i] for i in range(GROUP)]
+            at = [keys[tiles[g * GROUP // TILE], (g * GROUP + i) % TILE] for i in range(GROUP)]
             return at, [tables[g % 2][pl.ds(k, 1), :] for k in at]
 
         def store(g, at, held):
@@ -218,16 +219,20 @@
             if g + 2 < groups:
                 flying[g + 2] = load(g + 2)
 
-    def sure(i, carry):
-        scatter(i, (i // 2) * 8 + i % 2)
+    def sure(m, carry):
+        scatter(2 * m, 8 * m, 8 * m + 1)
         return carry
 
     def rest(i, carry):
-        scatter(BATCH + i, tile_at(i))
-        return carry
-
-    lax.fori_loop(0, BATCH, sure, 0)
-    lax.fori_loop(0, ends[MICRO], rest, 0)
+        scatter(BATCH + 2 * i, tile_at(2 * i), tile_at(2 * i + 1))
+        return carry
+
+    lax.fori_loop(0, MICRO, sure, 0)
+    lax.fori_loop(0, ends[MICRO] // 2, rest, 0)
+
+    @pl.when(ends[MICRO] % 2 == 1)
+    def _():
+        scatter(BATCH + ends[MICRO] - 1, tile_at(ends[MICRO] - 1))
 
 
 def sections(rows, keys, w, b, same, words, limits, clear_a, clear_b, valid):

time: 41.3 us -> 41 us (level)
    pallas_call x1, Pallas kernels: 7.49 us -> 5.27 us  [sections(): pl.pallas_call(sections_kernel, out_shape=(jax.ShapeDtypeStruct((KEYS, D)...]
    pallas_call x1, Pallas kernels: 22.8 us -> 25 us  [reduce_to_owner(): pl.pallas_call(reduce_kernel, out_shape=jax.ShapeDtypeStruct((HEIGHT, D),...]
where the time goes in v13:
time: 41 us; the launch traced here: 40.9 us
  Pallas kernels  40.2 us (98%)
  between operations  0.67 us (2%)
    pallas_call x1, Pallas kernels, reduce_to_owner(): pl.pallas_call(reduce_kernel, out_shape=jax.ShapeDtypeStruct((HEIGHT, D),...  25 us
    pallas_call x1, Pallas kernels, exchange(): pl.pallas_call(exchange_kernel, out_shape=(jax.ShapeDtypeStruct((4, 256,...  9.23 us
    pallas_call x1, Pallas kernels, sections(): pl.pallas_call(sections_kernel, out_shape=(jax.ShapeDtypeStruct((KEYS, D)...  5.27 us

profile of v13, /device:TPU:0, one launch (start us, length us, event | category | flops | bytes accessed | tf_op | source)
XLA Modules:
  0.0 40.9 jit_solution(4883099685409996065)
XLA Ops:
  0.6 0.0 copy-start
  0.6 9.2 %shard_map.77 = (bf16[4,256,256]{2,1,0:T(8,128)(2,1)S(1)}, f32[4,1,128]{2,1,0:T(1,128)S(1)}, bf16[32,128,128]{2,1,0:T(8,128)(2,1)S(1)}, s32[4,4,32]{2,1,0:T(4,12...) custom-call(f32[1,128,128]{2,1,0:T(8,128)} %w_in.1, ...), custom_call_target="tpu_custom_call" | custom-call | flops 40000000000 | bytes 1048576 | tf_op jit(solution)/shard_map/pallas_call | solution.py:117
  9.9 0.0 copy-done
  9.9 5.3 %shard_map.78 = (f32[8192,128]{1,0:T(8,128)S(1)}, f32[8192,128]{1,0:T(8,128)S(1)}, s32[32,128]{1,0:T(8,128)S(1)}) custom-call(f32[4,1024,128]{2,1,0:T(8,128)S(1)} %copy-done, s32[32,128]{1,0:T(8,128)S(1)} %get-tuple-element.15.keys_in.keys, bf16[4,256,256]{2,1,0:T(8,128)(2,1)S(1)} %get-tuple-element.16.w2, ...), custom_call_target="tpu_custom_call", output_to_operand_aliasing={{0}: (7, {}), {1}: (8, {})} | custom-call | tf_op jit(solution)/shard_map/pallas_call | solution.py:239
  15.2 25.0 %shard_map.79.sums = f32[72,128]{1,0:T(8,128)S(1)} custom-call(f32[4,4,4,2,64,128]{5,4,3,2,1,0:T(8,128)S(1)} %bitcast.6, f32[4,4,4,2,64,128]{5,4,3,2,1,0:T(8,128)S(1)} %bitcast.7, s32[32,128]{1,0:T(8,128)S(1)} %get-tuple-element.15.keys_in.keys, s32[32,128]{1,0:T(8,128)S(1)} %get-tuple-element.25.lives), custom_call_target="tpu_custom_call" | custom-call | tf_op jit(solution)/shard_map/pallas_call | solution.py:424
  40.2 0.7 %shard_map.80 = (f32[64,128]{1,0:T(8,128)}, f32[1,64]{1,0:T(1,128)}) custom-call(f32[72,128]{1,0:T(8,128)S(1)} %shard_map.79.sums), custom_call_target="tpu_custom_call" | custom-call | tf_op jit(solution)/shard_map/pallas_call | solution.py:448
Async XLA Ops:
  0.6 9.3 %copy-start = (f32[4,1024,128]{2,1,0:T(8,128)S(1)}, f32[4,1024,128]{2,1,0:T(8,128)}, u32[]{:S(2)}) copy-start(f32[4,1024,128]{2,1,0:T(8,128)} %rows.1) | copy-start | bytes 6291460

commit v14 on v13

--- a/solution.py
+++ b/solution.py
@@ -282,11 +282,11 @@
         pl.semaphore_signal(barrier, inc=1, device_id=peer, device_id_type=MESH)
 
     def join(i, carry):
-        at = (i // 16, (i // 4) % 4, i % 4)
+        at = (i // 4, i % 4, slice(None))
         pair[(*at, slice(0, 64))] = table_a[(*at, 1 - c)] + table_b[(*at, 1 - c)]
         return carry
 
-    lax.fori_loop(0, 64, join, 0)
+    lax.fori_loop(0, 16, join, 0)
     pl.semaphore_wait(barrier, len(peers))
 
     def send(src, dst, send_sem, recv_sem, to):

time: 41 us -> 41 us (level)
    pallas_call x1, Pallas kernels: 5.27 us -> 5.84 us  [sections(): pl.pallas_call(sections_kernel, out_shape=(jax.ShapeDtypeStruct((KEYS, D)...]
    pallas_call x1, Pallas kernels: 25 us -> 24.5 us  [reduce_to_owner(): pl.pallas_call(reduce_kernel, out_shape=jax.ShapeDtypeStruct((HEIGHT, D),...]
where the time goes in v14:
time: 41 us
  Pallas kernels  40.3 us (98%)
  between operations  0.67 us (2%)
    pallas_call x1, Pallas kernels, reduce_to_owner(): pl.pallas_call(reduce_kernel, out_shape=jax.ShapeDtypeStruct((HEIGHT, D),...  24.5 us
    pallas_call x1, Pallas kernels, exchange(): pl.pallas_call(exchange_kernel, out_shape=(jax.ShapeDtypeStruct((4, 256,...  9.23 us
    pallas_call x1, Pallas kernels, sections(): pl.pallas_call(sections_kernel, out_shape=(jax.ShapeDtypeStruct((KEYS, D)...  5.84 us

profile of v14, /device:TPU:0, one launch (start us, length us, event | category | flops | bytes accessed | tf_op | source)
XLA Modules:
  0.0 41.0 jit_solution(11636532927258906623)
XLA Ops:
  0.6 0.0 copy-start
  0.6 9.2 %shard_map.77 = (bf16[4,256,256]{2,1,0:T(8,128)(2,1)S(1)}, f32[4,1,128]{2,1,0:T(1,128)S(1)}, bf16[32,128,128]{2,1,0:T(8,128)(2,1)S(1)}, s32[4,4,32]{2,1,0:T(4,12...) custom-call(f32[1,128,128]{2,1,0:T(8,128)} %w_in.1, ...), custom_call_target="tpu_custom_call" | custom-call | flops 40000000000 | bytes 1048576 | tf_op jit(solution)/shard_map/pallas_call | solution.py:117
  9.9 0.0 copy-done
  9.9 5.8 %shard_map.78 = (f32[8192,128]{1,0:T(8,128)S(1)}, f32[8192,128]{1,0:T(8,128)S(1)}, s32[32,128]{1,0:T(8,128)S(1)}) custom-call(f32[4,1024,128]{2,1,0:T(8,128)S(1)} %copy-done, s32[32,128]{1,0:T(8,128)S(1)} %get-tuple-element.15.keys_in.keys, bf16[4,256,256]{2,1,0:T(8,128)(2,1)S(1)} %get-tuple-element.16.w2, ...), custom_call_target="tpu_custom_call", output_to_operand_aliasing={{0}: (7, {}), {1}: (8, {})} | custom-call | tf_op jit(solution)/shard_map/pallas_call | solution.py:239
  15.7 24.5 %shard_map.79.sums = f32[72,128]{1,0:T(8,128)S(1)} custom-call(f32[4,4,4,2,64,128]{5,4,3,2,1,0:T(8,128)S(1)} %bitcast.6, f32[4,4,4,2,64,128]{5,4,3,2,1,0:T(8,128)S(1)} %bitcast.7, s32[32,128]{1,0:T(8,128)S(1)} %get-tuple-element.15.keys_in.keys, s32[32,128]{1,0:T(8,128)S(1)} %get-tuple-element.25.lives), custom_call_target="tpu_custom_call" | custom-call | tf_op jit(solution)/shard_map/pallas_call | solution.py:424
  40.3 0.7 %shard_map.80 = (f32[64,128]{1,0:T(8,128)}, f32[1,64]{1,0:T(1,128)}) custom-call(f32[72,128]{1,0:T(8,128)S(1)} %shard_map.79.sums), custom_call_target="tpu_custom_call" | custom-call | tf_op jit(solution)/shard_map/pallas_call | solution.py:448
Async XLA Ops:
  0.6 9.3 %copy-start = (f32[4,1024,128]{2,1,0:T(8,128)S(1)}, f32[4,1024,128]{2,1,0:T(8,128)}, u32[]{:S(2)}) copy-start(f32[4,1024,128]{2,1,0:T(8,128)} %rows.1) | copy-start | bytes 6291460
